TPU v7x, 1024 devices: a whole 4x4x32 slice. The times are simulated.
1024 devices in a mesh: gx: 4 (over x_hi, core), gy: 4 (over y), gz: 64 (over z, x_lo).
Axes of the slice: x: 4 (x_hi: 2, x_lo: 2; x = x_hi * 2 + x_lo), y: 4, z: 32, core: 2. Of those that a mesh axis runs over, the one named last changes fastest.
Arguments:
- velocity: float32 [3, 512, 16384], P(None, None, ('gx', 'gy', 'gz')), may hold values from -4 to 4
- inv_density: float32 [512, 16384], P(None, ('gx', 'gy', 'gz')), may hold values from 0.25 to 4
- element_place: int32 [16384], P(('gx', 'gy', 'gz')), may hold values from 0 to 15, as said below
Outputs:
- advected: float32 [3, 512, 16384], P(None, None, ('gx', 'gy', 'gz'))
- pressure: float32 [512, 16384], P(None, ('gx', 'gy', 'gz'))
- residual: float32 [512, 16384], P(None, ('gx', 'gy', 'gz'))
Inputs may be any that keep to these rules, and one draw needn't show every extreme that they name: `element_place`: within each device's 16 consecutive elements every block position appears exactly once.
All inputs are finite; a program needn't handle non-finite values.
Results may differ from a plain program's by a relative error of at most 0.0003.
Values sent between devices are 32-bit elements; how exact they have to be, the bound alone decides.
No kernel may reach another device: no remote copies, remote signals or barrier semaphores. Data moves between devices by JAX's collectives and lax.ppermute only.
A program may use at most 32 MiB of HBM per device.

v0:
```python
import jax
import jax.numpy as jnp
from jax import lax
from jax.sharding import Mesh
from jax.sharding import PartitionSpec as P

BX = 4
BY = 4
BZ = 1
CG_ITERS = 2
GX = ("gx_0", "gx_1")
GZ = ("gz_0", "gz_1")
GX_GY_GZ = ("gx_0", "gx_1", "gy", "gz_0", "gz_1")


time_step = 0.03
mass_shift = 4.0
inner_nodes = (
    -0.8717401485096066,
    -0.5917001814331423,
    -0.2092992179024789,
    0.2092992179024789,
    0.5917001814331423,
    0.8717401485096066,
)


def extended(cells, sides, width):
    for axis, dim in sides:
        count = lax.axis_size(axis)
        ends = count - 1
        head = lax.slice_in_dim(cells, 0, width, axis=dim)
        tail = lax.slice_in_dim(cells, cells.shape[dim] - width, cells.shape[dim], axis=dim)
        cells = jnp.concatenate(
            [
                lax.ppermute(tail, axis, [(i, (i + 1) % count) for i in range(ends)]),
                cells,
                lax.ppermute(head, axis, [((i + 1) % count, i) for i in range(ends)]),
            ],
            axis=dim,
        )
    return cells


def by_axis(x, axes):
    for axis in axes:
        x = lax.psum(x, axis)
    return x


def legendre_seven(position):
    previous = 1.0
    current_value = position
    for degree_index in range(1, 7):
        following = (
            (2 * degree_index + 1) * position * current_value - degree_index * previous
        ) / (degree_index + 1)
        previous = current_value
        current_value = following
    return current_value


def tables():
    node_values = [-1.0] + list(inner_nodes) + [1.0]
    poly_values = [legendre_seven(node) for node in node_values]
    weights = [2.0 / (56.0 * value * value) for value in poly_values]
    derivative = [[0.0] * 8 for row_index in range(8)]
    for row_index in range(8):
        for col_index in range(8):
            if row_index != col_index:
                derivative[row_index][col_index] = poly_values[row_index] / (
                    poly_values[col_index] * (node_values[row_index] - node_values[col_index])
                )
    derivative[0][0] = -14.0
    derivative[7][7] = 14.0
    squared_t = [
        [derivative[col_index][row_index] ** 2 for col_index in range(8)] for row_index in range(8)
    ]
    quad_list = [
        weights[first] * weights[second] * weights[third]
        for first in range(8)
        for second in range(8)
        for third in range(8)
    ]
    quadrature = jnp.asarray(quad_list, jnp.float32).reshape(1, 8, 8, 8, 1)
    return (quadrature, jnp.asarray(derivative, jnp.float32), jnp.asarray(squared_t, jnp.float32))


def apply_along(matrix, widened, values, direction):
    if direction == 0:
        return jnp.einsum("ij,sjbk->sibk", matrix, values, precision=lax.Precision.HIGHEST)
    if direction == 1:
        return jnp.einsum("ij,sajk->saik", matrix, values, precision=lax.Precision.HIGHEST)
    return jnp.einsum("ij,sabj->sabi", widened, values, precision=lax.Precision.HIGHEST)


def multiplicity(offsets, totals, block_shape, elements):
    slot_index = jnp.arange(elements, dtype=jnp.int32)
    places = (
        slot_index // (block_shape[1] * block_shape[2]),
        slot_index // block_shape[2] % block_shape[1],
        slot_index % block_shape[2],
    )
    node_index = jnp.arange(8, dtype=jnp.int32)
    first_node = (node_index == 0).astype(jnp.float32)[:, None]
    last_node = (node_index == 7).astype(jnp.float32)[:, None]
    factors = []
    for direction in range(3):
        position = places[direction] + offsets[direction]
        lower_open = (position > 0).astype(jnp.float32)[None, :]
        upper_open = (position < totals[direction] - 1).astype(jnp.float32)[None, :]
        factors.append(1.0 + first_node * lower_open + last_node * upper_open)
    joined = (
        factors[0][:, None, None, :] * factors[1][None, :, None, :] * factors[2][None, None, :, :]
    )
    return joined[None]


def face_take(values, direction, node, block_shape):
    elements = block_shape[0] * block_shape[1] * block_shape[2]
    if direction == 2:
        piece = lax.slice_in_dim(values, node * elements, (node + 1) * elements, axis=3)
    else:
        piece = lax.index_in_dim(values, node, 1 + direction, keepdims=False).reshape(
            values.shape[0], 8, 8, elements
        )
    return piece.reshape(piece.shape[:3] + tuple(block_shape))


def face_write(values, direction, node, piece, elements):
    flat = piece.reshape(piece.shape[:3] + (elements,))
    if direction == 2:
        return lax.dynamic_update_slice_in_dim(values, flat, node * elements, 3)
    widened = jnp.expand_dims(flat.reshape(flat.shape[0], 8, 8 * elements), 1 + direction)
    return lax.dynamic_update_slice_in_dim(values, widened, node, 1 + direction)


def assemble_axis(values, direction, block_shape, sender):
    elements = block_shape[0] * block_shape[1] * block_shape[2]
    lower_faces = face_take(values, direction, 0, block_shape)
    upper_faces = face_take(values, direction, 7, block_shape)
    element_axis = 3 + direction
    length = block_shape[direction]
    interior = lax.slice_in_dim(upper_faces, 0, length - 1, axis=element_axis) + lax.slice_in_dim(
        lower_faces, 1, length, axis=element_axis
    )
    lower_edge = lax.slice_in_dim(lower_faces, 0, 1, axis=element_axis)
    upper_edge = lax.slice_in_dim(upper_faces, length - 1, length, axis=element_axis)
    arrived = sender(jnp.stack([lower_edge, upper_edge]))
    first_sum = lower_edge + arrived[0]
    last_sum = upper_edge + arrived[3]
    new_lower = jnp.concatenate([first_sum, interior], axis=element_axis)
    new_upper = jnp.concatenate([interior, last_sum], axis=element_axis)
    values = face_write(values, direction, 0, new_lower, elements)
    return face_write(values, direction, 7, new_upper, elements)


def send_along_x(face_pair):
    return extended(face_pair, ((GX, 0),), 1)


def send_along_y(face_pair):
    return extended(face_pair, (("gy", 0),), 1)


def send_along_z(face_pair):
    return extended(face_pair, ((GZ, 0),), 1)


def assemble(values):
    block_shape = (BX, BY, BZ)
    values = assemble_axis(values, 0, block_shape, send_along_x)
    values = assemble_axis(values, 1, block_shape, send_along_y)
    return assemble_axis(values, 2, block_shape, send_along_z)


def joined_sums(residual, precond, applied_precond, inverse_copies):
    return (
        by_axis(jnp.sum(residual * precond * inverse_copies), GX_GY_GZ),
        by_axis(jnp.sum(precond * applied_precond * inverse_copies), GX_GY_GZ),
    )


def per_device(velocity, inv_density, element_place):
    elements = element_place.shape[0]
    width = 8 * elements
    quadrature, derivative, square_table = tables()
    identity = jnp.eye(elements, dtype=jnp.float32)
    derivative_wide = jnp.kron(derivative, identity)
    transpose_wide = jnp.kron(derivative.T, identity)
    square_wide = jnp.kron(square_table, identity)
    slot_index = jnp.arange(elements, dtype=jnp.int32)
    inverse = jnp.zeros((elements,), jnp.int32).at[element_place].set(slot_index)
    advector = jnp.take(velocity, inverse, axis=2).reshape(3, 8, 8, width)
    mobility = jnp.take(inv_density, inverse, axis=1).reshape(1, 8, 8, width)
    quad_wide = jnp.broadcast_to(quadrature, (1, 8, 8, 8, elements)).reshape(1, 8, 8, width)
    offsets = (lax.axis_index(GX) * BX, lax.axis_index("gy") * BY, lax.axis_index(GZ) * BZ)
    totals = (BX * lax.axis_size(GX), BY * lax.axis_size("gy"), BZ * lax.axis_size(GZ))
    copies = multiplicity(offsets, totals, (BX, BY, BZ), elements).reshape(1, 8, 8, width)
    mass = quad_wide * copies
    inverse_copies = 1.0 / copies

    def advection_rate(section_value):
        convective = advector[0:1] * apply_along(derivative, derivative_wide, section_value, 0)
        convective = convective + advector[1:2] * apply_along(
            derivative, derivative_wide, section_value, 1
        )
        convective = convective + advector[2:3] * apply_along(
            derivative, derivative_wide, section_value, 2
        )
        return assemble(-quad_wide * convective) / mass

    first_rate = advection_rate(advector)
    second_rate = advection_rate(advector + 0.5 * time_step * first_rate)
    third_rate = advection_rate(advector + 0.5 * time_step * second_rate)
    fourth_rate = advection_rate(advector + time_step * third_rate)
    advected = advector + time_step / 6.0 * (
        first_rate + 2.0 * second_rate + 2.0 * third_rate + fourth_rate
    )
    divergence = (
        apply_along(derivative, derivative_wide, advected[0:1], 0)
        + apply_along(derivative, derivative_wide, advected[1:2], 1)
        + apply_along(derivative, derivative_wide, advected[2:3], 2)
    )
    weighted = quad_wide * mobility
    diag_local = (
        mass_shift * quad_wide
        + apply_along(square_table, square_wide, weighted, 0)
        + apply_along(square_table, square_wide, weighted, 1)
        + apply_along(square_table, square_wide, weighted, 2)
    )
    source_local = -quad_wide * divergence / time_step
    assembled = assemble(jnp.concatenate([source_local, diag_local], axis=0))
    source = assembled[0:1]
    inverse_jacobi = 1.0 / assembled[1:2]

    def operator(values):
        summed = mass_shift * quad_wide * values
        for direction in range(3):
            slope = apply_along(derivative, derivative_wide, values, direction)
            summed = summed + apply_along(derivative.T, transpose_wide, weighted * slope, direction)
        return assemble(summed)

    pressure = jnp.zeros_like(source)
    residual = source
    precond = residual * inverse_jacobi
    applied_precond = operator(precond)
    current, curvature = joined_sums(residual, precond, applied_precond, inverse_copies)
    step_size = current / curvature
    search = precond
    applied_search = applied_precond
    for iteration in range(CG_ITERS):
        pressure = pressure + step_size * search
        residual = residual - step_size * applied_search
        if iteration + 1 < CG_ITERS:
            precond = residual * inverse_jacobi
            applied_precond = operator(precond)
            following, curvature = joined_sums(residual, precond, applied_precond, inverse_copies)
            ratio = following / current
            step_size = following / (curvature - ratio * following / step_size)
            search = precond + ratio * search
            applied_search = applied_precond + ratio * applied_search
            current = following
    advected_out = jnp.take(advected.reshape(3, 512, elements), element_place, axis=2)
    pressure_out = jnp.take(pressure.reshape(512, elements), element_place, axis=1)
    residual_out = jnp.take(residual.reshape(512, elements), element_place, axis=1)
    return (advected_out, pressure_out, residual_out)


def solution(mesh):
    torus = Mesh(
        mesh.devices.reshape(2, 2, mesh.shape["gy"], 32, 2), ("gx_0", "gx_1", "gy", "gz_0", "gz_1")
    )
    placed = (P(None, None, GX_GY_GZ), P(None, GX_GY_GZ), P(GX_GY_GZ))
    return jax.shard_map(
        per_device,
        mesh=torus,
        in_specs=placed,
        out_specs=(P(None, None, GX_GY_GZ), P(None, GX_GY_GZ), P(None, GX_GY_GZ)),
        check_vma=False,
    )
```

profile of v0, /device:TPU:6, one launch (start us, length us, event | category | flops | bytes accessed | tf_op | source)
XLA Modules:
  0.0 484.8 jit_solution(1921852989644304081)
XLA Ops:
  17.6 5.0 %collective-permute-done = f32[1,3,8,8,1,4,1]{2,5,3,1,6,4,0:T(4,128)S(1)} collective-permute-done((f32[1,3,8,8,1,4,1]{2,5,3,1,6,4,0:T(4,128)S(1)}, f32[1,3,8,8,1,4,1]{2,5,3,1,6,4,0:T(4,128)S(1)}, u32[]{:S(2)}, u32[]{:S(2)}) %collective-permute-start) | collective-permute-done | bytes 3104 | tf_op jit(solution)/shard_map/ppermute | solution.py:36
  24.6 4.5 collective-permute-done.3
  39.4 7.1 %collective-permute-start.5 = (f32[1,3,8,8,4,4,1]{3,2,5,4,1,6,0:T(8,128)}, f32[1,3,8,8,4,4,1]{3,2,5,4,1,6,0:T(8,128)}, u32[]{:S(2)}, u32[]{:S(2)}) collective-permute-start(f32[1,3,8,8,4,4,1]{3,2,5,4,1,6,0:T(8,128)} %bitcast.638), channel_id=1, source_target_pairs={{1,0},{2,1},{3,2},{4,3},{5,4},{6,5},{7,6},{8,7},{9,8},{10,9},{11,1... | collective-permute-start | bytes 36872 | tf_op jit(solution)/shard_map/ppermute | solution.py:38
  63.1 5.0 %collective-permute-done.6 = f32[1,3,8,8,1,4,1]{2,5,3,1,6,4,0:T(4,128)S(1)} collective-permute-done((f32[1,3,8,8,1,4,1]{2,5,3,1,6,4,0:T(4,128)S(1)}, f32[1,3,8,8,1,4,1]{2,5,3,1,6,4,0:T(4,128)S(1)}, u32[]{:S(2)}, u32[]{:S(2)}) %collective-permute-start.6) | collective-permute-done | bytes 3104 | tf_op jit(solution)/shard_map/ppermute | solution.py:36
  70.2 4.6 collective-permute-done.9
  105.6 5.1 %collective-permute-done.12 = f32[1,3,8,8,1,4,1]{2,5,3,1,6,4,0:T(4,128)S(1)} collective-permute-done((f32[1,3,8,8,1,4,1]{2,5,3,1,6,4,0:T(4,128)S(1)}, f32[1,3,8,8,1,4,1]{2,5,3,1,6,4,0:T(4,128)S(1)}, u32[]{:S(2)}, u32[]{:S(2)}) %collective-permute-start.12) | collective-permute-done | bytes 3104 | tf_op jit(solution)/shard_map/ppermute | solution.py:36
  112.7 5.0 %collective-permute-done.15 = f32[1,3,8,8,4,1,1]{2,4,3,1,6,5,0:T(4,128)} collective-permute-done((f32[1,3,8,8,4,1,1]{2,4,3,1,6,5,0:T(4,128)S(1)}, f32[1,3,8,8,4,1,1]{2,4,3,1,6,5,0:T(4,128)}, u32[]{:S(2)}, u32[]{:S(2)}) %collective-permute-start.15) | collective-permute-done | bytes 3104 | tf_op jit(solution)/shard_map/ppermute | solution.py:38
  128.4 4.1 collective-permute-start.17
  154.0 5.0 %collective-permute-done.18 = f32[1,3,8,8,1,4,1]{2,5,3,1,6,4,0:T(4,128)S(1)} collective-permute-done((f32[1,3,8,8,1,4,1]{2,5,3,1,6,4,0:T(4,128)S(1)}, f32[1,3,8,8,1,4,1]{2,5,3,1,6,4,0:T(4,128)S(1)}, u32[]{:S(2)}, u32[]{:S(2)}) %collective-permute-start.18) | collective-permute-done | bytes 3104 | tf_op jit(solution)/shard_map/ppermute | solution.py:36
  195.6 4.8 collective-permute-done.24
  202.3 4.7 collective-permute-done.27
  220.1 4.8 collective-permute-done.29
  234.7 4.6 collective-permute-done.30
  241.1 4.5 collective-permute-done.33
  257.7 4.8 collective-permute-done.35
  264.9 7.1 %all-reduce.9 = (f32[]{:T(128)}, f32[]{:T(128)}) all-reduce(f32[]{:T(128)} %get-tuple-element.11, f32[]{:T(128)} %get-tuple-element.10), channel_id=1, replica_groups=mesh['gx_0'=2,'gx_1'=2,'gy'=4,'gz_0'=32,'gz_1'=2] {'gx_0'}, use_global_device_ids=true, to_apply=%region_2.5 | all-reduce | flops 2 | bytes 16 | tf_op jit(solution)/shard_map/psum | solution.py:47
  275.0 10.8 %all-reduce.3 = (f32[]{:T(128)}, f32[]{:T(128)}) all-reduce(f32[]{:T(128)} %get-tuple-element.26, f32[]{:T(128)} %get-tuple-element.27), channel_id=1, replica_groups=mesh['gx_0'=2,'gx_1'=2,'gy'=4,'gz_0'=32,'gz_1'=2] {'gy'}, use_global_device_ids=true, to_apply=%region_4.7 | all-reduce | flops 2 | bytes 16 | tf_op jit(solution)/shard_map/psum | solution.py:47
  285.8 67.8 %all-reduce.1 = (f32[]{:T(128)}, f32[]{:T(128)}) all-reduce(f32[]{:T(128)} %get-tuple-element.18, f32[]{:T(128)} %get-tuple-element.19), channel_id=1, replica_groups=mesh['gx_0'=2,'gx_1'=2,'gy'=4,'gz_0'=32,'gz_1'=2] {'gz_0'}, use_global_device_ids=true, to_apply=%region_5.8 | all-reduce | flops 2 | bytes 16 | tf_op jit(solution)/shard_map/psum | solution.py:47
  353.6 5.6 %all-reduce.5 = (f32[]{:T(128)}, f32[]{:T(128)}) all-reduce(f32[]{:T(128)} %get-tuple-element.14, f32[]{:T(128)} %get-tuple-element.15), channel_id=1, replica_groups=mesh['gx_0'=2,'gx_1'=2,'gy'=4,'gz_0'=32,'gz_1'=2] {'gz_1'}, use_global_device_ids=true, to_apply=%region_6.9 | all-reduce | flops 2 | bytes 16 | tf_op jit(solution)/shard_map/psum | solution.py:47
  367.3 4.6 collective-permute-done.36
  394.0 7.1 %all-reduce.8 = (f32[]{:T(128)}, f32[]{:T(128)}) all-reduce(f32[]{:T(128)} %get-tuple-element.9, f32[]{:T(128)} %get-tuple-element.8), channel_id=1, replica_groups=mesh['gx_0'=2,'gx_1'=2,'gy'=4,'gz_0'=32,'gz_1'=2] {'gx_0'}, use_global_device_ids=true, to_apply=%region_14.17 | all-reduce | flops 2 | bytes 16 | tf_op jit(solution)/shard_map/psum | solution.py:47
  404.2 10.7 %all-reduce.2 = (f32[]{:T(128)}, f32[]{:T(128)}) all-reduce(f32[]{:T(128)} %get-tuple-element.24, f32[]{:T(128)} %get-tuple-element.25), channel_id=1, replica_groups=mesh['gx_0'=2,'gx_1'=2,'gy'=4,'gz_0'=32,'gz_1'=2] {'gy'}, use_global_device_ids=true, to_apply=%region_16.19 | all-reduce | flops 2 | bytes 16 | tf_op jit(solution)/shard_map/psum | solution.py:47
  414.9 57.1 %all-reduce = (f32[]{:T(128)}, f32[]{:T(128)}) all-reduce(f32[]{:T(128)} %get-tuple-element.16, f32[]{:T(128)} %get-tuple-element.17), channel_id=1, replica_groups=mesh['gx_0'=2,'gx_1'=2,'gy'=4,'gz_0'=32,'gz_1'=2] {'gz_0'}, use_global_device_ids=true, to_apply=%region_17.20 | all-reduce | flops 2 | bytes 16 | tf_op jit(solution)/shard_map/psum | solution.py:47
  472.0 5.6 %all-reduce.4 = (f32[]{:T(128)}, f32[]{:T(128)}) all-reduce(f32[]{:T(128)} %get-tuple-element.12, f32[]{:T(128)} %get-tuple-element.13), channel_id=1, replica_groups=mesh['gx_0'=2,'gx_1'=2,'gy'=4,'gz_0'=32,'gz_1'=2] {'gz_1'}, use_global_device_ids=true, to_apply=%region_18.21 | all-reduce | flops 2 | bytes 16 | tf_op jit(solution)/shard_map/psum | solution.py:47
  (460 shorter events, 225.7 us)
Async XLA Ops:
  15.6 6.9 %collective-permute-start = (f32[1,3,8,8,1,4,1]{2,5,3,1,6,4,0:T(4,128)S(1)}, f32[1,3,8,8,1,4,1]{2,5,3,1,6,4,0:T(4,128)S(1)}, u32[]{:S(2)}, u32[]{:S(2)}) collective-permute-start(f32[1,3,8,8,1,4,1]{2,5,3,1,6,4,0:T(4,128)S(1)} %get-tuple-element.57), channel_id=1, source_target_pairs={{0,256},{256,512},{512,768},{1,257},{257,513},{513,769},{2,258},{2... | collective-permute-start | bytes 9224 | tf_op jit(solution)/shard_map/ppermute | solution.py:36
  35.3 14.2 %collective-permute-start.4 = (f32[1,3,8,8,4,4,1]{3,2,5,4,1,6,0:T(8,128)S(1)}, f32[1,3,8,8,4,4,1]{3,2,5,4,1,6,0:T(8,128)S(1)}, u32[]{:S(2)}, u32[]{:S(2)}) collective-permute-start(f32[1,3,8,8,4,4,1]{3,2,5,4,1,6,0:T(8,128)S(1)} %bitcast.636), channel_id=1, source_target_pairs={{0,1},{1,2},{2,3},{3,4},{4,5},{5,6},{6,7},{7,8},{8,9},{9,10},{10,1... | collective-permute-start | bytes 36872 | tf_op jit(solution)/shard_map/ppermute | solution.py:36
  39.4 10.6 %collective-permute-start.5 = (f32[1,3,8,8,4,4,1]{3,2,5,4,1,6,0:T(8,128)}, f32[1,3,8,8,4,4,1]{3,2,5,4,1,6,0:T(8,128)}, u32[]{:S(2)}, u32[]{:S(2)}) collective-permute-start(f32[1,3,8,8,4,4,1]{3,2,5,4,1,6,0:T(8,128)} %bitcast.638), channel_id=1, source_target_pairs={{1,0},{2,1},{3,2},{4,3},{5,4},{6,5},{7,6},{8,7},{9,8},{10,9},{11,1... | collective-permute-start | bytes 36872 | tf_op jit(solution)/shard_map/ppermute | solution.py:38
  61.1 6.9 %collective-permute-start.6 = (f32[1,3,8,8,1,4,1]{2,5,3,1,6,4,0:T(4,128)S(1)}, f32[1,3,8,8,1,4,1]{2,5,3,1,6,4,0:T(4,128)S(1)}, u32[]{:S(2)}, u32[]{:S(2)}) collective-permute-start(f32[1,3,8,8,1,4,1]{2,5,3,1,6,4,0:T(4,128)S(1)} %get-tuple-element.51), channel_id=1, source_target_pairs={{0,256},{256,512},{512,768},{1,257},{257,513},{513,769},{2,258},{2... | collective-permute-start | bytes 9224 | tf_op jit(solution)/shard_map/ppermute | solution.py:36
  80.9 7.6 %collective-permute-start.10 = (f32[1,3,8,8,4,4,1]{3,2,5,4,1,6,0:T(8,128)S(1)}, f32[1,3,8,8,4,4,1]{3,2,5,4,1,6,0:T(8,128)S(1)}, u32[]{:S(2)}, u32[]{:S(2)}) collective-permute-start(f32[1,3,8,8,4,4,1]{3,2,5,4,1,6,0:T(8,128)S(1)} %bitcast.639), channel_id=1, source_target_pairs={{0,1},{1,2},{2,3},{3,4},{4,5},{5,6},{6,7},{7,8},{8,9},{9,10},{10,1... | collective-permute-start | bytes 36872 | tf_op jit(solution)/shard_map/ppermute | solution.py:36
  83.6 8.8 %collective-permute-start.11 = (f32[1,3,8,8,4,4,1]{3,2,5,4,1,6,0:T(8,128)}, f32[1,3,8,8,4,4,1]{3,2,5,4,1,6,0:T(8,128)}, u32[]{:S(2)}, u32[]{:S(2)}) collective-permute-start(f32[1,3,8,8,4,4,1]{3,2,5,4,1,6,0:T(8,128)} %bitcast.641), channel_id=1, source_target_pairs={{1,0},{2,1},{3,2},{4,3},{5,4},{6,5},{7,6},{8,7},{9,8},{10,9},{11,1... | collective-permute-start | bytes 36872 | tf_op jit(solution)/shard_map/ppermute | solution.py:38
  103.6 7.0 %collective-permute-start.12 = (f32[1,3,8,8,1,4,1]{2,5,3,1,6,4,0:T(4,128)S(1)}, f32[1,3,8,8,1,4,1]{2,5,3,1,6,4,0:T(4,128)S(1)}, u32[]{:S(2)}, u32[]{:S(2)}) collective-permute-start(f32[1,3,8,8,1,4,1]{2,5,3,1,6,4,0:T(4,128)S(1)} %get-tuple-element.45), channel_id=1, source_target_pairs={{0,256},{256,512},{512,768},{1,257},{257,513},{513,769},{2,258},{2... | collective-permute-start | bytes 9224 | tf_op jit(solution)/shard_map/ppermute | solution.py:36
  111.3 6.4 %collective-permute-start.15 = (f32[1,3,8,8,4,1,1]{2,4,3,1,6,5,0:T(4,128)S(1)}, f32[1,3,8,8,4,1,1]{2,4,3,1,6,5,0:T(4,128)}, u32[]{:S(2)}, u32[]{:S(2)}) collective-permute-start(f32[1,3,8,8,4,1,1]{2,4,3,1,6,5,0:T(4,128)S(1)} %bitcast.649), channel_id=1, source_target_pairs={{64,0},{128,64},{192,128},{65,1},{129,65},{193,129},{66,2},{130,66... | collective-permute-start | bytes 9224 | tf_op jit(solution)/shard_map/ppermute | solution.py:38
  126.4 7.8 %collective-permute-start.16 = (f32[1,3,8,8,4,4,1]{3,2,5,4,1,6,0:T(8,128)}, f32[1,3,8,8,4,4,1]{3,2,5,4,1,6,0:T(8,128)S(1)}, u32[]{:S(2)}, u32[]{:S(2)}) collective-permute-start(f32[1,3,8,8,4,4,1]{3,2,5,4,1,6,0:T(8,128)} %bitcast.76), channel_id=1, source_target_pairs={{0,1},{1,2},{2,3},{3,4},{4,5},{5,6},{6,7},{7,8},{8,9},{9,10},{10,1... | collective-permute-start | bytes 36872 | tf_op jit(solution)/shard_map/ppermute | solution.py:36
  128.4 8.8 %collective-permute-start.17 = (f32[1,3,8,8,4,4,1]{3,2,5,4,1,6,0:T(8,128)}, f32[1,3,8,8,4,4,1]{3,2,5,4,1,6,0:T(8,128)}, u32[]{:S(2)}, u32[]{:S(2)}) collective-permute-start(f32[1,3,8,8,4,4,1]{3,2,5,4,1,6,0:T(8,128)} %bitcast.78), channel_id=1, source_target_pairs={{1,0},{2,1},{3,2},{4,3},{5,4},{6,5},{7,6},{8,7},{9,8},{10,9},{11,1... | collective-permute-start | bytes 36872 | tf_op jit(solution)/shard_map/ppermute | solution.py:38
  152.0 6.9 %collective-permute-start.18 = (f32[1,3,8,8,1,4,1]{2,5,3,1,6,4,0:T(4,128)S(1)}, f32[1,3,8,8,1,4,1]{2,5,3,1,6,4,0:T(4,128)S(1)}, u32[]{:S(2)}, u32[]{:S(2)}) collective-permute-start(f32[1,3,8,8,1,4,1]{2,5,3,1,6,4,0:T(4,128)S(1)} %get-tuple-element.39), channel_id=1, source_target_pairs={{0,256},{256,512},{512,768},{1,257},{257,513},{513,769},{2,258},{2... | collective-permute-start | bytes 9224 | tf_op jit(solution)/shard_map/ppermute | solution.py:36
  159.6 6.3 %collective-permute-start.21 = (f32[1,3,8,8,4,1,1]{2,4,3,1,6,5,0:T(4,128)S(1)}, f32[1,3,8,8,4,1,1]{2,4,3,1,6,5,0:T(4,128)S(1)}, u32[]{:S(2)}, u32[]{:S(2)}) collective-permute-start(f32[1,3,8,8,4,1,1]{2,4,3,1,6,5,0:T(4,128)S(1)} %bitcast.643), channel_id=1, source_target_pairs={{64,0},{128,64},{192,128},{65,1},{129,65},{193,129},{66,2},{130,66... | collective-permute-start | bytes 9224 | tf_op jit(solution)/shard_map/ppermute | solution.py:38
  172.5 7.6 %collective-permute-start.22 = (f32[1,3,8,8,4,4,1]{3,2,5,4,1,6,0:T(8,128)S(1)}, f32[1,3,8,8,4,4,1]{3,2,5,4,1,6,0:T(8,128)S(1)}, u32[]{:S(2)}, u32[]{:S(2)}) collective-permute-start(f32[1,3,8,8,4,4,1]{3,2,5,4,1,6,0:T(8,128)S(1)} %bitcast.634), channel_id=1, source_target_pairs={{0,1},{1,2},{2,3},{3,4},{4,5},{5,6},{6,7},{7,8},{8,9},{9,10},{10,1... | collective-permute-start | bytes 36872 | tf_op jit(solution)/shard_map/ppermute | solution.py:36
  175.5 8.7 %collective-permute-start.23 = (f32[1,3,8,8,4,4,1]{3,2,5,4,1,6,0:T(8,128)S(1)}, f32[1,3,8,8,4,4,1]{3,2,5,4,1,6,0:T(8,128)S(1)}, u32[]{:S(2)}, u32[]{:S(2)}) collective-permute-start(f32[1,3,8,8,4,4,1]{3,2,5,4,1,6,0:T(8,128)S(1)} %bitcast.632), channel_id=1, source_target_pairs={{1,0},{2,1},{3,2},{4,3},{5,4},{6,5},{7,6},{8,7},{9,8},{10,9},{11,1... | collective-permute-start | bytes 36872 | tf_op jit(solution)/shard_map/ppermute | solution.py:38
  193.7 6.7 %collective-permute-start.24 = (f32[1,2,8,8,1,4,1]{2,5,3,1,6,4,0:T(4,128)S(1)}, f32[1,2,8,8,1,4,1]{2,5,3,1,6,4,0:T(4,128)S(1)}, u32[]{:S(2)}, u32[]{:S(2)}) collective-permute-start(f32[1,2,8,8,1,4,1]{2,5,3,1,6,4,0:T(4,128)S(1)} %get-tuple-element.71), channel_id=1, source_target_pairs={{0,256},{256,512},{512,768},{1,257},{257,513},{513,769},{2,258},{2... | collective-permute-start | bytes 6152 | tf_op jit(solution)/shard_map/ppermute | solution.py:36
  200.9 6.1 %collective-permute-start.27 = (f32[1,2,8,8,4,1,1]{2,4,3,1,6,5,0:T(4,128)S(1)}, f32[1,2,8,8,4,1,1]{2,4,3,1,6,5,0:T(4,128)S(1)}, u32[]{:S(2)}, u32[]{:S(2)}) collective-permute-start(f32[1,2,8,8,4,1,1]{2,4,3,1,6,5,0:T(4,128)S(1)} %bitcast.656), channel_id=1, source_target_pairs={{64,0},{128,64},{192,128},{65,1},{129,65},{193,129},{66,2},{130,66... | collective-permute-start | bytes 6152 | tf_op jit(solution)/shard_map/ppermute | solution.py:38
  213.1 6.9 %collective-permute-start.28 = (f32[1,2,8,8,4,4,1]{3,2,5,4,1,6,0:T(8,128)S(1)}, f32[1,2,8,8,4,4,1]{3,2,5,4,1,6,0:T(8,128)S(1)}, u32[]{:S(2)}, u32[]{:S(2)}) collective-permute-start(f32[1,2,8,8,4,4,1]{3,2,5,4,1,6,0:T(8,128)S(1)} %bitcast.658), channel_id=1, source_target_pairs={{0,1},{1,2},{2,3},{3,4},{4,5},{5,6},{6,7},{7,8},{8,9},{9,10},{10,1... | collective-permute-start | bytes 24584 | tf_op jit(solution)/shard_map/ppermute | solution.py:36
  217.2 7.8 %collective-permute-start.29 = (f32[1,2,8,8,4,4,1]{3,2,5,4,1,6,0:T(8,128)S(1)}, f32[1,2,8,8,4,4,1]{3,2,5,4,1,6,0:T(8,128)S(1)}, u32[]{:S(2)}, u32[]{:S(2)}) collective-permute-start(f32[1,2,8,8,4,4,1]{3,2,5,4,1,6,0:T(8,128)S(1)} %bitcast.660), channel_id=1, source_target_pairs={{1,0},{2,1},{3,2},{4,3},{5,4},{6,5},{7,6},{8,7},{9,8},{10,9},{11,1... | collective-permute-start | bytes 24584 | tf_op jit(solution)/shard_map/ppermute | solution.py:38
  232.8 6.5 %collective-permute-start.30 = (f32[1,1,8,8,1,4,1]{2,5,3,6,4,1,0:T(4,128)S(1)}, f32[1,1,8,8,1,4,1]{2,5,3,6,4,1,0:T(4,128)S(1)}, u32[]{:S(2)}, u32[]{:S(2)}) collective-permute-start(f32[1,1,8,8,1,4,1]{2,5,3,6,4,1,0:T(4,128)S(1)} %get-tuple-element.120), channel_id=1, source_target_pairs={{0,256},{256,512},{512,768},{1,257},{257,513},{513,769},{2,258},{2... | collective-permute-start | bytes 3080 | tf_op jit(solution)/shard_map/ppermute | solution.py:36
  251.4 6.2 %collective-permute-start.34 = (f32[1,1,8,8,4,4,1]{3,2,5,4,6,1,0:T(8,128)S(1)}, f32[1,1,8,8,4,4,1]{3,2,5,4,6,1,0:T(8,128)S(1)}, u32[]{:S(2)}, u32[]{:S(2)}) collective-permute-start(f32[1,1,8,8,4,4,1]{3,2,5,4,6,1,0:T(8,128)S(1)} %bitcast.670), channel_id=1, source_target_pairs={{0,1},{1,2},{2,3},{3,4},{4,5},{5,6},{6,7},{7,8},{8,9},{9,10},{10,1... | collective-permute-start | bytes 12296 | tf_op jit(solution)/shard_map/ppermute | solution.py:36
  255.5 7.1 %collective-permute-start.35 = (f32[1,1,8,8,4,4,1]{3,2,5,4,6,1,0:T(8,128)S(1)}, f32[1,1,8,8,4,4,1]{3,2,5,4,6,1,0:T(8,128)S(1)}, u32[]{:S(2)}, u32[]{:S(2)}) collective-permute-start(f32[1,1,8,8,4,4,1]{3,2,5,4,6,1,0:T(8,128)S(1)} %bitcast.674), channel_id=1, source_target_pairs={{1,0},{2,1},{3,2},{4,3},{5,4},{6,5},{7,6},{8,7},{9,8},{10,9},{11,1... | collective-permute-start | bytes 12296 | tf_op jit(solution)/shard_map/ppermute | solution.py:38
  365.3 6.5 %collective-permute-start.36 = (f32[1,1,8,8,1,4,1]{2,5,3,6,4,1,0:T(4,128)S(1)}, f32[1,1,8,8,1,4,1]{2,5,3,6,4,1,0:T(4,128)S(1)}, u32[]{:S(2)}, u32[]{:S(2)}) collective-permute-start(f32[1,1,8,8,1,4,1]{2,5,3,6,4,1,0:T(4,128)S(1)} %get-tuple-element.114), channel_id=1, source_target_pairs={{0,256},{256,512},{512,768},{1,257},{257,513},{513,769},{2,258},{2... | collective-permute-start | bytes 3080 | tf_op jit(solution)/shard_map/ppermute | solution.py:36
  382.6 6.7 %collective-permute-start.40 = (f32[1,1,8,8,4,4,1]{3,2,5,4,6,1,0:T(8,128)S(1)}, f32[1,1,8,8,4,4,1]{3,2,5,4,6,1,0:T(8,128)S(1)}, u32[]{:S(2)}, u32[]{:S(2)}) collective-permute-start(f32[1,1,8,8,4,4,1]{3,2,5,4,6,1,0:T(8,128)S(1)} %bitcast.672), channel_id=1, source_target_pairs={{0,1},{1,2},{2,3},{3,4},{4,5},{5,6},{6,7},{7,8},{8,9},{9,10},{10,1... | collective-permute-start | bytes 12296 | tf_op jit(solution)/shard_map/ppermute | solution.py:36
  384.6 7.1 %collective-permute-start.41 = (f32[1,1,8,8,4,4,1]{3,2,5,4,6,1,0:T(8,128)S(1)}, f32[1,1,8,8,4,4,1]{3,2,5,4,6,1,0:T(8,128)S(1)}, u32[]{:S(2)}, u32[]{:S(2)}) collective-permute-start(f32[1,1,8,8,4,4,1]{3,2,5,4,6,1,0:T(8,128)S(1)} %bitcast.668), channel_id=1, source_target_pairs={{1,0},{2,1},{3,2},{4,3},{5,4},{6,5},{7,6},{8,7},{9,8},{10,9},{11,1... | collective-permute-start | bytes 12296 | tf_op jit(solution)/shard_map/ppermute | solution.py:38
  (46 other events, 242.1 us)
where the time goes:
time: 487 us; the launch traced here: 485 us
  blocking collectives  178 us (37%)
  waiting for transfers between devices  113 us (23%)
  starting transfers between devices  109 us (22%)
  local copies, waits for them, and re-layouts  56.5 us (12%)
  other arithmetic  11.5 us (2%)
  between operations  9 us (2%)
  matrix products  7.07 us (1%)
    psum x10, blocking collectives, by_axis(): x = lax.psum(x, axis)  178 us
    ppermute x21, waiting for transfers between devices, extended(): lax.ppermute(head, axis, [((i + 1) % count, i) for i in range(ends)])  61.1 us
    ppermute x21, starting transfers between devices, extended(): lax.ppermute(tail, axis, [(i, (i + 1) % count) for i in range(ends)])  58.9 us
    ppermute x21, waiting for transfers between devices, extended(): lax.ppermute(tail, axis, [(i, (i + 1) % count) for i in range(ends)])  52.2 us
    ppermute x21, starting transfers between devices, extended(): lax.ppermute(head, axis, [((i + 1) % count, i) for i in range(ends)])  50.6 us
    dynamic_update_slice x14, local copies, waits for them, and re-layouts, face_write(): return lax.dynamic_update_slice_in_dim(values, flat, node * elements, 3)  22.8 us
  transfers between devices with their start and end apart: 42, of which 41 were waited for; matrix products, arithmetic and copies ran while one was open for 2% of the time, Pallas kernels for 0%

commit v1 on v0

--- a/solution.py
+++ b/solution.py
@@ -10,6 +10,7 @@
 CG_ITERS = 2
 GX = ("gx_0", "gx_1")
 GZ = ("gz_0", "gz_1")
+GX_GY = ("gx_0", "gx_1", "gy")
 GX_GY_GZ = ("gx_0", "gx_1", "gy", "gz_0", "gz_1")
 
 
@@ -42,10 +43,13 @@
     return cells
 
 
-def by_axis(x, axes):
-    for axis in axes:
-        x = lax.psum(x, axis)
-    return x
+def total(values):
+    row = jnp.pad(jnp.stack(values), (0, 124)).reshape(1, 128)
+    for axes in (GZ, GX_GY):
+        count = lax.axis_size(axes)
+        pieces = lax.all_to_all(jnp.broadcast_to(row[None], (count, 1, 128)), axes, 0, 0)
+        row = jnp.sum(pieces, axis=0)
+    return [row[0, index] for index in range(len(values))]
 
 
 def legendre_seven(position):
@@ -174,13 +178,6 @@
     return assemble_axis(values, 2, block_shape, send_along_z)
 
 
-def joined_sums(residual, precond, applied_precond, inverse_copies):
-    return (
-        by_axis(jnp.sum(residual * precond * inverse_copies), GX_GY_GZ),
-        by_axis(jnp.sum(precond * applied_precond * inverse_copies), GX_GY_GZ),
-    )
-
-
 def per_device(velocity, inv_density, element_place):
     elements = element_place.shape[0]
     width = 8 * elements
@@ -241,26 +238,27 @@
             summed = summed + apply_along(derivative.T, transpose_wide, weighted * slope, direction)
         return assemble(summed)
 
-    pressure = jnp.zeros_like(source)
-    residual = source
-    precond = residual * inverse_jacobi
-    applied_precond = operator(precond)
-    current, curvature = joined_sums(residual, precond, applied_precond, inverse_copies)
-    step_size = current / curvature
-    search = precond
-    applied_search = applied_precond
-    for iteration in range(CG_ITERS):
-        pressure = pressure + step_size * search
-        residual = residual - step_size * applied_search
-        if iteration + 1 < CG_ITERS:
-            precond = residual * inverse_jacobi
-            applied_precond = operator(precond)
-            following, curvature = joined_sums(residual, precond, applied_precond, inverse_copies)
-            ratio = following / current
-            step_size = following / (curvature - ratio * following / step_size)
-            search = precond + ratio * search
-            applied_search = applied_precond + ratio * applied_search
-            current = following
+    first = source * inverse_jacobi
+    first_applied = operator(first)
+    second = first_applied * inverse_jacobi
+    second_applied = operator(second)
+    rho, curvature, cross, last = total(
+        [
+            jnp.sum(source * first * inverse_copies),
+            jnp.sum(first * first_applied * inverse_copies),
+            jnp.sum(first_applied * second * inverse_copies),
+            jnp.sum(second * second_applied * inverse_copies),
+        ]
+    )
+    step = rho / curvature
+    rho_next = step * step * cross - rho
+    ratio = rho_next / rho
+    step_next = rho_next / (
+        curvature - 2.0 * step * cross + step * step * last - ratio * ratio * curvature
+    )
+    keep = step + step_next * (1.0 + ratio)
+    pressure = keep * first - step_next * step * second
+    residual = source - keep * first_applied + step_next * step * second_applied
     advected_out = jnp.take(advected.reshape(3, 512, elements), element_place, axis=2)
     pressure_out = jnp.take(pressure.reshape(512, elements), element_place, axis=1)
     residual_out = jnp.take(residual.reshape(512, elements), element_place, axis=1)

time: 487 us -> 384 us (0.79)
  blocking collectives: 178 us -> 0 us
  starting transfers between devices: 109 us -> 147 us
  waiting for transfers between devices: 113 us -> 142 us
    psum x10 -> x0, blocking collectives: 178 us -> none  [by_axis(): x = lax.psum(x, axis)]
    all_to_all x0 -> x2, starting transfers between devices: none -> 36.3 us  [total(): lax.all_to_all(jnp.broadcast_to(row[None], (count, 1, 128)), axes, 0, 0)]
    all_to_all x0 -> x2, waiting for transfers between devices: none -> 24.5 us  [total(): lax.all_to_all(jnp.broadcast_to(row[None], (count, 1, 128)), axes, 0, 0)]
  transfers between devices with their start and end apart: 42 -> 44, of which waited for: 41 -> 43; matrix products, arithmetic and copies ran while one was open for 2% -> 3% of each run, Pallas kernels for 0% -> 0%
where the time goes in v1:
time: 384 us; the launch traced here: 378 us
  starting transfers between devices  147 us (38%)
  waiting for transfers between devices  142 us (37%)
  local copies, waits for them, and re-layouts  59 us (15%)
  other arithmetic  13.6 us (4%)
  between operations  8.91 us (2%)
  matrix products  7.08 us (2%)
    ppermute x21, waiting for transfers between devices, extended(): lax.ppermute(head, axis, [((i + 1) % count, i) for i in range(ends)])  65.3 us
    ppermute x21, starting transfers between devices, extended(): lax.ppermute(tail, axis, [(i, (i + 1) % count) for i in range(ends)])  62.1 us
    ppermute x21, waiting for transfers between devices, extended(): lax.ppermute(tail, axis, [(i, (i + 1) % count) for i in range(ends)])  52.3 us
    ppermute x21, starting transfers between devices, extended(): lax.ppermute(head, axis, [((i + 1) % count, i) for i in range(ends)])  48.6 us
    all_to_all x2, starting transfers between devices, total(): lax.all_to_all(jnp.broadcast_to(row[None], (count, 1, 128)), axes, 0, 0)  36.3 us
    all_to_all x2, waiting for transfers between devices, total(): lax.all_to_all(jnp.broadcast_to(row[None], (count, 1, 128)), axes, 0, 0)  24.5 us
    dynamic_update_slice x14, local copies, waits for them, and re-layouts, face_write(): return lax.dynamic_update_slice_in_dim(values, flat, node * elements, 3)  22.8 us
  transfers between devices with their start and end apart: 44, of which 43 were waited for; matrix products, arithmetic and copies ran while one was open for 3% of the time, Pallas kernels for 0%

profile of v1, /device:TPU:6, one launch (start us, length us, event | category | flops | bytes accessed | tf_op | source)
XLA Modules:
  0.0 377.7 jit_solution(14177729006632761441)
XLA Ops:
  17.6 5.0 %collective-permute-done = f32[1,3,8,8,1,4,1]{2,5,3,1,6,4,0:T(4,128)S(1)} collective-permute-done((f32[1,3,8,8,1,4,1]{2,5,3,1,6,4,0:T(4,128)S(1)}, f32[1,3,8,8,1,4,1]{2,5,3,1,6,4,0:T(4,128)S(1)}, u32[]{:S(2)}, u32[]{:S(2)}) %collective-permute-start) | collective-permute-done | bytes 3104 | tf_op jit(solution)/shard_map/ppermute | solution.py:37
  24.7 4.5 %collective-permute-done.3 = f32[1,3,8,8,4,1,1]{2,4,3,1,6,5,0:T(4,128)S(1)} collective-permute-done((f32[1,3,8,8,4,1,1]{2,4,3,1,6,5,0:T(4,128)S(1)}, f32[1,3,8,8,4,1,1]{2,4,3,1,6,5,0:T(4,128)S(1)}, u32[]{:S(2)}, u32[]{:S(2)}) %collective-permute-start.3) | collective-permute-done | bytes 3104 | tf_op jit(solution)/shard_map/ppermute | solution.py:39
  39.4 7.1 %collective-permute-start.5 = (f32[1,3,8,8,4,4,1]{3,2,5,4,1,6,0:T(8,128)}, f32[1,3,8,8,4,4,1]{3,2,5,4,1,6,0:T(8,128)}, u32[]{:S(2)}, u32[]{:S(2)}) collective-permute-start(f32[1,3,8,8,4,4,1]{3,2,5,4,1,6,0:T(8,128)} %bitcast.649), channel_id=1, source_target_pairs={{1,0},{2,1},{3,2},{4,3},{5,4},{6,5},{7,6},{8,7},{9,8},{10,9},{11,1... | collective-permute-start | bytes 36872 | tf_op jit(solution)/shard_map/ppermute | solution.py:39
  63.2 5.0 %collective-permute-done.6 = f32[1,3,8,8,1,4,1]{2,5,3,1,6,4,0:T(4,128)S(1)} collective-permute-done((f32[1,3,8,8,1,4,1]{2,5,3,1,6,4,0:T(4,128)S(1)}, f32[1,3,8,8,1,4,1]{2,5,3,1,6,4,0:T(4,128)S(1)}, u32[]{:S(2)}, u32[]{:S(2)}) %collective-permute-start.6) | collective-permute-done | bytes 3104 | tf_op jit(solution)/shard_map/ppermute | solution.py:37
  70.2 4.6 %collective-permute-done.9 = f32[1,3,8,8,4,1,1]{2,4,3,1,6,5,0:T(4,128)S(1)} collective-permute-done((f32[1,3,8,8,4,1,1]{2,4,3,1,6,5,0:T(4,128)S(1)}, f32[1,3,8,8,4,1,1]{2,4,3,1,6,5,0:T(4,128)S(1)}, u32[]{:S(2)}, u32[]{:S(2)}) %collective-permute-start.9) | collective-permute-done | bytes 3104 | tf_op jit(solution)/shard_map/ppermute | solution.py:39
  105.6 5.1 %collective-permute-done.12 = f32[1,3,8,8,1,4,1]{2,5,3,1,6,4,0:T(4,128)S(1)} collective-permute-done((f32[1,3,8,8,1,4,1]{2,5,3,1,6,4,0:T(4,128)S(1)}, f32[1,3,8,8,1,4,1]{2,5,3,1,6,4,0:T(4,128)S(1)}, u32[]{:S(2)}, u32[]{:S(2)}) %collective-permute-start.12) | collective-permute-done | bytes 3104 | tf_op jit(solution)/shard_map/ppermute | solution.py:37
  112.8 5.0 %collective-permute-done.15 = f32[1,3,8,8,4,1,1]{2,4,3,1,6,5,0:T(4,128)} collective-permute-done((f32[1,3,8,8,4,1,1]{2,4,3,1,6,5,0:T(4,128)S(1)}, f32[1,3,8,8,4,1,1]{2,4,3,1,6,5,0:T(4,128)}, u32[]{:S(2)}, u32[]{:S(2)}) %collective-permute-start.15) | collective-permute-done | bytes 3104 | tf_op jit(solution)/shard_map/ppermute | solution.py:39
  128.4 4.1 %collective-permute-start.17 = (f32[1,3,8,8,4,4,1]{3,2,5,4,1,6,0:T(8,128)}, f32[1,3,8,8,4,4,1]{3,2,5,4,1,6,0:T(8,128)}, u32[]{:S(2)}, u32[]{:S(2)}) collective-permute-start(f32[1,3,8,8,4,4,1]{3,2,5,4,1,6,0:T(8,128)} %bitcast.78), channel_id=1, source_target_pairs={{1,0},{2,1},{3,2},{4,3},{5,4},{6,5},{7,6},{8,7},{9,8},{10,9},{11,1... | collective-permute-start | bytes 36872 | tf_op jit(solution)/shard_map/ppermute | solution.py:39
  154.0 5.0 %collective-permute-done.18 = f32[1,3,8,8,1,4,1]{2,5,3,1,6,4,0:T(4,128)S(1)} collective-permute-done((f32[1,3,8,8,1,4,1]{2,5,3,1,6,4,0:T(4,128)S(1)}, f32[1,3,8,8,1,4,1]{2,5,3,1,6,4,0:T(4,128)S(1)}, u32[]{:S(2)}, u32[]{:S(2)}) %collective-permute-start.18) | collective-permute-done | bytes 3104 | tf_op jit(solution)/shard_map/ppermute | solution.py:37
  180.2 4.0 %collective-permute-done.23 = f32[1,3,8,8,4,4,1]{3,2,5,4,1,6,0:T(8,128)S(1)} collective-permute-done((f32[1,3,8,8,4,4,1]{3,2,5,4,1,6,0:T(8,128)S(1)}, f32[1,3,8,8,4,4,1]{3,2,5,4,1,6,0:T(8,128)S(1)}, u32[]{:S(2)}, u32[]{:S(2)}) %collective-permute-start.23) | collective-permute-done | bytes 12320 | tf_op jit(solution)/shard_map/ppermute | solution.py:39
  195.6 4.8 %collective-permute-done.24 = f32[1,2,8,8,1,4,1]{2,5,3,1,6,4,0:T(4,128)S(1)} collective-permute-done((f32[1,2,8,8,1,4,1]{2,5,3,1,6,4,0:T(4,128)S(1)}, f32[1,2,8,8,1,4,1]{2,5,3,1,6,4,0:T(4,128)S(1)}, u32[]{:S(2)}, u32[]{:S(2)}) %collective-permute-start.24) | collective-permute-done | bytes 2080 | tf_op jit(solution)/shard_map/ppermute | solution.py:37
  202.3 4.7 %collective-permute-done.27 = f32[1,2,8,8,4,1,1]{2,4,3,1,6,5,0:T(4,128)S(1)} collective-permute-done((f32[1,2,8,8,4,1,1]{2,4,3,1,6,5,0:T(4,128)S(1)}, f32[1,2,8,8,4,1,1]{2,4,3,1,6,5,0:T(4,128)S(1)}, u32[]{:S(2)}, u32[]{:S(2)}) %collective-permute-start.27) | collective-permute-done | bytes 2080 | tf_op jit(solution)/shard_map/ppermute | solution.py:39
  220.1 4.8 %collective-permute-done.29 = f32[1,2,8,8,4,4,1]{3,2,5,4,1,6,0:T(8,128)S(1)} collective-permute-done((f32[1,2,8,8,4,4,1]{3,2,5,4,1,6,0:T(8,128)S(1)}, f32[1,2,8,8,4,4,1]{3,2,5,4,1,6,0:T(8,128)S(1)}, u32[]{:S(2)}, u32[]{:S(2)}) %collective-permute-start.29) | collective-permute-done | bytes 8224 | tf_op jit(solution)/shard_map/ppermute | solution.py:39
  234.7 4.6 %collective-permute-done.30 = f32[1,1,8,8,1,4,1]{2,5,3,6,4,1,0:T(4,128)S(1)} collective-permute-done((f32[1,1,8,8,1,4,1]{2,5,3,6,4,1,0:T(4,128)S(1)}, f32[1,1,8,8,1,4,1]{2,5,3,6,4,1,0:T(4,128)S(1)}, u32[]{:S(2)}, u32[]{:S(2)}) %collective-permute-start.30) | collective-permute-done | bytes 1056 | tf_op jit(solution)/shard_map/ppermute | solution.py:37
  241.1 4.5 %collective-permute-done.33 = f32[1,1,8,8,4,1,1]{2,4,3,6,5,1,0:T(4,128)S(1)} collective-permute-done((f32[1,1,8,8,4,1,1]{2,4,3,6,5,1,0:T(4,128)S(1)}, f32[1,1,8,8,4,1,1]{2,4,3,6,5,1,0:T(4,128)S(1)}, u32[]{:S(2)}, u32[]{:S(2)}) %collective-permute-start.33) | collective-permute-done | bytes 1056 | tf_op jit(solution)/shard_map/ppermute | solution.py:39
  251.5 3.9 %collective-permute-start.34 = (f32[1,1,8,8,4,4,1]{3,2,5,4,6,1,0:T(8,128)S(1)}, f32[1,1,8,8,4,4,1]{3,2,5,4,6,1,0:T(8,128)S(1)}, u32[]{:S(2)}, u32[]{:S(2)}) collective-permute-start(f32[1,1,8,8,4,4,1]{3,2,5,4,6,1,0:T(8,128)S(1)} %bitcast.684), channel_id=1, source_target_pairs={{0,1},{1,2},{2,3},{3,4},{4,5},{5,6},{6,7},{7,8},{8,9},{9,10},{10,1... | collective-permute-start | bytes 12296 | tf_op jit(solution)/shard_map/ppermute | solution.py:37
  257.7 4.8 %collective-permute-done.35 = f32[1,1,8,8,4,4,1]{3,2,5,4,6,1,0:T(8,128)S(1)} collective-permute-done((f32[1,1,8,8,4,4,1]{3,2,5,4,6,1,0:T(8,128)S(1)}, f32[1,1,8,8,4,4,1]{3,2,5,4,6,1,0:T(8,128)S(1)}, u32[]{:S(2)}, u32[]{:S(2)}) %collective-permute-start.35) | collective-permute-done | bytes 4128 | tf_op jit(solution)/shard_map/ppermute | solution.py:39
  271.0 4.6 %collective-permute-done.36 = f32[1,1,8,8,1,4,1]{2,5,3,6,4,1,0:T(4,128)S(1)} collective-permute-done((f32[1,1,8,8,1,4,1]{2,5,3,6,4,1,0:T(4,128)S(1)}, f32[1,1,8,8,1,4,1]{2,5,3,6,4,1,0:T(4,128)S(1)}, u32[]{:S(2)}, u32[]{:S(2)}) %collective-permute-start.36) | collective-permute-done | bytes 1056 | tf_op jit(solution)/shard_map/ppermute | solution.py:37
  277.4 4.5 %collective-permute-done.39 = f32[1,1,8,8,4,1,1]{2,4,3,6,5,1,0:T(4,128)S(1)} collective-permute-done((f32[1,1,8,8,4,1,1]{2,4,3,6,5,1,0:T(4,128)S(1)}, f32[1,1,8,8,4,1,1]{2,4,3,6,5,1,0:T(4,128)S(1)}, u32[]{:S(2)}, u32[]{:S(2)}) %collective-permute-start.39) | collective-permute-done | bytes 1056 | tf_op jit(solution)/shard_map/ppermute | solution.py:39
  287.7 3.9 %collective-permute-start.40 = (f32[1,1,8,8,4,4,1]{3,2,5,4,6,1,0:T(8,128)S(1)}, f32[1,1,8,8,4,4,1]{3,2,5,4,6,1,0:T(8,128)S(1)}, u32[]{:S(2)}, u32[]{:S(2)}) collective-permute-start(f32[1,1,8,8,4,4,1]{3,2,5,4,6,1,0:T(8,128)S(1)} %bitcast.680), channel_id=1, source_target_pairs={{0,1},{1,2},{2,3},{3,4},{4,5},{5,6},{6,7},{7,8},{8,9},{9,10},{10,1... | collective-permute-start | bytes 12296 | tf_op jit(solution)/shard_map/ppermute | solution.py:37
  294.1 4.7 %collective-permute-done.41 = f32[1,1,8,8,4,4,1]{3,2,5,4,6,1,0:T(8,128)S(1)} collective-permute-done((f32[1,1,8,8,4,4,1]{3,2,5,4,6,1,0:T(8,128)S(1)}, f32[1,1,8,8,4,4,1]{3,2,5,4,6,1,0:T(8,128)S(1)}, u32[]{:S(2)}, u32[]{:S(2)}) %collective-permute-start.41) | collective-permute-done | bytes 4128 | tf_op jit(solution)/shard_map/ppermute | solution.py:39
  304.5 28.2 %all-to-all-start = ((f32[64,1,128]{2,1,0:T(1,128)}), f32[64,1,128]{2,1,0:T(1,128)S(1)}, u32[]{:S(2)}, u32[]{:S(2)}) async-start(f32[64,1,128]{2,1,0:T(1,128)} %broadcast_in_dim.69), calls=%async_computation | async-start | bytes 65536 | tf_op jit(solution)/shard_map/all_to_all | solution.py:50
  333.9 21.3 %all-to-all-done = f32[64,1,128]{2,1,0:T(1,128)S(1)} async-done(((f32[64,1,128]{2,1,0:T(1,128)}), f32[64,1,128]{2,1,0:T(1,128)S(1)}, u32[]{:S(2)}, u32[]{:S(2)}) %all-to-all-start) | async-done | bytes 32800 | tf_op jit(solution)/shard_map/all_to_all | solution.py:50
  355.8 8.2 %all-to-all-start.1 = ((f32[16,1,128]{2,1,0:T(1,128)}), f32[16,1,128]{2,1,0:T(1,128)S(1)}, u32[]{:S(2)}, u32[]{:S(2)}) async-start(f32[16,1,128]{2,1,0:T(1,128)} %broadcast_in_dim.70), calls=%async_computation.1 | async-start | bytes 16384 | tf_op jit(solution)/shard_map/all_to_all | solution.py:50
  (459 shorter events, 211.9 us)
Async XLA Ops:
  15.6 6.9 %collective-permute-start = (f32[1,3,8,8,1,4,1]{2,5,3,1,6,4,0:T(4,128)S(1)}, f32[1,3,8,8,1,4,1]{2,5,3,1,6,4,0:T(4,128)S(1)}, u32[]{:S(2)}, u32[]{:S(2)}) collective-permute-start(f32[1,3,8,8,1,4,1]{2,5,3,1,6,4,0:T(4,128)S(1)} %get-tuple-element.43), channel_id=1, source_target_pairs={{0,256},{256,512},{512,768},{1,257},{257,513},{513,769},{2,258},{2... | collective-permute-start | bytes 9224 | tf_op jit(solution)/shard_map/ppermute | solution.py:37
  35.4 14.2 %collective-permute-start.4 = (f32[1,3,8,8,4,4,1]{3,2,5,4,1,6,0:T(8,128)S(1)}, f32[1,3,8,8,4,4,1]{3,2,5,4,1,6,0:T(8,128)S(1)}, u32[]{:S(2)}, u32[]{:S(2)}) collective-permute-start(f32[1,3,8,8,4,4,1]{3,2,5,4,1,6,0:T(8,128)S(1)} %bitcast.647), channel_id=1, source_target_pairs={{0,1},{1,2},{2,3},{3,4},{4,5},{5,6},{6,7},{7,8},{8,9},{9,10},{10,1... | collective-permute-start | bytes 36872 | tf_op jit(solution)/shard_map/ppermute | solution.py:37
  39.4 10.6 %collective-permute-start.5 = (f32[1,3,8,8,4,4,1]{3,2,5,4,1,6,0:T(8,128)}, f32[1,3,8,8,4,4,1]{3,2,5,4,1,6,0:T(8,128)}, u32[]{:S(2)}, u32[]{:S(2)}) collective-permute-start(f32[1,3,8,8,4,4,1]{3,2,5,4,1,6,0:T(8,128)} %bitcast.649), channel_id=1, source_target_pairs={{1,0},{2,1},{3,2},{4,3},{5,4},{6,5},{7,6},{8,7},{9,8},{10,9},{11,1... | collective-permute-start | bytes 36872 | tf_op jit(solution)/shard_map/ppermute | solution.py:39
  61.2 6.9 %collective-permute-start.6 = (f32[1,3,8,8,1,4,1]{2,5,3,1,6,4,0:T(4,128)S(1)}, f32[1,3,8,8,1,4,1]{2,5,3,1,6,4,0:T(4,128)S(1)}, u32[]{:S(2)}, u32[]{:S(2)}) collective-permute-start(f32[1,3,8,8,1,4,1]{2,5,3,1,6,4,0:T(4,128)S(1)} %get-tuple-element.37), channel_id=1, source_target_pairs={{0,256},{256,512},{512,768},{1,257},{257,513},{513,769},{2,258},{2... | collective-permute-start | bytes 9224 | tf_op jit(solution)/shard_map/ppermute | solution.py:37
  80.9 7.6 %collective-permute-start.10 = (f32[1,3,8,8,4,4,1]{3,2,5,4,1,6,0:T(8,128)S(1)}, f32[1,3,8,8,4,4,1]{3,2,5,4,1,6,0:T(8,128)S(1)}, u32[]{:S(2)}, u32[]{:S(2)}) collective-permute-start(f32[1,3,8,8,4,4,1]{3,2,5,4,1,6,0:T(8,128)S(1)} %bitcast.650), channel_id=1, source_target_pairs={{0,1},{1,2},{2,3},{3,4},{4,5},{5,6},{6,7},{7,8},{8,9},{9,10},{10,1... | collective-permute-start | bytes 36872 | tf_op jit(solution)/shard_map/ppermute | solution.py:37
  83.7 8.8 %collective-permute-start.11 = (f32[1,3,8,8,4,4,1]{3,2,5,4,1,6,0:T(8,128)}, f32[1,3,8,8,4,4,1]{3,2,5,4,1,6,0:T(8,128)}, u32[]{:S(2)}, u32[]{:S(2)}) collective-permute-start(f32[1,3,8,8,4,4,1]{3,2,5,4,1,6,0:T(8,128)} %bitcast.652), channel_id=1, source_target_pairs={{1,0},{2,1},{3,2},{4,3},{5,4},{6,5},{7,6},{8,7},{9,8},{10,9},{11,1... | collective-permute-start | bytes 36872 | tf_op jit(solution)/shard_map/ppermute | solution.py:39
  103.6 7.0 %collective-permute-start.12 = (f32[1,3,8,8,1,4,1]{2,5,3,1,6,4,0:T(4,128)S(1)}, f32[1,3,8,8,1,4,1]{2,5,3,1,6,4,0:T(4,128)S(1)}, u32[]{:S(2)}, u32[]{:S(2)}) collective-permute-start(f32[1,3,8,8,1,4,1]{2,5,3,1,6,4,0:T(4,128)S(1)} %get-tuple-element.31), channel_id=1, source_target_pairs={{0,256},{256,512},{512,768},{1,257},{257,513},{513,769},{2,258},{2... | collective-permute-start | bytes 9224 | tf_op jit(solution)/shard_map/ppermute | solution.py:37
  111.3 6.4 %collective-permute-start.15 = (f32[1,3,8,8,4,1,1]{2,4,3,1,6,5,0:T(4,128)S(1)}, f32[1,3,8,8,4,1,1]{2,4,3,1,6,5,0:T(4,128)}, u32[]{:S(2)}, u32[]{:S(2)}) collective-permute-start(f32[1,3,8,8,4,1,1]{2,4,3,1,6,5,0:T(4,128)S(1)} %bitcast.660), channel_id=1, source_target_pairs={{64,0},{128,64},{192,128},{65,1},{129,65},{193,129},{66,2},{130,66... | collective-permute-start | bytes 9224 | tf_op jit(solution)/shard_map/ppermute | solution.py:39
  126.4 7.8 %collective-permute-start.16 = (f32[1,3,8,8,4,4,1]{3,2,5,4,1,6,0:T(8,128)}, f32[1,3,8,8,4,4,1]{3,2,5,4,1,6,0:T(8,128)S(1)}, u32[]{:S(2)}, u32[]{:S(2)}) collective-permute-start(f32[1,3,8,8,4,4,1]{3,2,5,4,1,6,0:T(8,128)} %bitcast.76), channel_id=1, source_target_pairs={{0,1},{1,2},{2,3},{3,4},{4,5},{5,6},{6,7},{7,8},{8,9},{9,10},{10,1... | collective-permute-start | bytes 36872 | tf_op jit(solution)/shard_map/ppermute | solution.py:37
  128.4 8.8 %collective-permute-start.17 = (f32[1,3,8,8,4,4,1]{3,2,5,4,1,6,0:T(8,128)}, f32[1,3,8,8,4,4,1]{3,2,5,4,1,6,0:T(8,128)}, u32[]{:S(2)}, u32[]{:S(2)}) collective-permute-start(f32[1,3,8,8,4,4,1]{3,2,5,4,1,6,0:T(8,128)} %bitcast.78), channel_id=1, source_target_pairs={{1,0},{2,1},{3,2},{4,3},{5,4},{6,5},{7,6},{8,7},{9,8},{10,9},{11,1... | collective-permute-start | bytes 36872 | tf_op jit(solution)/shard_map/ppermute | solution.py:39
  152.0 6.9 %collective-permute-start.18 = (f32[1,3,8,8,1,4,1]{2,5,3,1,6,4,0:T(4,128)S(1)}, f32[1,3,8,8,1,4,1]{2,5,3,1,6,4,0:T(4,128)S(1)}, u32[]{:S(2)}, u32[]{:S(2)}) collective-permute-start(f32[1,3,8,8,1,4,1]{2,5,3,1,6,4,0:T(4,128)S(1)} %get-tuple-element.25), channel_id=1, source_target_pairs={{0,256},{256,512},{512,768},{1,257},{257,513},{513,769},{2,258},{2... | collective-permute-start | bytes 9224 | tf_op jit(solution)/shard_map/ppermute | solution.py:37
  159.6 6.3 %collective-permute-start.21 = (f32[1,3,8,8,4,1,1]{2,4,3,1,6,5,0:T(4,128)S(1)}, f32[1,3,8,8,4,1,1]{2,4,3,1,6,5,0:T(4,128)S(1)}, u32[]{:S(2)}, u32[]{:S(2)}) collective-permute-start(f32[1,3,8,8,4,1,1]{2,4,3,1,6,5,0:T(4,128)S(1)} %bitcast.654), channel_id=1, source_target_pairs={{64,0},{128,64},{192,128},{65,1},{129,65},{193,129},{66,2},{130,66... | collective-permute-start | bytes 9224 | tf_op jit(solution)/shard_map/ppermute | solution.py:39
  172.5 7.6 %collective-permute-start.22 = (f32[1,3,8,8,4,4,1]{3,2,5,4,1,6,0:T(8,128)S(1)}, f32[1,3,8,8,4,4,1]{3,2,5,4,1,6,0:T(8,128)S(1)}, u32[]{:S(2)}, u32[]{:S(2)}) collective-permute-start(f32[1,3,8,8,4,4,1]{3,2,5,4,1,6,0:T(8,128)S(1)} %bitcast.645), channel_id=1, source_target_pairs={{0,1},{1,2},{2,3},{3,4},{4,5},{5,6},{6,7},{7,8},{8,9},{9,10},{10,1... | collective-permute-start | bytes 36872 | tf_op jit(solution)/shard_map/ppermute | solution.py:37
  175.5 8.7 %collective-permute-start.23 = (f32[1,3,8,8,4,4,1]{3,2,5,4,1,6,0:T(8,128)S(1)}, f32[1,3,8,8,4,4,1]{3,2,5,4,1,6,0:T(8,128)S(1)}, u32[]{:S(2)}, u32[]{:S(2)}) collective-permute-start(f32[1,3,8,8,4,4,1]{3,2,5,4,1,6,0:T(8,128)S(1)} %bitcast.643), channel_id=1, source_target_pairs={{1,0},{2,1},{3,2},{4,3},{5,4},{6,5},{7,6},{8,7},{9,8},{10,9},{11,1... | collective-permute-start | bytes 36872 | tf_op jit(solution)/shard_map/ppermute | solution.py:39
  193.7 6.7 %collective-permute-start.24 = (f32[1,2,8,8,1,4,1]{2,5,3,1,6,4,0:T(4,128)S(1)}, f32[1,2,8,8,1,4,1]{2,5,3,1,6,4,0:T(4,128)S(1)}, u32[]{:S(2)}, u32[]{:S(2)}) collective-permute-start(f32[1,2,8,8,1,4,1]{2,5,3,1,6,4,0:T(4,128)S(1)} %get-tuple-element.57), channel_id=1, source_target_pairs={{0,256},{256,512},{512,768},{1,257},{257,513},{513,769},{2,258},{2... | collective-permute-start | bytes 6152 | tf_op jit(solution)/shard_map/ppermute | solution.py:37
  213.1 6.9 %collective-permute-start.28 = (f32[1,2,8,8,4,4,1]{3,2,5,4,1,6,0:T(8,128)S(1)}, f32[1,2,8,8,4,4,1]{3,2,5,4,1,6,0:T(8,128)S(1)}, u32[]{:S(2)}, u32[]{:S(2)}) collective-permute-start(f32[1,2,8,8,4,4,1]{3,2,5,4,1,6,0:T(8,128)S(1)} %bitcast.669), channel_id=1, source_target_pairs={{0,1},{1,2},{2,3},{3,4},{4,5},{5,6},{6,7},{7,8},{8,9},{9,10},{10,1... | collective-permute-start | bytes 24584 | tf_op jit(solution)/shard_map/ppermute | solution.py:37
  217.2 7.8 %collective-permute-start.29 = (f32[1,2,8,8,4,4,1]{3,2,5,4,1,6,0:T(8,128)S(1)}, f32[1,2,8,8,4,4,1]{3,2,5,4,1,6,0:T(8,128)S(1)}, u32[]{:S(2)}, u32[]{:S(2)}) collective-permute-start(f32[1,2,8,8,4,4,1]{3,2,5,4,1,6,0:T(8,128)S(1)} %bitcast.671), channel_id=1, source_target_pairs={{1,0},{2,1},{3,2},{4,3},{5,4},{6,5},{7,6},{8,7},{9,8},{10,9},{11,1... | collective-permute-start | bytes 24584 | tf_op jit(solution)/shard_map/ppermute | solution.py:39
  232.8 6.5 %collective-permute-start.30 = (f32[1,1,8,8,1,4,1]{2,5,3,6,4,1,0:T(4,128)S(1)}, f32[1,1,8,8,1,4,1]{2,5,3,6,4,1,0:T(4,128)S(1)}, u32[]{:S(2)}, u32[]{:S(2)}) collective-permute-start(f32[1,1,8,8,1,4,1]{2,5,3,6,4,1,0:T(4,128)S(1)} %get-tuple-element.106), channel_id=1, source_target_pairs={{0,256},{256,512},{512,768},{1,257},{257,513},{513,769},{2,258},{2... | collective-permute-start | bytes 3080 | tf_op jit(solution)/shard_map/ppermute | solution.py:37
  255.5 7.1 %collective-permute-start.35 = (f32[1,1,8,8,4,4,1]{3,2,5,4,6,1,0:T(8,128)S(1)}, f32[1,1,8,8,4,4,1]{3,2,5,4,6,1,0:T(8,128)S(1)}, u32[]{:S(2)}, u32[]{:S(2)}) collective-permute-start(f32[1,1,8,8,4,4,1]{3,2,5,4,6,1,0:T(8,128)S(1)} %bitcast.686), channel_id=1, source_target_pairs={{1,0},{2,1},{3,2},{4,3},{5,4},{6,5},{7,6},{8,7},{9,8},{10,9},{11,1... | collective-permute-start | bytes 12296 | tf_op jit(solution)/shard_map/ppermute | solution.py:39
  269.1 6.5 %collective-permute-start.36 = (f32[1,1,8,8,1,4,1]{2,5,3,6,4,1,0:T(4,128)S(1)}, f32[1,1,8,8,1,4,1]{2,5,3,6,4,1,0:T(4,128)S(1)}, u32[]{:S(2)}, u32[]{:S(2)}) collective-permute-start(f32[1,1,8,8,1,4,1]{2,5,3,6,4,1,0:T(4,128)S(1)} %get-tuple-element.100), channel_id=1, source_target_pairs={{0,256},{256,512},{512,768},{1,257},{257,513},{513,769},{2,258},{2... | collective-permute-start | bytes 3080 | tf_op jit(solution)/shard_map/ppermute | solution.py:37
  287.7 6.3 %collective-permute-start.40 = (f32[1,1,8,8,4,4,1]{3,2,5,4,6,1,0:T(8,128)S(1)}, f32[1,1,8,8,4,4,1]{3,2,5,4,6,1,0:T(8,128)S(1)}, u32[]{:S(2)}, u32[]{:S(2)}) collective-permute-start(f32[1,1,8,8,4,4,1]{3,2,5,4,6,1,0:T(8,128)S(1)} %bitcast.680), channel_id=1, source_target_pairs={{0,1},{1,2},{2,3},{3,4},{4,5},{5,6},{6,7},{7,8},{8,9},{9,10},{10,1... | collective-permute-start | bytes 12296 | tf_op jit(solution)/shard_map/ppermute | solution.py:37
  291.7 7.1 %collective-permute-start.41 = (f32[1,1,8,8,4,4,1]{3,2,5,4,6,1,0:T(8,128)S(1)}, f32[1,1,8,8,4,4,1]{3,2,5,4,6,1,0:T(8,128)S(1)}, u32[]{:S(2)}, u32[]{:S(2)}) collective-permute-start(f32[1,1,8,8,4,4,1]{3,2,5,4,6,1,0:T(8,128)S(1)} %bitcast.682), channel_id=1, source_target_pairs={{1,0},{2,1},{3,2},{4,3},{5,4},{6,5},{7,6},{8,7},{9,8},{10,9},{11,1... | collective-permute-start | bytes 12296 | tf_op jit(solution)/shard_map/ppermute | solution.py:39
  304.5 50.7 %all-to-all-start = ((f32[64,1,128]{2,1,0:T(1,128)}), f32[64,1,128]{2,1,0:T(1,128)S(1)}, u32[]{:S(2)}, u32[]{:S(2)}) async-start(f32[64,1,128]{2,1,0:T(1,128)} %broadcast_in_dim.69), calls=%async_computation | async-start | bytes 65536 | tf_op jit(solution)/shard_map/all_to_all | solution.py:50
  355.8 12.8 %all-to-all-start.1 = ((f32[16,1,128]{2,1,0:T(1,128)}), f32[16,1,128]{2,1,0:T(1,128)S(1)}, u32[]{:S(2)}, u32[]{:S(2)}) async-start(f32[16,1,128]{2,1,0:T(1,128)} %broadcast_in_dim.70), calls=%async_computation.1 | async-start | bytes 16384 | tf_op jit(solution)/shard_map/all_to_all | solution.py:50
  (48 other events, 279.3 us)

commit v2 on v1

v2 whole, which is shorter than its diff:
```python
import jax
import jax.numpy as jnp
from jax import lax
from jax.experimental import pallas as pl
from jax.experimental.pallas import tpu as pltpu
from jax.sharding import Mesh
from jax.sharding import PartitionSpec as P

GX = ("gx_0", "gx_1")
GZ = ("gz_0", "gz_1")
GX_GY = ("gx_0", "gx_1", "gy")
GX_GY_GZ = ("gx_0", "gx_1", "gy", "gz_0", "gz_1")
F32 = jnp.float32
PTS = 512
LANES = 128

time_step = 0.03
mass_shift = 4.0
inner_nodes = (
    -0.8717401485096066,
    -0.5917001814331423,
    -0.2092992179024789,
    0.2092992179024789,
    0.5917001814331423,
    0.8717401485096066,
)


def legendre_seven(position):
    previous = 1.0
    current_value = position
    for degree_index in range(1, 7):
        following = (
            (2 * degree_index + 1) * position * current_value - degree_index * previous
        ) / (degree_index + 1)
        previous = current_value
        current_value = following
    return current_value


def tables():
    nodes = [-1.0] + list(inner_nodes) + [1.0]
    poly = [legendre_seven(node) for node in nodes]
    weights = [2.0 / (56.0 * value * value) for value in poly]
    deriv = [[0.0] * 8 for _ in range(8)]
    for i in range(8):
        for j in range(8):
            if i != j:
                deriv[i][j] = poly[i] / (poly[j] * (nodes[i] - nodes[j]))
    deriv[0][0] = -14.0
    deriv[7][7] = 14.0
    return weights, deriv


WEIGHTS, DERIV = tables()
DERIV_T = [[DERIV[j][i] for j in range(8)] for i in range(8)]
SQUARE = [[DERIV[j][i] ** 2 for j in range(8)] for i in range(8)]
MINUS = [[-DERIV[i][j] for j in range(8)] for i in range(8)]


def mix(matrix, values, which=range(8)):
    out = []
    for i in which:
        total_value = None
        for j in range(8):
            if matrix[i][j] != 0.0:
                term = matrix[i][j] * values[j]
                total_value = term if total_value is None else total_value + term
        out.append(total_value)
    return out


def columns(matrix):
    sub = lax.broadcasted_iota(jnp.int32, (8, LANES), 0)
    out = []
    for j in range(8):
        col = jnp.zeros((8, LANES), F32)
        for i in range(8):
            col = jnp.where(sub == i, F32(matrix[i][j]), col)
        out.append(col)
    return out


def weight_column():
    sub = lax.broadcasted_iota(jnp.int32, (8, LANES), 0)
    col = jnp.zeros((8, LANES), F32)
    for i in range(8):
        col = jnp.where(sub == i, F32(WEIGHTS[i]), col)
    return col


def rows8(start):
    return pl.ds(pl.multiple_of(start, 8), 8)


def mix_inner(cols, ref, lead, start):
    total_value = None
    for j in range(8):
        term = cols[j] * ref[lead + (pl.ds(start + j, 8, stride=0), slice(None))]
        total_value = term if total_value is None else total_value + term
    return total_value


def place_of(tile):
    lane = lax.broadcasted_iota(jnp.int32, (1, LANES), 1)
    block = lane >> 4
    if tile == 0:
        row = block + 2
    else:
        row = jnp.where(block == 0, 1, jnp.where(block == 1, 10, jnp.where(block == 2, 0, 11)))
    return lane, block, lane & 15, row + 4 * (lax.axis_index("gy") - 1)


def pair_weights(has_low, has_high, average):
    own, other = (0.5, 0.5) if average else (1.0, 1.0)
    return (
        jnp.where(has_low, F32(own), F32(1.0)),
        jnp.where(has_low, F32(other), F32(0.0)),
        jnp.where(has_high, F32(own), F32(1.0)),
        jnp.where(has_high, F32(other), F32(0.0)),
    )


def x_weights(average):
    _, _, ix, _ = place_of(0)
    return pair_weights(ix > 0, ix < 15, average)


def y_weights(tile, average):
    _, _, _, y = place_of(tile)
    return pair_weights(y > 0, y < 4 * lax.axis_size("gy") - 1, average)


def z_index():
    return lax.axis_index("gz_0") * lax.axis_size("gz_1") + lax.axis_index("gz_1")


def z_weights():
    z = jnp.full((1, LANES), z_index(), jnp.int32)
    return pair_weights(z > 0, z < lax.axis_size("gz_0") * lax.axis_size("gz_1") - 1, True)


def roll(x, shift):
    return pltpu.roll(x, shift % LANES, 1)


def x_join(ref, lead, w):
    low, high = lead + (slice(0, 64),), lead + (slice(448, 512),)
    f0, f7 = ref[low], ref[high]
    ref[low] = w[0] * f0 + w[1] * roll(f7, 1)
    ref[high] = w[2] * f7 + w[3] * roll(f0, -1)


def y_join(ref, lead, w):
    for a in range(8):
        low, high = lead + (slice(64 * a, 64 * a + 8),), lead + (slice(64 * a + 56, 64 * a + 64),)
        f0, f7 = ref[low], ref[high]
        ref[low] = w[0] * f0 + w[1] * roll(f7, 16)
        ref[high] = w[2] * f7 + w[3] * roll(f0, -16)


def y_join_two(ref, far, lead, w, far_w):
    lane, block, _, _ = place_of(0)
    for a in range(8):
        low, high = lead + (slice(64 * a, 64 * a + 8),), lead + (slice(64 * a + 56, 64 * a + 64),)
        f0, f7, g0, g7 = ref[low], ref[high], far[low], far[high]
        below = jnp.where(block == 0, g7, roll(f7, 16))
        above = jnp.where(block == 7, roll(g0, -32), roll(f0, -16))
        ref[low] = w[0] * f0 + w[1] * below
        ref[high] = w[2] * f7 + w[3] * above
        if far_w is not None:
            below = jnp.where(block == 0, roll(g7, -32), roll(f7, 32))
            above = jnp.where(block == 0, f0, roll(g0, -32))
            far[low] = far_w[0] * g0 + far_w[1] * below
            far[high] = far_w[2] * g7 + far_w[3] * above


def face(ref, lead, c):
    return ref[lead + (pl.ds(c, 64, stride=8), slice(None))]


def set_face(ref, lead, c, value):
    ref[lead + (pl.ds(c, 64, stride=8), slice(None))] = value


def convect(i, v, vel, out, minus_cols):
    def along_a(b, carry):
        start = 8 * b
        got = mix(MINUS, [v[i, rows8(64 * a + start)] for a in range(8)])
        for a in range(8):
            at = rows8(64 * a + start)
            out[i, at] = vel[0, at] * got[a]
        return carry

    lax.fori_loop(0, 8, along_a, 0)

    def along_bc(a, carry):
        start = 64 * a
        got = mix(MINUS, [v[i, rows8(start + 8 * b)] for b in range(8)])
        for b in range(8):
            at = rows8(start + 8 * b)
            inner = mix_inner(minus_cols, v, (i,), start + 8 * b)
            out[i, at] = out[i, at] + (vel[1, at] * got[b] + vel[2, at] * inner)
        return carry

    lax.fori_loop(0, 8, along_bc, 0)


def convect_y_faces(i, v, vel, out, minus_cols):
    for b in (0, 7):
        got = mix(MINUS, [v[i, slice(64 * a + 8 * b, 64 * a + 8 * b + 8)] for a in range(8)])
        for a in range(8):
            at = slice(64 * a + 8 * b, 64 * a + 8 * b + 8)
            out[i, at] = vel[0, at] * got[a]

    def along_bc(a, carry):
        start = 64 * a
        got = mix(MINUS, [v[i, rows8(start + 8 * b)] for b in range(8)], (0, 7))
        for b, value in zip((0, 7), got):
            at = rows8(start + 8 * b)
            inner = mix_inner(minus_cols, v, (i,), start + 8 * b)
            out[i, at] = out[i, at] + (vel[1, at] * value + vel[2, at] * inner)
        return carry

    lax.fori_loop(0, 8, along_bc, 0)


def pack_kernel(place, vel, inv, out):
    def move(s, carry):
        q = place[s]
        r = (q % 4) * 4 + q // 4
        for i in range(3):
            out[i, pl.ds(r, 1), :] = vel[i, pl.ds(s, 1), :]
        out[3, pl.ds(r, 1), :] = inv[pl.ds(s, 1), :]
        return carry

    lax.fori_loop(0, 16, move, 0)


FAR_ROWS = (1, 10, 0, 11)


def unpack(got, i, near, far, scratch, lead):
    for r in range(12):
        base = 16 * (r - 2) if 2 <= r <= 9 else LANES + 16 * FAR_ROWS.index(r)
        for g in range(4):
            first = 4 * (r % 4)
            scratch[slice(base + 4 * g, base + 4 * g + 4), :] = got[
                g, r // 4, i, slice(first, first + 4), :
            ]
    for p in range(4):
        at = slice(128 * p, 128 * p + 128)
        near[lead + (at,)] = jnp.transpose(scratch[0:128, at])
        far[lead + (at,)] = jnp.transpose(scratch[128:256, at])


def first_kernel(got, vel, vel_far, rate, rate_far, up, down, inv, inv_far, scratch):
    scratch[192:256, :] = jnp.zeros((64, PTS), F32)
    for i in range(3):
        unpack(got, i, vel, vel_far, scratch, (i,))
    unpack(got, 3, inv, inv_far, scratch, ())
    minus_cols = columns(MINUS)
    xw = x_weights(True)
    yw = y_weights(0, True)
    fw = y_weights(1, True)

    def component(i, carry):
        convect(i, vel, vel, rate, minus_cols)
        convect(i, vel_far, vel_far, rate_far, minus_cols)
        x_join(rate, (i,), xw)
        x_join(rate_far, (i,), xw)
        y_join_two(rate, rate_far, (i,), yw, fw)
        return carry

    lax.fori_loop(0, 3, component, 0)
    lane, _, _, _ = place_of(0)
    for c, out in ((7, up), (0, down)):
        for i in range(3):
            out[slice(64 * i, 64 * i + 64), :] = face(rate, (i,), c)
        far = [face(rate_far, (i,), c) for i in range(3)]
        out[192:256, :] = jnp.where(
            lane < 32, far[0], jnp.where(lane < 64, roll(far[1], 32), roll(far[2], 64))
        )


def advance(vel, rate, below, above, acc_in, scale, acc_scale, v, acc):
    zw = z_weights()

    def step(k, carry):
        at = rows8(8 * k)
        for i in range(3):
            r = rate[i, at]
            v[i, at] = vel[i, at] + scale * r
            if acc is not None:
                acc[i, at] = acc_in[i, at] + acc_scale * r
        return carry

    lax.fori_loop(0, 64, step, 0, unroll=2)
    for i in range(3):
        for c, got, own, other in ((0, below, zw[0], zw[1]), (7, above, zw[2], zw[3])):
            k = own * face(rate, (i,), c) + other * got[i]
            set_face(v, (i,), c, face(vel, (i,), c) + scale * k)
            if acc is not None:
                set_face(acc, (i,), c, face(acc_in, (i,), c) + acc_scale * k)


def thirds(ref):
    return [ref[slice(64 * i, 64 * i + 64), :] for i in range(3)]


def second_kernel(
    vel, vel_far, rate, rate_far, below, above, acc, out, up, down, v, v_far, out_far
):
    advance(
        vel, rate, thirds(below), thirds(above), vel, 0.5 * time_step, time_step / 6.0, v, acc
    )
    far = [[roll(ref[192:256, :], -32 * i) for i in range(3)] for ref in (below, above)]
    advance(vel_far, rate_far, far[0], far[1], None, 0.5 * time_step, 0.0, v_far, None)
    minus_cols = columns(MINUS)
    xw = x_weights(True)
    yw = y_weights(0, True)

    def component(i, carry):
        convect(i, v, vel, out, minus_cols)
        convect_y_faces(i, v_far, vel_far, out_far, minus_cols)
        x_join(out, (i,), xw)
        x_join_faces(out_far, i, xw)
        y_join_two(out, out_far, (i,), yw, None)
        return carry

    lax.fori_loop(0, 3, component, 0)
    send_faces(out, up, down)


def x_join_faces(ref, i, w):
    for b in (0, 7):
        low, high = slice(8 * b, 8 * b + 8), slice(448 + 8 * b, 448 + 8 * b + 8)
        f0, f7 = ref[i, low], ref[i, high]
        ref[i, low] = w[0] * f0 + w[1] * roll(f7, 1)
        ref[i, high] = w[2] * f7 + w[3] * roll(f0, -1)


def send_faces(rate, up, down):
    for i in range(3):
        up[slice(64 * i, 64 * i + 64), :] = face(rate, (i,), 7)
        down[slice(64 * i, 64 * i + 64), :] = face(rate, (i,), 0)


def stage_kernel(scale, acc_scale):
    def kernel(vel, acc_in, rate, below, above, acc, out, up, down, v):
        advance(vel, rate, thirds(below), thirds(above), acc_in, scale, acc_scale, v, acc)
        minus_cols = columns(MINUS)
        xw = x_weights(True)
        yw = y_weights(0, True)

        def component(i, carry):
            convect(i, v, vel, out, minus_cols)
            x_join(out, (i,), xw)
            y_join(out, (i,), yw)
            return carry

        lax.fori_loop(0, 3, component, 0)
        send_faces(out, up, down)

    return kernel


def own_rows():
    _, block, _, _ = place_of(0)
    return block


def source_kernel(acc_in, rate, below, above, advected, source, up, down, joined):
    advance(acc_in, rate, thirds(below), thirds(above), None, time_step / 6.0, 0.0, advected, None)
    cols = columns(DERIV)
    wc = weight_column()

    def along_a(b, carry):
        start = 8 * b
        got = mix(DERIV, [advected[0, rows8(64 * a + start)] for a in range(8)])
        for a in range(8):
            source[rows8(64 * a + start)] = got[a]
        return carry

    lax.fori_loop(0, 8, along_a, 0)
    for a in range(8):
        start = 64 * a
        got = mix(DERIV, [advected[1, slice(start + 8 * b, start + 8 * b + 8)] for b in range(8)])
        for b in range(8):
            at = slice(start + 8 * b, start + 8 * b + 8)
            inner = mix_inner(cols, advected, (2,), start + 8 * b)
            scale = -WEIGHTS[a] * WEIGHTS[b] / time_step
            source[at] = (source[at] + got[b] + inner) * (scale * wc)
    joined[...] = source[...]
    block = own_rows()
    take_low = jnp.where((block >= 3) & (block <= 5), F32(1.0), F32(0.0))
    take_high = jnp.where((block >= 2) & (block <= 4), F32(1.0), F32(0.0))
    y_join(joined, (), (1.0, take_low, 1.0, take_high))
    lane, _, _, _ = place_of(0)
    for out, first in ((down, 1), (up, 2)):
        total_value = None
        for q in range(4):
            part = roll(joined[slice(128 * q, 128 * q + 128), :], 32 * (q - first))
            total_value = part if q == 0 else jnp.where(lane >> 5 == q, part, total_value)
        out[...] = total_value


def spread_kernel(joined, below, above, full, up, down):
    lane, block, _, _ = place_of(0)
    for q in range(4):
        at = slice(128 * q, 128 * q + 128)
        full[at, :] = jnp.where(
            lane < 32,
            roll(below[...], -32 * q),
            jnp.where(lane >= 96, roll(above[...], 96 - 32 * q), joined[at, :]),
        )
    take_low = jnp.where((block == 2) | (block == 6), F32(1.0), F32(0.0))
    take_high = jnp.where((block == 1) | (block == 5), F32(1.0), F32(0.0))
    y_join(full, (), (1.0, take_low, 1.0, take_high))
    x_join(full, (), x_weights(False))
    up[...] = face(full, (), 7)
    down[...] = face(full, (), 0)


def diagonal_kernel(inv, inv_far, weighted, diag, up, down, weighted_far, diag_far):
    wc = weight_column()
    cols = columns(SQUARE)
    for a in range(8):
        for b in range(8):
            at = slice(64 * a + 8 * b, 64 * a + 8 * b + 8)
            scale = WEIGHTS[a] * WEIGHTS[b] * wc
            weighted[at] = scale * inv[at]
            weighted_far[at] = scale * inv_far[at]
    for src, out, bs in ((weighted, diag, range(8)), (weighted_far, diag_far, (0, 7))):
        for b in bs:
            got = mix(SQUARE, [src[slice(64 * a + 8 * b, 64 * a + 8 * b + 8)] for a in range(8)])
            for a in range(8):
                out[slice(64 * a + 8 * b, 64 * a + 8 * b + 8)] = got[a]
        for a in range(8):
            start = 64 * a
            got = mix(SQUARE, [src[slice(start + 8 * b, start + 8 * b + 8)] for b in range(8)], bs)
            for b, value in zip(bs, got):
                at = slice(start + 8 * b, start + 8 * b + 8)
                inner = mix_inner(cols, src, (), start + 8 * b)
                scale = mass_shift * WEIGHTS[a] * WEIGHTS[b]
                out[at] = out[at] + value + inner + scale * wc
    xw = x_weights(False)
    x_join(diag, (), xw)
    for b in (0, 7):
        low, high = slice(8 * b, 8 * b + 8), slice(448 + 8 * b, 448 + 8 * b + 8)
        f0, f7 = diag_far[low], diag_far[high]
        diag_far[low] = xw[0] * f0 + xw[1] * roll(f7, 1)
        diag_far[high] = xw[2] * f7 + xw[3] * roll(f0, -1)
    y_join_two(diag, diag_far, (), y_weights(0, False), None)
    up[...] = face(diag, (), 7)
    down[...] = face(diag, (), 0)


def z_sum(src, below, above, dst):
    dst[...] = src[...]
    set_face(dst, (), 0, face(src, (), 0) + below)
    set_face(dst, (), 7, face(src, (), 7) + above)


def operate(u, weighted, out, flux):
    cols = columns(DERIV)
    cols_t = columns(DERIV_T)
    _, _, _, y = place_of(0)
    inside = (y >= 0) & (y < 4 * lax.axis_size("gy"))
    wc = jnp.where(inside, weight_column(), F32(0.0))

    def along_a(b, carry):
        start = 8 * b
        at = [rows8(64 * a + start) for a in range(8)]
        slope = mix(DERIV, [u[at[a]] for a in range(8)])
        got = mix(DERIV_T, [weighted[at[a]] * slope[a] for a in range(8)])
        for a in range(8):
            out[at[a]] = got[a]
        return carry

    lax.fori_loop(0, 8, along_a, 0)

    for a in range(8):
        start = 64 * a
        at = [slice(start + 8 * b, start + 8 * b + 8) for b in range(8)]
        values = [u[at[b]] for b in range(8)]
        weights = [weighted[at[b]] for b in range(8)]
        slope = mix(DERIV, values)
        got = mix(DERIV_T, [weights[b] * slope[b] for b in range(8)])
        for b in range(8):
            flux[at[b]] = weights[b] * mix_inner(cols, u, (), start + 8 * b)
            scale = mass_shift * WEIGHTS[a] * WEIGHTS[b]
            out[at[b]] = out[at[b]] + (got[b] + (scale * wc) * values[b])

    def along_c(k, carry):
        at = rows8(8 * k)
        out[at] = out[at] + mix_inner(cols_t, flux, (), 8 * k)
        return carry

    lax.fori_loop(0, 64, along_c, 0, unroll=4)


def own_mask():
    _, block, ix, _ = place_of(0)
    gx = lax.axis_index("gx_0") * lax.axis_size("gx_1") + lax.axis_index("gx_1")
    return jnp.where((block >= 2) & (block <= 5) & ((ix >> 2) == gx), F32(1.0), F32(0.0))


def dot(left, right):
    def step(k, carry):
        at = rows8(8 * k)
        return carry + left[at] * right[at]

    return lax.fori_loop(0, 64, step, jnp.zeros((8, LANES), F32), unroll=8)


def operator_one_kernel(
    partial, below, above, diag, diag_below, diag_above, source, weighted,
    residual, inverse, first, local, out, up, down, sums, flux,
):
    z_sum(partial, below[...], above[...], residual)
    z_sum(diag, diag_below[...], diag_above[...], inverse)
    inverse[...] = 1.0 / inverse[...]
    first[...] = residual[...] * inverse[...]
    operate(first, weighted, local, flux)
    out[...] = local[...]
    x_join(out, (), x_weights(False))
    y_join(out, (), y_weights(0, False))
    up[...] = face(out, (), 7)
    down[...] = face(out, (), 0)
    sums[0] = dot(source, first)
    sums[1] = dot(local, first)


def operator_two_kernel(
    partial, below, above, inverse, weighted, local, sums,
    applied, second, out, up, down, totals, local_two, flux,
):
    z_sum(partial, below[...], above[...], applied)
    second[...] = applied[...] * inverse[...]
    operate(second, weighted, local_two, flux)
    mask = own_mask()
    lane = lax.broadcasted_iota(jnp.int32, (1, LANES), 1)
    row = jnp.zeros((1, LANES), F32)
    for k, value in enumerate((sums[0], sums[1], dot(local, second), dot(local_two, second))):
        part = jnp.sum(mask * value, axis=0, keepdims=True)
        part = jnp.sum(part, axis=1, keepdims=True)
        row = jnp.where(lane == k, part, row)
    totals[...] = row
    out[...] = local_two[...]
    x_join(out, (), x_weights(False))
    y_join(out, (), y_weights(0, False))
    up[...] = face(out, (), 7)
    down[...] = face(out, (), 0)


def to_slots(place, ref, lead, out, k, scratch):
    for p in range(4):
        at = slice(128 * p, 128 * p + 128)
        scratch[:, at] = jnp.transpose(ref[lead + (at,)])
    gx = lax.axis_index("gx_0") * lax.axis_size("gx_1") + lax.axis_index("gx_1")
    for s in range(16):
        q = place[s]
        lane = (2 + q % 4) * 16 + 4 * gx + q // 4
        out[k, slice(s, s + 1), :] = scratch[pl.ds(lane, 1), :]


def advected_kernel(place, advected, out, scratch):
    for i in range(3):
        to_slots(place, advected, (i,), out, i, scratch)


def fields_kernel(place, residual, first, applied, second, out, scratch):
    for k, ref in enumerate((residual, first, applied, second)):
        to_slots(place, ref, (), out, k, scratch)


def last_kernel(place, partial, below, above, out, full, scratch):
    z_sum(partial, below[...], above[...], full)
    to_slots(place, full, (), out, 0, scratch)


def call(kernel, outs, scratch=(), scalars=0):
    def run(*args):
        vm = pl.BlockSpec(memory_space=pltpu.VMEM)
        sm = pl.BlockSpec(memory_space=pltpu.SMEM)
        result = pl.pallas_call(
            kernel,
            out_shape=tuple(jax.ShapeDtypeStruct(shape, F32) for shape in outs),
            in_specs=[sm] * scalars + [vm] * (len(args) - scalars),
            out_specs=tuple(vm for _ in outs),
            scratch_shapes=[pltpu.VMEM(shape, F32) for shape in scratch],
        )(*args)
        return result

    return run


def shift(values, axis, step):
    count = lax.axis_size(axis)
    pairs = [(i, i + step) for i in range(count) if 0 <= i + step < count]
    return lax.ppermute(values, axis, pairs)


def along(axis, up, down):
    return shift(up, axis, 1), shift(down, axis, -1)


def total(row):
    for axes in (GX_GY, GZ):
        count = lax.axis_size(axes)
        pieces = lax.all_to_all(jnp.broadcast_to(row[None], (count, 1, 128)), axes, 0, 0)
        row = jnp.sum(pieces, axis=0)
    return row


FULL = (PTS, LANES)
THREE = (3, PTS, LANES)
FACE = (64, LANES)


def per_device(velocity, inv_density, element_place):
    by_slot = jnp.transpose(velocity, (0, 2, 1))
    inv_slot = jnp.transpose(inv_density)
    (block,) = call(pack_kernel, [(4, 16, PTS)], scalars=1)(element_place, by_slot, inv_slot)
    below, above = along("gy", block, block)
    got = lax.all_gather(jnp.stack([below, block, above]), GX)
    vel, vel_far, rate, rate_far, up, down, inv, inv_far = call(
        first_kernel,
        [THREE, THREE, THREE, THREE, (256, LANES), (256, LANES), FULL, FULL],
        [(256, PTS)],
    )(got)
    below, above = along(GZ, up, down)
    weighted, diag, diag_up, diag_down = call(
        diagonal_kernel, [FULL, FULL, FACE, FACE], [FULL, FULL]
    )(inv, inv_far)
    acc, rate, up, down = call(
        second_kernel, [THREE, THREE, (192, LANES), (192, LANES)], [THREE, THREE, THREE]
    )(vel, vel_far, rate, rate_far, below, above)
    for scale in (0.5 * time_step, time_step):
        below, above = along(GZ, up, down)
        acc, rate, up, down = call(
            stage_kernel(scale, time_step / 3.0),
            [THREE, THREE, (192, LANES), (192, LANES)],
            [THREE],
        )(vel, acc, rate, below, above)
    below, above = along(GZ, up, down)
    advected, source, up, down, joined = call(
        source_kernel, [THREE, FULL, (128, LANES), (128, LANES), FULL]
    )(acc, rate, below, above)
    below, above = along("gy", up, down)
    (advected_slots,) = call(advected_kernel, [(3, 16, PTS)], [(LANES, PTS)], 1)(
        element_place, advected
    )
    full, up, down = call(spread_kernel, [FULL, FACE, FACE])(joined, below, above)
    below, above = along(
        GZ, jnp.concatenate([up, diag_up]), jnp.concatenate([down, diag_down])
    )
    residual, inverse, first, local, partial, up, down, sums = call(
        operator_one_kernel, [FULL, FULL, FULL, FULL, FULL, FACE, FACE, (2, 8, LANES)], [FULL]
    )(full, below[:64], above[:64], diag, below[64:], above[64:], source, weighted)
    below, above = along(GZ, up, down)
    applied, second, partial, up, down, totals = call(
        operator_two_kernel, [FULL, FULL, FULL, FACE, FACE, (1, LANES)], [FULL, FULL]
    )(partial, below, above, inverse, weighted, local, sums)
    below, above = along(GZ, up, down)
    sums = total(totals)
    (fields,) = call(fields_kernel, [(4, 16, PTS)], [(LANES, PTS)], 1)(
        element_place, residual, first, applied, second
    )
    (last,) = call(last_kernel, [(1, 16, PTS)], [FULL, (LANES, PTS)], 1)(
        element_place, partial, below, above
    )
    rho, curvature, cross, tail = sums[0, 0], sums[0, 1], sums[0, 2], sums[0, 3]
    step = rho / curvature
    rho_next = step * step * cross - rho
    ratio = rho_next / rho
    step_next = rho_next / (
        curvature - 2.0 * step * cross + step * step * tail - ratio * ratio * curvature
    )
    keep = step + step_next * (1.0 + ratio)
    pressure = keep * fields[1] - step_next * step * fields[3]
    residual = fields[0] - keep * fields[2] + step_next * step * last[0]
    return (
        jnp.transpose(advected_slots, (0, 2, 1)),
        jnp.transpose(pressure),
        jnp.transpose(residual),
    )


def solution(mesh):
    torus = Mesh(
        mesh.devices.reshape(2, 2, mesh.shape["gy"], -1, 2),
        ("gx_0", "gx_1", "gy", "gz_0", "gz_1"),
    )
    placed = (P(None, None, GX_GY_GZ), P(None, GX_GY_GZ), P(GX_GY_GZ))
    return jax.shard_map(
        per_device,
        mesh=torus,
        in_specs=placed,
        out_specs=(P(None, None, GX_GY_GZ), P(None, GX_GY_GZ), P(None, GX_GY_GZ)),
        check_vma=False,
    )
```

time: 384 us -> 268 us (0.70)
  starting transfers between devices: 147 us -> 83.5 us
  waiting for transfers between devices: 142 us -> 89.7 us
  local copies, waits for them, and re-layouts: 59 us -> 7.55 us
  Pallas kernels: 0 us -> 47.4 us
  blocking collectives: 0 us -> 12.1 us
  between operations: 8.91 us -> 20.2 us
  other arithmetic: 13.6 us -> 4.73 us
  matrix products: 7.08 us -> 0 us
    ppermute x42 -> x18, waiting for transfers between devices: 118 us -> 31.4 us  [shift(): return lax.ppermute(values, axis, pairs)]
    ppermute x42 -> x18, starting transfers between devices: 111 us -> 53.5 us  [shift(): return lax.ppermute(values, axis, pairs)]
    all_gather x0 -> x1, waiting for transfers between devices: none -> 48.5 us  [per_device(): got = lax.all_gather(jnp.stack([below, block, above]), GX)]
    pallas_call x0 -> x13, Pallas kernels: none -> 47.4 us  [run(): pl.pallas_call(kernel, out_shape=tuple((jax.ShapeDtypeStruct(shape, F32)...]
    dynamic_update_slice x42 -> x0, local copies, waits for them, and re-layouts: 23.7 us -> none  [the longest x14 22.8 us: face_write(): return lax.dynamic_update_slice_in_dim(values, flat, node * elements, 3)]
    all_to_all x2 -> x1, waiting for transfers between devices: 24.5 us -> 9.77 us  [total(): lax.all_to_all(jnp.broadcast_to(row[None], (count, 1, 128)), axes, 0, 0)]
    all_to_all x0 -> x1, blocking collectives: none -> 12.1 us  [total(): lax.all_to_all(jnp.broadcast_to(row[None], (count, 1, 128)), axes, 0, 0)]
    slice x74 -> x3, local copies, waits for them, and re-layouts: 9.75 us -> 1.85 us  [the longest x1 0.63 us: per_device(): below[64:]]
  transfers between devices with their start and end apart: 44 -> 20, of which waited for: 43 -> 15; matrix products, arithmetic and copies ran while one was open for 3% -> 1% of each run, Pallas kernels for 0% -> 3%
where the time goes in v2:
time: 268 us; the launch traced here: 265 us
  waiting for transfers between devices  89.7 us (33%)
  starting transfers between devices  83.5 us (31%)
  Pallas kernels  47.4 us (18%)
  between operations  20.2 us (8%)
  blocking collectives  12.1 us (5%)
  local copies, waits for them, and re-layouts  7.55 us (3%)
  other arithmetic  4.73 us (2%)
    ppermute x18, starting transfers between devices, shift(): return lax.ppermute(values, axis, pairs)  53.5 us
    all_gather x1, waiting for transfers between devices, per_device(): got = lax.all_gather(jnp.stack([below, block, above]), GX)  48.5 us
    pallas_call x13, Pallas kernels, run(): pl.pallas_call(kernel, out_shape=tuple((jax.ShapeDtypeStruct(shape, F32)...  47.4 us
    ppermute x18, waiting for transfers between devices, shift(): return lax.ppermute(values, axis, pairs)  31.4 us
    all_to_all x1, starting transfers between devices, total(): lax.all_to_all(jnp.broadcast_to(row[None], (count, 1, 128)), axes, 0, 0)  30 us
    all_to_all x1, blocking collectives, total(): lax.all_to_all(jnp.broadcast_to(row[None], (count, 1, 128)), axes, 0, 0)  12.1 us
    all_to_all x1, waiting for transfers between devices, total(): lax.all_to_all(jnp.broadcast_to(row[None], (count, 1, 128)), axes, 0, 0)  9.77 us
  transfers between devices with their start and end apart: 20, of which 15 were waited for; matrix products, arithmetic and copies ran while one was open for 1% of the time, Pallas kernels for 3%

profile of v2, /device:TPU:6, one launch (start us, length us, event | category | flops | bytes accessed | tf_op | source)
XLA Modules:
  0.0 265.2 jit_solution(8415907967386385852)
XLA Ops:
  10.3 4.6 %collective-permute-start = (f32[4,16,512]{2,1,0:T(8,128)}, f32[4,16,512]{2,1,0:T(8,128)S(1)}, u32[]{:S(2)}, u32[]{:S(2)}) collective-permute-start(f32[4,16,512]{2,1,0:T(8,128)} %shard_map.58), channel_id=1, source_target_pairs={{0,64},{64,128},{128,192},{1,65},{65,129},{129,193},{2,66},{66,130... | collective-permute-start | bytes 393224 | tf_op jit(solution)/shard_map/ppermute | solution.py:602
  19.3 48.5 %all-gather.3.cloned.1.call-done = f32[12,4,16,512]{3,2,1,0:T(8,128)} async-done(((f32[3,4,16,512]{3,2,1,0:T(8,128)}), f32[12,4,16,512]{3,2,1,0:T(8,128)}) %all-gather.3.cloned.1.call-update) | async-done | bytes 1572880 | tf_op jit(solution)/shard_map/all_gather | solution.py:627
  67.8 7.8 %shard_map.59 = (f32[3,512,128]{2,1,0:T(8,128)}, f32[3,512,128]{2,1,0:T(8,128)}, f32[3,512,128]{2,1,0:T(8,128)}, f32[3,512,128]{2,1,0:T(8,128)}, f32[256,128]{1,...) custom-call(f32[4,3,4,16,512]{4,3,2,1,0:T(8,128)} %bitcast.23), custom_call_target="tpu_custom_call" | custom-call | tf_op jit(solution)/shard_map/pallas_call | solution.py:587
  78.5 3.0 %collective-permute-start.3 = (f32[256,128]{1,0:T(8,128)}, f32[256,128]{1,0:T(8,128)S(1)}, u32[]{:S(2)}, u32[]{:S(2)}) collective-permute-start(f32[256,128]{1,0:T(8,128)} %get-tuple-element.54), channel_id=1, source_target_pairs={{1,0},{2,1},{3,2},{4,3},{5,4},{6,5},{7,6},{8,7},{9,8},{10,9},{11,1... | collective-permute-start | bytes 393224 | tf_op jit(solution)/shard_map/ppermute | solution.py:602
  83.4 3.5 %collective-permute-done.3.above = f32[256,128]{1,0:T(8,128)S(1)} collective-permute-done((f32[256,128]{1,0:T(8,128)}, f32[256,128]{1,0:T(8,128)S(1)}, u32[]{:S(2)}, u32[]{:S(2)}) %collective-permute-start.3) | collective-permute-done | bytes 131104 | tf_op jit(solution)/shard_map/ppermute | solution.py:602
  87.5 6.4 %shard_map.60 = (f32[3,512,128]{2,1,0:T(8,128)}, f32[3,512,128]{2,1,0:T(8,128)}, f32[192,128]{1,0:T(8,128)}, f32[192,128]{1,0:T(8,128)}) custom-call(f32[3,512,128]{2,1,0:T(8,128)} %get-tuple-element.49.vel, f32[3,512,128]{2,1,0:T(8,128)} %get-tuple-element.50.vel_far, f32[3,512,128]{2,1,0:T(8,128)} %get-tuple-element.51.rate, ...), custom_call_target="tpu_custom_call" | custom-call | tf_op jit(solution)/shard_map/pallas_call | solution.py:587
  93.9 3.1 %collective-permute-start.4 = (f32[192,128]{1,0:T(8,128)}, f32[192,128]{1,0:T(8,128)S(1)}, u32[]{:S(2)}, u32[]{:S(2)}) collective-permute-start(f32[192,128]{1,0:T(8,128)} %get-tuple-element.57), channel_id=1, source_target_pairs={{0,1},{1,2},{2,3},{3,4},{4,5},{5,6},{6,7},{7,8},{8,9},{9,10},{10,1... | collective-permute-start | bytes 294920 | tf_op jit(solution)/shard_map/ppermute | solution.py:602
  100.6 4.0 %collective-permute-done.5.above = f32[192,128]{1,0:T(8,128)S(1)} collective-permute-done((f32[192,128]{1,0:T(8,128)}, f32[192,128]{1,0:T(8,128)S(1)}, u32[]{:S(2)}, u32[]{:S(2)}) %collective-permute-start.5) | collective-permute-done | bytes 98336 | tf_op jit(solution)/shard_map/ppermute | solution.py:602
  105.2 5.3 %shard_map.61 = (f32[3,512,128]{2,1,0:T(8,128)}, f32[3,512,128]{2,1,0:T(8,128)}, f32[192,128]{1,0:T(8,128)}, f32[192,128]{1,0:T(8,128)}) custom-call(f32[3,512,128]{2,1,0:T(8,128)} %get-tuple-element.49.vel, f32[3,512,128]{2,1,0:T(8,128)} %get-tuple-element.55.acc_in, f32[3,512,128]{2,1,0:T(8,128)} %get-tuple-element.56.rate, f32[192,128]{1,0:T(8,128)} %copy-done.3, ...), custom_call_target="tpu_custom_call" | custom-call | tf_op jit(solution)/shard_map/pallas_call | solution.py:587
  113.4 3.0 %collective-permute-start.7 = (f32[192,128]{1,0:T(8,128)}, f32[192,128]{1,0:T(8,128)S(1)}, u32[]{:S(2)}, u32[]{:S(2)}) collective-permute-start(f32[192,128]{1,0:T(8,128)} %get-tuple-element.62), channel_id=1, source_target_pairs={{1,0},{2,1},{3,2},{4,3},{5,4},{6,5},{7,6},{8,7},{9,8},{10,9},{11,1... | collective-permute-start | bytes 294920 | tf_op jit(solution)/shard_map/ppermute | solution.py:602
  121.6 5.3 %shard_map.62 = (f32[3,512,128]{2,1,0:T(8,128)}, f32[3,512,128]{2,1,0:T(8,128)}, f32[192,128]{1,0:T(8,128)}, f32[192,128]{1,0:T(8,128)}) custom-call(f32[3,512,128]{2,1,0:T(8,128)} %get-tuple-element.49.vel, f32[3,512,128]{2,1,0:T(8,128)} %get-tuple-element.59.acc_in, f32[3,512,128]{2,1,0:T(8,128)} %get-tuple-element.60.rate, f32[192,128]{1,0:T(8,128)} %copy-done.2, ...), custom_call_target="tpu_custom_call" | custom-call | tf_op jit(solution)/shard_map/pallas_call | solution.py:587
  126.9 3.1 %collective-permute-start.8 = (f32[192,128]{1,0:T(8,128)}, f32[192,128]{1,0:T(8,128)S(1)}, u32[]{:S(2)}, u32[]{:S(2)}) collective-permute-start(f32[192,128]{1,0:T(8,128)} %get-tuple-element.65), channel_id=1, source_target_pairs={{0,1},{1,2},{2,3},{3,4},{4,5},{5,6},{6,7},{7,8},{8,9},{9,10},{10,1... | collective-permute-start | bytes 294920 | tf_op jit(solution)/shard_map/ppermute | solution.py:602
  134.7 2.9 %collective-permute-done.9.above = f32[192,128]{1,0:T(8,128)S(1)} collective-permute-done((f32[192,128]{1,0:T(8,128)}, f32[192,128]{1,0:T(8,128)S(1)}, u32[]{:S(2)}, u32[]{:S(2)}) %collective-permute-start.9) | collective-permute-done | bytes 98336 | tf_op jit(solution)/shard_map/ppermute | solution.py:602
  138.2 3.0 %shard_map.63 = (f32[3,512,128]{2,1,0:T(8,128)}, f32[512,128]{1,0:T(8,128)}, f32[128,128]{1,0:T(8,128)}, f32[128,128]{1,0:T(8,128)}, f32[512,128]{1,0:T(8,128)}) custom-call(f32[3,512,128]{2,1,0:T(8,128)} %get-tuple-element.63.acc_in, f32[3,512,128]{2,1,0:T(8,128)} %get-tuple-element.64.rate, f32[192,128]{1,0:T(8,128)} %copy-done.6, f32[192,128]{1,0:T(8,128)} %copy-done.7), custom_call_target="tpu_custom_call" | custom-call | tf_op jit(solution)/shard_map/pallas_call | solution.py:587
  141.3 3.4 %collective-permute-start.10 = (f32[128,128]{1,0:T(8,128)}, f32[128,128]{1,0:T(8,128)S(1)}, u32[]{:S(2)}, u32[]{:S(2)}) collective-permute-start(f32[128,128]{1,0:T(8,128)} %get-tuple-element.69), channel_id=1, source_target_pairs={{0,64},{64,128},{128,192},{1,65},{65,129},{129,193},{2,66},{66,130... | collective-permute-start | bytes 196616 | tf_op jit(solution)/shard_map/ppermute | solution.py:602
  157.1 4.8 %collective-permute-start.12 = (f32[128,128]{1,0:T(8,128)S(1)}, f32[128,128]{1,0:T(8,128)S(1)}, u32[]{:S(2)}, u32[]{:S(2)}) collective-permute-start(f32[128,128]{1,0:T(8,128)S(1)} %pad_maximum_fusion.1), channel_id=1, source_target_pairs={{0,1},{1,2},{2,3},{3,4},{4,5},{5,6},{6,7},{7,8},{8,9},{9,10},{10,1... | collective-permute-start | bytes 196616 | tf_op jit(solution)/shard_map/ppermute | solution.py:602
  164.4 3.8 %shard_map.67 = (f32[512,128]{1,0:T(8,128)}, f32[512,128]{1,0:T(8,128)}, f32[512,128]{1,0:T(8,128)}, f32[512,128]{1,0:T(8,128)}, f32[512,128]{1,0:T(8,128)}, /*i...) custom-call(f32[512,128]{1,0:T(8,128)} %get-tuple-element.71.partial, ...), custom_call_target="tpu_custom_call" | custom-call | tf_op jit(solution)/shard_map/pallas_call | solution.py:587
  168.2 5.2 %collective-permute-start.14 = (f32[64,128]{1,0:T(8,128)}, f32[64,128]{1,0:T(8,128)S(1)}, u32[]{:S(2)}, u32[]{:S(2)}) collective-permute-start(f32[64,128]{1,0:T(8,128)} %get-tuple-element.82), channel_id=1, source_target_pairs={{0,1},{1,2},{2,3},{3,4},{4,5},{5,6},{6,7},{7,8},{8,9},{9,10},{10,1... | collective-permute-start | bytes 98312 | tf_op jit(solution)/shard_map/ppermute | solution.py:602
  175.3 5.0 %collective-permute-done.15.above = f32[64,128]{1,0:T(8,128)S(1)} collective-permute-done((f32[64,128]{1,0:T(8,128)}, f32[64,128]{1,0:T(8,128)S(1)}, u32[]{:S(2)}, u32[]{:S(2)}) %collective-permute-start.15) | collective-permute-done | bytes 32800 | tf_op jit(solution)/shard_map/ppermute | solution.py:602
  180.9 3.4 %shard_map.68 = (f32[512,128]{1,0:T(8,128)}, f32[512,128]{1,0:T(8,128)}, f32[512,128]{1,0:T(8,128)}, f32[64,128]{1,0:T(8,128)}, f32[64,128]{1,0:T(8,128)}, /*index=5*/f32[1,128]{1,0:T(1,128)}) custom-call(f32[512,128]{1,0:T(8,128)} %get-tuple-element.81.partial, f32[64,128]{1,0:T(8,128)} %copy-done.10, f32[64,128]{1,0:T(8,128)} %copy-done.11, ...), custom_call_target="tpu_custom_call" | custom-call | tf_op jit(solution)/shard_map/pallas_call | solution.py:587
  184.9 12.1 %all_to_all.10 = f32[16,1,128]{2,1,0:T(1,128)S(1)} all-to-all(f32[16,1,128]{2,1,0:T(1,128)S(1)} %broadcast_in_dim.7), channel_id=1, replica_groups=mesh['gx_0'=2,'gx_1'=2,'gy'=4,'gz_0'=32,'gz_1'=2] {'gx_0','gx_1','gy'}, dimensions={0} | all-to-all | bytes 16384 | tf_op jit(solution)/shard_map/all_to_all | solution.py:612
  197.6 30.0 %all-to-all-start.1 = ((f32[64,1,128]{2,1,0:T(1,128)}), f32[64,1,128]{2,1,0:T(1,128)S(1)}, u32[]{:S(2)}, u32[]{:S(2)}) async-start(f32[64,1,128]{2,1,0:T(1,128)} %broadcast_in_dim.16), calls=%async_computation.1 | async-start | bytes 65536 | tf_op jit(solution)/shard_map/all_to_all | solution.py:612
  227.7 3.4 %collective-permute-start.16 = (f32[64,128]{1,0:T(8,128)}, f32[64,128]{1,0:T(8,128)S(1)}, u32[]{:S(2)}, u32[]{:S(2)}) collective-permute-start(f32[64,128]{1,0:T(8,128)} %get-tuple-element.93), channel_id=1, source_target_pairs={{0,1},{1,2},{2,3},{3,4},{4,5},{5,6},{6,7},{7,8},{8,9},{9,10},{10,1... | collective-permute-start | bytes 98312 | tf_op jit(solution)/shard_map/ppermute | solution.py:602
  240.6 9.8 %all-to-all-done.1 = f32[64,1,128]{2,1,0:T(1,128)S(1)} async-done(((f32[64,1,128]{2,1,0:T(1,128)}), f32[64,1,128]{2,1,0:T(1,128)S(1)}, u32[]{:S(2)}, u32[]{:S(2)}) %all-to-all-start.1) | async-done | bytes 32800 | tf_op jit(solution)/shard_map/all_to_all | solution.py:612
  (70 shorter events, 60.9 us)
Async XLA Ops:
  7.2 60.7 %all-gather.3.cloned.1.call-start = ((), (), s32[]{:S(2)}) async-start(), calls=%async_computation.2 | async-start | bytes 1966080 | tf_op jit(solution)/shard_map/all_gather | solution.py:627
  9.0 7.3 %collective-permute-start.1 = (f32[4,16,512]{2,1,0:T(8,128)}, f32[4,16,512]{2,1,0:T(8,128)S(1)}, u32[]{:S(2)}, u32[]{:S(2)}) collective-permute-start(f32[4,16,512]{2,1,0:T(8,128)} %shard_map.58), channel_id=1, source_target_pairs={{64,0},{128,64},{192,128},{65,1},{129,65},{193,129},{66,2},{130,66... | collective-permute-start | bytes 393224 | tf_op jit(solution)/shard_map/ppermute | solution.py:602
  10.3 7.4 %collective-permute-start = (f32[4,16,512]{2,1,0:T(8,128)}, f32[4,16,512]{2,1,0:T(8,128)S(1)}, u32[]{:S(2)}, u32[]{:S(2)}) collective-permute-start(f32[4,16,512]{2,1,0:T(8,128)} %shard_map.58), channel_id=1, source_target_pairs={{0,64},{64,128},{128,192},{1,65},{65,129},{129,193},{2,66},{66,130... | collective-permute-start | bytes 393224 | tf_op jit(solution)/shard_map/ppermute | solution.py:602
  75.6 7.7 %collective-permute-start.2 = (f32[256,128]{1,0:T(8,128)}, f32[256,128]{1,0:T(8,128)S(1)}, u32[]{:S(2)}, u32[]{:S(2)}) collective-permute-start(f32[256,128]{1,0:T(8,128)} %get-tuple-element.53), channel_id=1, source_target_pairs={{0,1},{1,2},{2,3},{3,4},{4,5},{5,6},{6,7},{7,8},{8,9},{9,10},{10,1... | collective-permute-start | bytes 393224 | tf_op jit(solution)/shard_map/ppermute | solution.py:602
  78.5 8.4 %collective-permute-start.3 = (f32[256,128]{1,0:T(8,128)}, f32[256,128]{1,0:T(8,128)S(1)}, u32[]{:S(2)}, u32[]{:S(2)}) collective-permute-start(f32[256,128]{1,0:T(8,128)} %get-tuple-element.54), channel_id=1, source_target_pairs={{1,0},{2,1},{3,2},{4,3},{5,4},{6,5},{7,6},{8,7},{9,8},{10,9},{11,1... | collective-permute-start | bytes 393224 | tf_op jit(solution)/shard_map/ppermute | solution.py:602
  83.4 3.5 %copy-start = (f32[256,128]{1,0:T(8,128)}, f32[256,128]{1,0:T(8,128)S(1)}, u32[]{:S(2)}) copy-start(f32[256,128]{1,0:T(8,128)S(1)} %collective-permute-done.2.below) | copy-start | bytes 393220
  93.9 6.7 %collective-permute-start.4 = (f32[192,128]{1,0:T(8,128)}, f32[192,128]{1,0:T(8,128)S(1)}, u32[]{:S(2)}, u32[]{:S(2)}) collective-permute-start(f32[192,128]{1,0:T(8,128)} %get-tuple-element.57), channel_id=1, source_target_pairs={{0,1},{1,2},{2,3},{3,4},{4,5},{5,6},{6,7},{7,8},{8,9},{9,10},{10,1... | collective-permute-start | bytes 294920 | tf_op jit(solution)/shard_map/ppermute | solution.py:602
  97.0 7.6 %collective-permute-start.5 = (f32[192,128]{1,0:T(8,128)}, f32[192,128]{1,0:T(8,128)S(1)}, u32[]{:S(2)}, u32[]{:S(2)}) collective-permute-start(f32[192,128]{1,0:T(8,128)} %get-tuple-element.58), channel_id=1, source_target_pairs={{1,0},{2,1},{3,2},{4,3},{5,4},{6,5},{7,6},{8,7},{9,8},{10,9},{11,1... | collective-permute-start | bytes 294920 | tf_op jit(solution)/shard_map/ppermute | solution.py:602
  100.6 4.0 %copy-start.3 = (f32[192,128]{1,0:T(8,128)}, f32[192,128]{1,0:T(8,128)S(1)}, u32[]{:S(2)}) copy-start(f32[192,128]{1,0:T(8,128)S(1)} %collective-permute-done.4.below) | copy-start | bytes 294916
  110.5 7.8 %collective-permute-start.6 = (f32[192,128]{1,0:T(8,128)}, f32[192,128]{1,0:T(8,128)S(1)}, u32[]{:S(2)}, u32[]{:S(2)}) collective-permute-start(f32[192,128]{1,0:T(8,128)} %get-tuple-element.61), channel_id=1, source_target_pairs={{0,1},{1,2},{2,3},{3,4},{4,5},{5,6},{6,7},{7,8},{8,9},{9,10},{10,1... | collective-permute-start | bytes 294920 | tf_op jit(solution)/shard_map/ppermute | solution.py:602
  113.4 7.6 %collective-permute-start.7 = (f32[192,128]{1,0:T(8,128)}, f32[192,128]{1,0:T(8,128)S(1)}, u32[]{:S(2)}, u32[]{:S(2)}) collective-permute-start(f32[192,128]{1,0:T(8,128)} %get-tuple-element.62), channel_id=1, source_target_pairs={{1,0},{2,1},{3,2},{4,3},{5,4},{6,5},{7,6},{8,7},{9,8},{10,9},{11,1... | collective-permute-start | bytes 294920 | tf_op jit(solution)/shard_map/ppermute | solution.py:602
  126.9 7.8 %collective-permute-start.8 = (f32[192,128]{1,0:T(8,128)}, f32[192,128]{1,0:T(8,128)S(1)}, u32[]{:S(2)}, u32[]{:S(2)}) collective-permute-start(f32[192,128]{1,0:T(8,128)} %get-tuple-element.65), channel_id=1, source_target_pairs={{0,1},{1,2},{2,3},{3,4},{4,5},{5,6},{6,7},{7,8},{8,9},{9,10},{10,1... | collective-permute-start | bytes 294920 | tf_op jit(solution)/shard_map/ppermute | solution.py:602
  130.0 7.6 %collective-permute-start.9 = (f32[192,128]{1,0:T(8,128)}, f32[192,128]{1,0:T(8,128)S(1)}, u32[]{:S(2)}, u32[]{:S(2)}) collective-permute-start(f32[192,128]{1,0:T(8,128)} %get-tuple-element.66), channel_id=1, source_target_pairs={{1,0},{2,1},{3,2},{4,3},{5,4},{6,5},{7,6},{8,7},{9,8},{10,9},{11,1... | collective-permute-start | bytes 294920 | tf_op jit(solution)/shard_map/ppermute | solution.py:602
  134.7 2.9 %copy-start.6 = (f32[192,128]{1,0:T(8,128)}, f32[192,128]{1,0:T(8,128)S(1)}, u32[]{:S(2)}) copy-start(f32[192,128]{1,0:T(8,128)S(1)} %collective-permute-done.8.below) | copy-start | bytes 294916
  141.3 7.0 %collective-permute-start.10 = (f32[128,128]{1,0:T(8,128)}, f32[128,128]{1,0:T(8,128)S(1)}, u32[]{:S(2)}, u32[]{:S(2)}) collective-permute-start(f32[128,128]{1,0:T(8,128)} %get-tuple-element.69), channel_id=1, source_target_pairs={{0,64},{64,128},{128,192},{1,65},{65,129},{129,193},{2,66},{66,130... | collective-permute-start | bytes 196616 | tf_op jit(solution)/shard_map/ppermute | solution.py:602
  144.7 6.4 %collective-permute-start.11 = (f32[128,128]{1,0:T(8,128)}, f32[128,128]{1,0:T(8,128)S(1)}, u32[]{:S(2)}, u32[]{:S(2)}) collective-permute-start(f32[128,128]{1,0:T(8,128)} %get-tuple-element.70), channel_id=1, source_target_pairs={{64,0},{128,64},{192,128},{65,1},{129,65},{193,129},{66,2},{130,66... | collective-permute-start | bytes 196616 | tf_op jit(solution)/shard_map/ppermute | solution.py:602
  154.4 7.5 %collective-permute-start.13 = (f32[128,128]{1,0:T(8,128)S(1)}, f32[128,128]{1,0:T(8,128)S(1)}, u32[]{:S(2)}, u32[]{:S(2)}) collective-permute-start(f32[128,128]{1,0:T(8,128)S(1)} %pad_maximum_fusion.2), channel_id=1, source_target_pairs={{1,0},{2,1},{3,2},{4,3},{5,4},{6,5},{7,6},{8,7},{9,8},{10,9},{11,1... | collective-permute-start | bytes 196616 | tf_op jit(solution)/shard_map/ppermute | solution.py:602
  157.1 6.7 %collective-permute-start.12 = (f32[128,128]{1,0:T(8,128)S(1)}, f32[128,128]{1,0:T(8,128)S(1)}, u32[]{:S(2)}, u32[]{:S(2)}) collective-permute-start(f32[128,128]{1,0:T(8,128)S(1)} %pad_maximum_fusion.1), channel_id=1, source_target_pairs={{0,1},{1,2},{2,3},{3,4},{4,5},{5,6},{6,7},{7,8},{8,9},{9,10},{10,1... | collective-permute-start | bytes 196616 | tf_op jit(solution)/shard_map/ppermute | solution.py:602
  168.2 7.1 %collective-permute-start.14 = (f32[64,128]{1,0:T(8,128)}, f32[64,128]{1,0:T(8,128)S(1)}, u32[]{:S(2)}, u32[]{:S(2)}) collective-permute-start(f32[64,128]{1,0:T(8,128)} %get-tuple-element.82), channel_id=1, source_target_pairs={{0,1},{1,2},{2,3},{3,4},{4,5},{5,6},{6,7},{7,8},{8,9},{9,10},{10,1... | collective-permute-start | bytes 98312 | tf_op jit(solution)/shard_map/ppermute | solution.py:602
  173.3 6.9 %collective-permute-start.15 = (f32[64,128]{1,0:T(8,128)}, f32[64,128]{1,0:T(8,128)S(1)}, u32[]{:S(2)}, u32[]{:S(2)}) collective-permute-start(f32[64,128]{1,0:T(8,128)} %get-tuple-element.83), channel_id=1, source_target_pairs={{1,0},{2,1},{3,2},{4,3},{5,4},{6,5},{7,6},{8,7},{9,8},{10,9},{11,1... | collective-permute-start | bytes 98312 | tf_op jit(solution)/shard_map/ppermute | solution.py:602
  175.3 5.0 %copy-start.10 = (f32[64,128]{1,0:T(8,128)}, f32[64,128]{1,0:T(8,128)S(1)}, u32[]{:S(2)}) copy-start(f32[64,128]{1,0:T(8,128)S(1)} %collective-permute-done.14.below) | copy-start | bytes 98308
  197.6 52.7 %all-to-all-start.1 = ((f32[64,1,128]{2,1,0:T(1,128)}), f32[64,1,128]{2,1,0:T(1,128)S(1)}, u32[]{:S(2)}, u32[]{:S(2)}) async-start(f32[64,1,128]{2,1,0:T(1,128)} %broadcast_in_dim.16), calls=%async_computation.1 | async-start | bytes 65536 | tf_op jit(solution)/shard_map/all_to_all | solution.py:612
  227.7 10.5 %collective-permute-start.16 = (f32[64,128]{1,0:T(8,128)}, f32[64,128]{1,0:T(8,128)S(1)}, u32[]{:S(2)}, u32[]{:S(2)}) collective-permute-start(f32[64,128]{1,0:T(8,128)} %get-tuple-element.93), channel_id=1, source_target_pairs={{0,1},{1,2},{2,3},{3,4},{4,5},{5,6},{6,7},{7,8},{8,9},{9,10},{10,1... | collective-permute-start | bytes 98312 | tf_op jit(solution)/shard_map/ppermute | solution.py:602
  231.1 7.1 %collective-permute-start.17 = (f32[64,128]{1,0:T(8,128)}, f32[64,128]{1,0:T(8,128)S(1)}, u32[]{:S(2)}, u32[]{:S(2)}) collective-permute-start(f32[64,128]{1,0:T(8,128)} %get-tuple-element.94), channel_id=1, source_target_pairs={{1,0},{2,1},{3,2},{4,3},{5,4},{6,5},{7,6},{8,7},{9,8},{10,9},{11,1... | collective-permute-start | bytes 98312 | tf_op jit(solution)/shard_map/ppermute | solution.py:602
  (10 other events, 10.4 us)
Sparse Core Ops, SparseCore 0:
  19.5 48.3 all-gather.2

commit v3 on v2

--- a/solution.py
+++ b/solution.py
@@ -5,6 +5,7 @@
 from jax.experimental.pallas import tpu as pltpu
 from jax.sharding import Mesh
 from jax.sharding import PartitionSpec as P
+
 
 GX = ("gx_0", "gx_1")
 GZ = ("gz_0", "gz_1")
@@ -160,7 +161,7 @@
 
 
 def y_join_two(ref, far, lead, w, far_w):
-    lane, block, _, _ = place_of(0)
+    _, block, _, _ = place_of(0)
     for a in range(8):
         low, high = lead + (slice(64 * a, 64 * a + 8),), lead + (slice(64 * a + 56, 64 * a + 64),)
         f0, f7, g0, g7 = ref[low], ref[high], far[low], far[high]
@@ -225,40 +226,50 @@
     lax.fori_loop(0, 8, along_bc, 0)
 
 
-def pack_kernel(place, vel, inv, out):
+def pack_kernel(place, vel, inv, out, up, down):
     def move(s, carry):
         q = place[s]
         r = (q % 4) * 4 + q // 4
         for i in range(3):
-            out[i, pl.ds(r, 1), :] = vel[i, pl.ds(s, 1), :]
-        out[3, pl.ds(r, 1), :] = inv[pl.ds(s, 1), :]
+            out[pl.ds(16 * i + r, 1), :] = vel[i, pl.ds(s, 1), :]
+        out[pl.ds(48 + r, 1), :] = inv[pl.ds(s, 1), :]
         return carry
 
     lax.fori_loop(0, 16, move, 0)
+    for ref, first in ((up, 52), (down, 48)):
+        ref[0:48, :] = out[0:48, :]
+        ref[48:60, :] = out[slice(first, first + 12), :]
 
 
 FAR_ROWS = (1, 10, 0, 11)
 
 
-def unpack(got, i, near, far, scratch, lead):
+def unpack(middle, sides, i, near, far, scratch, lead):
     for r in range(12):
         base = 16 * (r - 2) if 2 <= r <= 9 else LANES + 16 * FAR_ROWS.index(r)
+        first = 16 * i + 4 * (r % 4)
+        if r < 4 and i == 3:
+            first -= 4
+        if r >= 8:
+            first += 60
         for g in range(4):
-            first = 4 * (r % 4)
-            scratch[slice(base + 4 * g, base + 4 * g + 4), :] = got[
-                g, r // 4, i, slice(first, first + 4), :
-            ]
+            at = slice(base + 4 * g, base + 4 * g + 4)
+            if i == 3 and r in (0, 11):
+                scratch[at, :] = jnp.zeros((4, PTS), F32)
+            else:
+                src = middle if 4 <= r < 8 else sides
+                scratch[at, :] = src[g, slice(first, first + 4), :]
     for p in range(4):
         at = slice(128 * p, 128 * p + 128)
         near[lead + (at,)] = jnp.transpose(scratch[0:128, at])
         far[lead + (at,)] = jnp.transpose(scratch[128:256, at])
 
 
-def first_kernel(got, vel, vel_far, rate, rate_far, up, down, inv, inv_far, scratch):
+def first_kernel(middle, sides, vel, vel_far, rate, rate_far, up, down, inv, inv_far, scratch):
     scratch[192:256, :] = jnp.zeros((64, PTS), F32)
     for i in range(3):
-        unpack(got, i, vel, vel_far, scratch, (i,))
-    unpack(got, 3, inv, inv_far, scratch, ())
+        unpack(middle, sides, i, vel, vel_far, scratch, (i,))
+    unpack(middle, sides, 3, inv, inv_far, scratch, ())
     minus_cols = columns(MINUS)
     xw = x_weights(True)
     yw = y_weights(0, True)
@@ -405,7 +416,7 @@
         out[...] = total_value
 
 
-def spread_kernel(joined, below, above, full, up, down):
+def spread_kernel(joined, below, above, diag_up, diag_down, full, up, down):
     lane, block, _, _ = place_of(0)
     for q in range(4):
         at = slice(128 * q, 128 * q + 128)
@@ -418,8 +429,10 @@
     take_high = jnp.where((block == 1) | (block == 5), F32(1.0), F32(0.0))
     y_join(full, (), (1.0, take_low, 1.0, take_high))
     x_join(full, (), x_weights(False))
-    up[...] = face(full, (), 7)
-    down[...] = face(full, (), 0)
+    up[0:64, :] = face(full, (), 7)
+    up[64:128, :] = diag_up[...]
+    down[0:64, :] = face(full, (), 0)
+    down[64:128, :] = diag_down[...]
 
 
 def diagonal_kernel(inv, inv_far, weighted, diag, up, down, weighted_far, diag_far):
@@ -515,11 +528,11 @@
 
 
 def operator_one_kernel(
-    partial, below, above, diag, diag_below, diag_above, source, weighted,
+    partial, below, above, diag, source, weighted,
     residual, inverse, first, local, out, up, down, sums, flux,
 ):
-    z_sum(partial, below[...], above[...], residual)
-    z_sum(diag, diag_below[...], diag_above[...], inverse)
+    z_sum(partial, below[0:64, :], above[0:64, :], residual)
+    z_sum(diag, below[64:128, :], above[64:128, :], inverse)
     inverse[...] = 1.0 / inverse[...]
     first[...] = residual[...] * inverse[...]
     operate(first, weighted, local, flux)
@@ -546,7 +559,7 @@
         part = jnp.sum(mask * value, axis=0, keepdims=True)
         part = jnp.sum(part, axis=1, keepdims=True)
         row = jnp.where(lane == k, part, row)
-    totals[...] = row
+    totals[...] = jnp.broadcast_to(row[None], totals.shape)
     out[...] = local_two[...]
     x_join(out, (), x_weights(False))
     y_join(out, (), y_weights(0, False))
@@ -570,9 +583,9 @@
         to_slots(place, advected, (i,), out, i, scratch)
 
 
-def fields_kernel(place, residual, first, applied, second, out, scratch):
-    for k, ref in enumerate((residual, first, applied, second)):
-        to_slots(place, ref, (), out, k, scratch)
+def fields_kernel(place, left, right, out, scratch):
+    to_slots(place, left, (), out, 0, scratch)
+    to_slots(place, right, (), out, 1, scratch)
 
 
 def last_kernel(place, partial, below, above, out, full, scratch):
@@ -580,7 +593,27 @@
     to_slots(place, full, (), out, 0, scratch)
 
 
-def call(kernel, outs, scratch=(), scalars=0):
+def gather_kernel(pieces, out):
+    row = jnp.sum(pieces[...], axis=0)
+    out[...] = jnp.broadcast_to(row[None], out.shape)
+
+
+def final_kernel(pieces, early, late, last, pressure, residual):
+    row = jnp.sum(pieces[...], axis=0)
+    rho, curvature, cross, tail = (row[:, k : k + 1] for k in range(4))
+    step = rho / curvature
+    rho_next = step * step * cross - rho
+    ratio = rho_next / rho
+    step_next = rho_next / (
+        curvature - 2.0 * step * cross + step * step * tail - ratio * ratio * curvature
+    )
+    keep = step + step_next * (1.0 + ratio)
+    both = step_next * step
+    pressure[...] = keep * early[1] - both * late[1]
+    residual[...] = early[0] - keep * late[0] + both * last[0]
+
+
+def call(kernel, outs, scratch=(), scalars=0, limit=16):
     def run(*args):
         vm = pl.BlockSpec(memory_space=pltpu.VMEM)
         sm = pl.BlockSpec(memory_space=pltpu.SMEM)
@@ -590,6 +623,7 @@
             in_specs=[sm] * scalars + [vm] * (len(args) - scalars),
             out_specs=tuple(vm for _ in outs),
             scratch_shapes=[pltpu.VMEM(shape, F32) for shape in scratch],
+            compiler_params=pltpu.CompilerParams(vmem_limit_bytes=limit * 1024 * 1024),
         )(*args)
         return result
 
@@ -606,30 +640,25 @@
     return shift(up, axis, 1), shift(down, axis, -1)
 
 
-def total(row):
-    for axes in (GX_GY, GZ):
-        count = lax.axis_size(axes)
-        pieces = lax.all_to_all(jnp.broadcast_to(row[None], (count, 1, 128)), axes, 0, 0)
-        row = jnp.sum(pieces, axis=0)
-    return row
-
-
 FULL = (PTS, LANES)
 THREE = (3, PTS, LANES)
 FACE = (64, LANES)
 
 
-def per_device(velocity, inv_density, element_place):
+def step(velocity, inv_density, element_place):
     by_slot = jnp.transpose(velocity, (0, 2, 1))
     inv_slot = jnp.transpose(inv_density)
-    (block,) = call(pack_kernel, [(4, 16, PTS)], scalars=1)(element_place, by_slot, inv_slot)
-    below, above = along("gy", block, block)
-    got = lax.all_gather(jnp.stack([below, block, above]), GX)
+    block, up, down = call(pack_kernel, [(64, PTS), (60, PTS), (60, PTS)], scalars=1)(
+        element_place, by_slot, inv_slot
+    )
+    below, above = along("gy", up, down)
+    middle = lax.all_gather(block, GX)
+    sides = lax.all_gather(jnp.concatenate([below, above]), GX)
     vel, vel_far, rate, rate_far, up, down, inv, inv_far = call(
         first_kernel,
         [THREE, THREE, THREE, THREE, (256, LANES), (256, LANES), FULL, FULL],
         [(256, PTS)],
-    )(got)
+    )(middle, sides)
     below, above = along(GZ, up, down)
     weighted, diag, diag_up, diag_down = call(
         diagonal_kernel, [FULL, FULL, FACE, FACE], [FULL, FULL]
@@ -652,35 +681,30 @@
     (advected_slots,) = call(advected_kernel, [(3, 16, PTS)], [(LANES, PTS)], 1)(
         element_place, advected
     )
-    full, up, down = call(spread_kernel, [FULL, FACE, FACE])(joined, below, above)
-    below, above = along(
-        GZ, jnp.concatenate([up, diag_up]), jnp.concatenate([down, diag_down])
-    )
+    full, up, down = call(spread_kernel, [FULL, (128, LANES), (128, LANES)])(
+        joined, below, above, diag_up, diag_down
+    )
+    below, above = along(GZ, up, down)
     residual, inverse, first, local, partial, up, down, sums = call(
         operator_one_kernel, [FULL, FULL, FULL, FULL, FULL, FACE, FACE, (2, 8, LANES)], [FULL]
-    )(full, below[:64], above[:64], diag, below[64:], above[64:], source, weighted)
+    )(full, below, above, diag, source, weighted)
     below, above = along(GZ, up, down)
+    (early,) = call(fields_kernel, [(2, 16, PTS)], [(LANES, PTS)], 1)(
+        element_place, residual, first
+    )
     applied, second, partial, up, down, totals = call(
-        operator_two_kernel, [FULL, FULL, FULL, FACE, FACE, (1, LANES)], [FULL, FULL]
+        operator_two_kernel, [FULL, FULL, FULL, FACE, FACE, (16, 1, LANES)], [FULL, FULL]
     )(partial, below, above, inverse, weighted, local, sums)
     below, above = along(GZ, up, down)
-    sums = total(totals)
-    (fields,) = call(fields_kernel, [(4, 16, PTS)], [(LANES, PTS)], 1)(
-        element_place, residual, first, applied, second
-    )
+    pieces = lax.all_to_all(totals, GX_GY, 0, 0)
+    count = lax.axis_size(GZ)
+    (pieces,) = call(gather_kernel, [(count, 1, LANES)])(pieces)
+    (late,) = call(fields_kernel, [(2, 16, PTS)], [(LANES, PTS)], 1)(element_place, applied, second)
     (last,) = call(last_kernel, [(1, 16, PTS)], [FULL, (LANES, PTS)], 1)(
         element_place, partial, below, above
     )
-    rho, curvature, cross, tail = sums[0, 0], sums[0, 1], sums[0, 2], sums[0, 3]
-    step = rho / curvature
-    rho_next = step * step * cross - rho
-    ratio = rho_next / rho
-    step_next = rho_next / (
-        curvature - 2.0 * step * cross + step * step * tail - ratio * ratio * curvature
-    )
-    keep = step + step_next * (1.0 + ratio)
-    pressure = keep * fields[1] - step_next * step * fields[3]
-    residual = fields[0] - keep * fields[2] + step_next * step * last[0]
+    pieces = lax.all_to_all(pieces, GZ, 0, 0)
+    pressure, residual = call(final_kernel, [(16, PTS), (16, PTS)])(pieces, early, late, last)
     return (
         jnp.transpose(advected_slots, (0, 2, 1)),
         jnp.transpose(pressure),
@@ -695,7 +719,7 @@
     )
     placed = (P(None, None, GX_GY_GZ), P(None, GX_GY_GZ), P(GX_GY_GZ))
     return jax.shard_map(
-        per_device,
+        step,
         mesh=torus,
         in_specs=placed,
         out_specs=(P(None, None, GX_GY_GZ), P(None, GX_GY_GZ), P(None, GX_GY_GZ)),

time: 268 us -> 190 us (0.71)
  waiting for transfers between devices: 89.7 us -> 41.1 us
  Pallas kernels: 47.4 us -> 24.4 us
  between operations: 20.2 us -> 0.91 us
  blocking collectives: 12.1 us -> 30.9 us
  local copies, waits for them, and re-layouts: 7.55 us -> 2.3 us
  other arithmetic: 4.73 us -> 0.02 us
  starting transfers between devices: 83.5 us -> 87.7 us
    all_gather x1 -> x0, waiting for transfers between devices: 48.5 us -> none  [per_device(): got = lax.all_gather(jnp.stack([below, block, above]), GX)]
    pallas_call x13 -> x16, Pallas kernels: 47.4 us -> 24.4 us  [run(): pl.pallas_call(kernel, out_shape=tuple((jax.ShapeDtypeStruct(shape, F32)...]
    all_gather x0 -> x2, blocking collectives: none -> 19.3 us  [the longest x1 11.3 us: step(): sides = lax.all_gather(jnp.concatenate([below, above]), GX)]
    ppermute x18, starting transfers between devices: 53.5 us -> 58.3 us  [shift(): return lax.ppermute(values, axis, pairs)]
  transfers between devices with their start and end apart: 20 -> 19, of which waited for: 15 -> 14; matrix products, arithmetic and copies ran while one was open for 1% -> 0% of each run, Pallas kernels for 3% -> 2%
where the time goes in v3:
time: 190 us; the launch traced here: 187 us
  starting transfers between devices  87.7 us (46%)
  waiting for transfers between devices  41.1 us (22%)
  blocking collectives  30.9 us (16%)
  Pallas kernels  24.4 us (13%)
  local copies, waits for them, and re-layouts  2.3 us (1%)
    ppermute x18, starting transfers between devices, shift(): return lax.ppermute(values, axis, pairs)  58.3 us
    all_to_all x1, starting transfers between devices, step(): pieces = lax.all_to_all(pieces, GZ, 0, 0)  29.4 us
    ppermute x18, waiting for transfers between devices, shift(): return lax.ppermute(values, axis, pairs)  29.3 us
    pallas_call x16, Pallas kernels, run(): pl.pallas_call(kernel, out_shape=tuple((jax.ShapeDtypeStruct(shape, F32)...  24.4 us
    all_to_all x1, waiting for transfers between devices, step(): pieces = lax.all_to_all(pieces, GZ, 0, 0)  11.8 us
    all_to_all x1, blocking collectives, step(): pieces = lax.all_to_all(totals, GX_GY, 0, 0)  11.7 us
    all_gather x1, blocking collectives, step(): sides = lax.all_gather(jnp.concatenate([below, above]), GX)  11.3 us
    all_gather x1, blocking collectives, step(): middle = lax.all_gather(block, GX)  8.01 us
  transfers between devices with their start and end apart: 19, of which 14 were waited for; matrix products, arithmetic and copies ran while one was open for 0% of the time, Pallas kernels for 2%

profile of v3, /device:TPU:6, one launch (start us, length us, event | category | flops | bytes accessed | tf_op | source)
XLA Modules:
  0.0 187.3 jit_solution(1550015040253793943)
XLA Ops:
  3.8 3.5 %collective-permute-start = (f32[60,512]{1,0:T(8,128)S(1)}, f32[60,512]{1,0:T(8,128)S(1)}, u32[]{:S(2)}, u32[]{:S(2)}) collective-permute-start(f32[60,512]{1,0:T(8,128)S(1)} %get-tuple-element.55), channel_id=1, source_target_pairs={{0,64},{64,128},{128,192},{1,65},{65,129},{129,193},{2,66},{66,130... | collective-permute-start | bytes 368648 | tf_op jit(solution)/shard_map/ppermute | solution.py:636
  8.6 8.0 %all-gather = f32[256,512]{1,0:T(8,128)S(1)} all-gather(f32[64,512]{1,0:T(8,128)S(1)} %get-tuple-element.54), channel_id=2, replica_groups=mesh['gx_0'=2,'gx_1'=2,'gy'=4,'gz_0'=32,'gz_1'=2] {'gx_0','gx_1'}, dimensions={0}, use_global_device_ids=true | all-gather | bytes 655360 | tf_op jit(solution)/shard_map/all_gather | solution.py:655
  16.6 11.3 %all-gather.1 = f32[480,512]{1,0:T(8,128)S(1)} all-gather(f32[120,512]{1,0:T(8,128)S(1)} %pad_maximum_fusion), channel_id=3, replica_groups=mesh['gx_0'=2,'gx_1'=2,'gy'=4,'gz_0'=32,'gz_1'=2] {'gx_0','gx_1'}, dimensions={0}, use_global_device_ids=true | all-gather | bytes 1228800 | tf_op jit(solution)/shard_map/all_gather | solution.py:656
  27.9 4.5 %shard_map.59 = (f32[3,512,128]{2,1,0:T(8,128)S(1)}, f32[3,512,128]{2,1,0:T(8,128)S(1)}, f32[3,512,128]{2,1,0:T(8,128)S(1)}, f32[3,512,128]{2,1,0:T(8,128)S(1)},...) custom-call(f32[4,64,512]{2,1,0:T(8,128)S(1)} %bitcast.8, ...), custom_call_target="tpu_custom_call" | custom-call | tf_op jit(solution)/shard_map/pallas_call | solution.py:620
  32.5 4.1 %collective-permute-start.2 = (f32[256,128]{1,0:T(8,128)S(1)}, f32[256,128]{1,0:T(8,128)S(1)}, u32[]{:S(2)}, u32[]{:S(2)}) collective-permute-start(f32[256,128]{1,0:T(8,128)S(1)} %get-tuple-element.61), channel_id=1, source_target_pairs={{0,1},{1,2},{2,3},{3,4},{4,5},{5,6},{6,7},{7,8},{8,9},{9,10},{10,1... | collective-permute-start | bytes 393224 | tf_op jit(solution)/shard_map/ppermute | solution.py:636
  36.6 8.6 %collective-permute-start.3 = (f32[256,128]{1,0:T(8,128)S(1)}, f32[256,128]{1,0:T(8,128)S(1)}, u32[]{:S(2)}, u32[]{:S(2)}) collective-permute-start(f32[256,128]{1,0:T(8,128)S(1)} %get-tuple-element.62), channel_id=1, source_target_pairs={{1,0},{2,1},{3,2},{4,3},{5,4},{6,5},{7,6},{8,7},{9,8},{10,9},{11,1... | collective-permute-start | bytes 393224 | tf_op jit(solution)/shard_map/ppermute | solution.py:636
  48.4 3.5 %shard_map.60 = (f32[3,512,128]{2,1,0:T(8,128)S(1)}, f32[3,512,128]{2,1,0:T(8,128)S(1)}, f32[192,128]{1,0:T(8,128)S(1)}, f32[192,128]{1,0:T(8,128)S(1)}) custom-call(f32[3,512,128]{2,1,0:T(8,128)S(1)} %get-tuple-element.57.vel, f32[3,512,128]{2,1,0:T(8,128)S(1)} %get-tuple-element.58.vel_far, f32[3,512,128]{2,1,0:T(8,128)S(1)} %get-tuple-element.59.rate, ...), custom_call_target="tpu_custom_call" | custom-call | tf_op jit(solution)/shard_map/pallas_call | solution.py:620
  53.8 3.9 %collective-permute-start.5 = (f32[192,128]{1,0:T(8,128)S(1)}, f32[192,128]{1,0:T(8,128)S(1)}, u32[]{:S(2)}, u32[]{:S(2)}) collective-permute-start(f32[192,128]{1,0:T(8,128)S(1)} %get-tuple-element.66), channel_id=1, source_target_pairs={{1,0},{2,1},{3,2},{4,3},{5,4},{6,5},{7,6},{8,7},{9,8},{10,9},{11,1... | collective-permute-start | bytes 294920 | tf_op jit(solution)/shard_map/ppermute | solution.py:636
  58.4 2.8 %collective-permute-done.5.above = f32[192,128]{1,0:T(8,128)S(1)} collective-permute-done((f32[192,128]{1,0:T(8,128)S(1)}, f32[192,128]{1,0:T(8,128)S(1)}, u32[]{:S(2)}, u32[]{:S(2)}) %collective-permute-start.5) | collective-permute-done | bytes 98336 | tf_op jit(solution)/shard_map/ppermute | solution.py:636
  61.2 2.6 %shard_map.61 = (f32[3,512,128]{2,1,0:T(8,128)S(1)}, f32[3,512,128]{2,1,0:T(8,128)S(1)}, f32[192,128]{1,0:T(8,128)S(1)}, f32[192,128]{1,0:T(8,128)S(1)}) custom-call(f32[3,512,128]{2,1,0:T(8,128)S(1)} %get-tuple-element.57.vel, f32[3,512,128]{2,1,0:T(8,128)S(1)} %get-tuple-element.63.acc_in, f32[3,512,128]{2,1,0:T(8,128)S(1)} %get-tuple-element.64.rate, ...), custom_call_target="tpu_custom_call" | custom-call | tf_op jit(solution)/shard_map/pallas_call | solution.py:620
  65.8 3.9 %collective-permute-start.7 = (f32[192,128]{1,0:T(8,128)S(1)}, f32[192,128]{1,0:T(8,128)S(1)}, u32[]{:S(2)}, u32[]{:S(2)}) collective-permute-start(f32[192,128]{1,0:T(8,128)S(1)} %get-tuple-element.70), channel_id=1, source_target_pairs={{1,0},{2,1},{3,2},{4,3},{5,4},{6,5},{7,6},{8,7},{9,8},{10,9},{11,1... | collective-permute-start | bytes 294920 | tf_op jit(solution)/shard_map/ppermute | solution.py:636
  70.4 2.9 %collective-permute-done.7.above = f32[192,128]{1,0:T(8,128)S(1)} collective-permute-done((f32[192,128]{1,0:T(8,128)S(1)}, f32[192,128]{1,0:T(8,128)S(1)}, u32[]{:S(2)}, u32[]{:S(2)}) %collective-permute-start.7) | collective-permute-done | bytes 98336 | tf_op jit(solution)/shard_map/ppermute | solution.py:636
  78.0 3.7 %collective-permute-start.9 = (f32[192,128]{1,0:T(8,128)S(1)}, f32[192,128]{1,0:T(8,128)S(1)}, u32[]{:S(2)}, u32[]{:S(2)}) collective-permute-start(f32[192,128]{1,0:T(8,128)S(1)} %get-tuple-element.74), channel_id=1, source_target_pairs={{1,0},{2,1},{3,2},{4,3},{5,4},{6,5},{7,6},{8,7},{9,8},{10,9},{11,1... | collective-permute-start | bytes 294920 | tf_op jit(solution)/shard_map/ppermute | solution.py:636
  82.4 3.1 %collective-permute-done.9.above = f32[192,128]{1,0:T(8,128)S(1)} collective-permute-done((f32[192,128]{1,0:T(8,128)S(1)}, f32[192,128]{1,0:T(8,128)S(1)}, u32[]{:S(2)}, u32[]{:S(2)}) %collective-permute-start.9) | collective-permute-done | bytes 98336 | tf_op jit(solution)/shard_map/ppermute | solution.py:636
  86.3 4.5 %collective-permute-start.10 = (f32[128,128]{1,0:T(8,128)S(1)}, f32[128,128]{1,0:T(8,128)S(1)}, u32[]{:S(2)}, u32[]{:S(2)}) collective-permute-start(f32[128,128]{1,0:T(8,128)S(1)} %get-tuple-element.77), channel_id=1, source_target_pairs={{0,64},{64,128},{128,192},{1,65},{65,129},{129,193},{2,66},{66,130... | collective-permute-start | bytes 196616 | tf_op jit(solution)/shard_map/ppermute | solution.py:636
  92.8 4.3 %collective-permute-done.11.above = f32[128,128]{1,0:T(8,128)S(1)} collective-permute-done((f32[128,128]{1,0:T(8,128)S(1)}, f32[128,128]{1,0:T(8,128)S(1)}, u32[]{:S(2)}, u32[]{:S(2)}) %collective-permute-start.11) | collective-permute-done | bytes 65568 | tf_op jit(solution)/shard_map/ppermute | solution.py:636
  97.3 3.9 %collective-permute-start.12 = (f32[128,128]{1,0:T(8,128)S(1)}, f32[128,128]{1,0:T(8,128)S(1)}, u32[]{:S(2)}, u32[]{:S(2)}) collective-permute-start(f32[128,128]{1,0:T(8,128)S(1)} %get-tuple-element.84), channel_id=1, source_target_pairs={{0,1},{1,2},{2,3},{3,4},{4,5},{5,6},{6,7},{7,8},{8,9},{9,10},{10,1... | collective-permute-start | bytes 196616 | tf_op jit(solution)/shard_map/ppermute | solution.py:636
  103.4 5.2 %collective-permute-done.13.above = f32[128,128]{1,0:T(8,128)S(1)} collective-permute-done((f32[128,128]{1,0:T(8,128)S(1)}, f32[128,128]{1,0:T(8,128)S(1)}, u32[]{:S(2)}, u32[]{:S(2)}) %collective-permute-start.13) | collective-permute-done | bytes 65568 | tf_op jit(solution)/shard_map/ppermute | solution.py:636
  110.1 3.9 %collective-permute-start.14 = (f32[64,128]{1,0:T(8,128)S(1)}, f32[64,128]{1,0:T(8,128)S(1)}, u32[]{:S(2)}, u32[]{:S(2)}) collective-permute-start(f32[64,128]{1,0:T(8,128)S(1)} %get-tuple-element.90), channel_id=1, source_target_pairs={{0,1},{1,2},{2,3},{3,4},{4,5},{5,6},{6,7},{7,8},{8,9},{9,10},{10,1... | collective-permute-start | bytes 98312 | tf_op jit(solution)/shard_map/ppermute | solution.py:636
  115.9 4.7 %collective-permute-done.15.above = f32[64,128]{1,0:T(8,128)S(1)} collective-permute-done((f32[64,128]{1,0:T(8,128)S(1)}, f32[64,128]{1,0:T(8,128)S(1)}, u32[]{:S(2)}, u32[]{:S(2)}) %collective-permute-start.15) | collective-permute-done | bytes 32800 | tf_op jit(solution)/shard_map/ppermute | solution.py:636
  122.1 11.7 %all_to_all.10.pieces = f32[16,1,128]{2,1,0:T(1,128)S(1)} all-to-all(f32[16,1,128]{2,1,0:T(1,128)S(1)} %get-tuple-element.95), channel_id=1, replica_groups=mesh['gx_0'=2,'gx_1'=2,'gy'=4,'gz_0'=32,'gz_1'=2] {'gx_0','gx_1','gy'}, dimensions={0} | all-to-all | bytes 16384 | tf_op jit(solution)/shard_map/all_to_all | solution.py:699
  134.4 29.4 %all-to-all-start.1 = ((f32[64,1,128]{2,1,0:T(1,128)}), f32[64,1,128]{2,1,0:T(1,128)S(1)}, u32[]{:S(2)}, u32[]{:S(2)}) async-start(f32[64,1,128]{2,1,0:T(1,128)} %shard_map.69), calls=%async_computation.1 | async-start | bytes 65536 | tf_op jit(solution)/shard_map/all_to_all | solution.py:706
  163.8 3.4 %collective-permute-start.16 = (f32[64,128]{1,0:T(8,128)S(1)}, f32[64,128]{1,0:T(8,128)S(1)}, u32[]{:S(2)}, u32[]{:S(2)}) collective-permute-start(f32[64,128]{1,0:T(8,128)S(1)} %get-tuple-element.101), channel_id=1, source_target_pairs={{0,1},{1,2},{2,3},{3,4},{4,5},{5,6},{6,7},{7,8},{8,9},{9,10},{10,1... | collective-permute-start | bytes 98312 | tf_op jit(solution)/shard_map/ppermute | solution.py:636
  174.6 11.8 %all-to-all-done.1.pieces = f32[64,1,128]{2,1,0:T(1,128)S(1)} async-done(((f32[64,1,128]{2,1,0:T(1,128)}), f32[64,1,128]{2,1,0:T(1,128)S(1)}, u32[]{:S(2)}, u32[]{:S(2)}) %all-to-all-start.1) | async-done | bytes 32800 | tf_op jit(solution)/shard_map/all_to_all | solution.py:706
  (40 shorter events, 37.4 us)
Async XLA Ops:
  0.6 0.7 copy-start.2
  1.3 0.9 copy-start
  2.2 0.8 copy-start.1
  3.8 12.8 %collective-permute-start = (f32[60,512]{1,0:T(8,128)S(1)}, f32[60,512]{1,0:T(8,128)S(1)}, u32[]{:S(2)}, u32[]{:S(2)}) collective-permute-start(f32[60,512]{1,0:T(8,128)S(1)} %get-tuple-element.55), channel_id=1, source_target_pairs={{0,64},{64,128},{128,192},{1,65},{65,129},{129,193},{2,66},{66,130... | collective-permute-start | bytes 368648 | tf_op jit(solution)/shard_map/ppermute | solution.py:636
  7.3 9.3 %collective-permute-start.1 = (f32[60,512]{1,0:T(8,128)S(1)}, f32[60,512]{1,0:T(8,128)S(1)}, u32[]{:S(2)}, u32[]{:S(2)}) collective-permute-start(f32[60,512]{1,0:T(8,128)S(1)} %get-tuple-element.56), channel_id=1, source_target_pairs={{64,0},{128,64},{192,128},{65,1},{129,65},{193,129},{66,2},{130,66... | collective-permute-start | bytes 368648 | tf_op jit(solution)/shard_map/ppermute | solution.py:636
  32.5 15.2 %collective-permute-start.2 = (f32[256,128]{1,0:T(8,128)S(1)}, f32[256,128]{1,0:T(8,128)S(1)}, u32[]{:S(2)}, u32[]{:S(2)}) collective-permute-start(f32[256,128]{1,0:T(8,128)S(1)} %get-tuple-element.61), channel_id=1, source_target_pairs={{0,1},{1,2},{2,3},{3,4},{4,5},{5,6},{6,7},{7,8},{8,9},{9,10},{10,1... | collective-permute-start | bytes 393224 | tf_op jit(solution)/shard_map/ppermute | solution.py:636
  36.6 11.8 %collective-permute-start.3 = (f32[256,128]{1,0:T(8,128)S(1)}, f32[256,128]{1,0:T(8,128)S(1)}, u32[]{:S(2)}, u32[]{:S(2)}) collective-permute-start(f32[256,128]{1,0:T(8,128)S(1)} %get-tuple-element.62), channel_id=1, source_target_pairs={{1,0},{2,1},{3,2},{4,3},{5,4},{6,5},{7,6},{8,7},{9,8},{10,9},{11,1... | collective-permute-start | bytes 393224 | tf_op jit(solution)/shard_map/ppermute | solution.py:636
  51.9 6.5 %collective-permute-start.4 = (f32[192,128]{1,0:T(8,128)S(1)}, f32[192,128]{1,0:T(8,128)S(1)}, u32[]{:S(2)}, u32[]{:S(2)}) collective-permute-start(f32[192,128]{1,0:T(8,128)S(1)} %get-tuple-element.65), channel_id=1, source_target_pairs={{0,1},{1,2},{2,3},{3,4},{4,5},{5,6},{6,7},{7,8},{8,9},{9,10},{10,1... | collective-permute-start | bytes 294920 | tf_op jit(solution)/shard_map/ppermute | solution.py:636
  53.8 7.4 %collective-permute-start.5 = (f32[192,128]{1,0:T(8,128)S(1)}, f32[192,128]{1,0:T(8,128)S(1)}, u32[]{:S(2)}, u32[]{:S(2)}) collective-permute-start(f32[192,128]{1,0:T(8,128)S(1)} %get-tuple-element.66), channel_id=1, source_target_pairs={{1,0},{2,1},{3,2},{4,3},{5,4},{6,5},{7,6},{8,7},{9,8},{10,9},{11,1... | collective-permute-start | bytes 294920 | tf_op jit(solution)/shard_map/ppermute | solution.py:636
  63.8 6.5 %collective-permute-start.6 = (f32[192,128]{1,0:T(8,128)S(1)}, f32[192,128]{1,0:T(8,128)S(1)}, u32[]{:S(2)}, u32[]{:S(2)}) collective-permute-start(f32[192,128]{1,0:T(8,128)S(1)} %get-tuple-element.69), channel_id=1, source_target_pairs={{0,1},{1,2},{2,3},{3,4},{4,5},{5,6},{6,7},{7,8},{8,9},{9,10},{10,1... | collective-permute-start | bytes 294920 | tf_op jit(solution)/shard_map/ppermute | solution.py:636
  65.8 7.4 %collective-permute-start.7 = (f32[192,128]{1,0:T(8,128)S(1)}, f32[192,128]{1,0:T(8,128)S(1)}, u32[]{:S(2)}, u32[]{:S(2)}) collective-permute-start(f32[192,128]{1,0:T(8,128)S(1)} %get-tuple-element.70), channel_id=1, source_target_pairs={{1,0},{2,1},{3,2},{4,3},{5,4},{6,5},{7,6},{8,7},{9,8},{10,9},{11,1... | collective-permute-start | bytes 294920 | tf_op jit(solution)/shard_map/ppermute | solution.py:636
  75.8 6.5 %collective-permute-start.8 = (f32[192,128]{1,0:T(8,128)S(1)}, f32[192,128]{1,0:T(8,128)S(1)}, u32[]{:S(2)}, u32[]{:S(2)}) collective-permute-start(f32[192,128]{1,0:T(8,128)S(1)} %get-tuple-element.73), channel_id=1, source_target_pairs={{0,1},{1,2},{2,3},{3,4},{4,5},{5,6},{6,7},{7,8},{8,9},{9,10},{10,1... | collective-permute-start | bytes 294920 | tf_op jit(solution)/shard_map/ppermute | solution.py:636
  78.0 7.4 %collective-permute-start.9 = (f32[192,128]{1,0:T(8,128)S(1)}, f32[192,128]{1,0:T(8,128)S(1)}, u32[]{:S(2)}, u32[]{:S(2)}) collective-permute-start(f32[192,128]{1,0:T(8,128)S(1)} %get-tuple-element.74), channel_id=1, source_target_pairs={{1,0},{2,1},{3,2},{4,3},{5,4},{6,5},{7,6},{8,7},{9,8},{10,9},{11,1... | collective-permute-start | bytes 294920 | tf_op jit(solution)/shard_map/ppermute | solution.py:636
  86.3 6.5 %collective-permute-start.10 = (f32[128,128]{1,0:T(8,128)S(1)}, f32[128,128]{1,0:T(8,128)S(1)}, u32[]{:S(2)}, u32[]{:S(2)}) collective-permute-start(f32[128,128]{1,0:T(8,128)S(1)} %get-tuple-element.77), channel_id=1, source_target_pairs={{0,64},{64,128},{128,192},{1,65},{65,129},{129,193},{2,66},{66,130... | collective-permute-start | bytes 196616 | tf_op jit(solution)/shard_map/ppermute | solution.py:636
  90.9 6.2 %collective-permute-start.11 = (f32[128,128]{1,0:T(8,128)S(1)}, f32[128,128]{1,0:T(8,128)S(1)}, u32[]{:S(2)}, u32[]{:S(2)}) collective-permute-start(f32[128,128]{1,0:T(8,128)S(1)} %get-tuple-element.78), channel_id=1, source_target_pairs={{64,0},{128,64},{192,128},{65,1},{129,65},{193,129},{66,2},{130,66... | collective-permute-start | bytes 196616 | tf_op jit(solution)/shard_map/ppermute | solution.py:636
  97.3 6.2 %collective-permute-start.12 = (f32[128,128]{1,0:T(8,128)S(1)}, f32[128,128]{1,0:T(8,128)S(1)}, u32[]{:S(2)}, u32[]{:S(2)}) collective-permute-start(f32[128,128]{1,0:T(8,128)S(1)} %get-tuple-element.84), channel_id=1, source_target_pairs={{0,1},{1,2},{2,3},{3,4},{4,5},{5,6},{6,7},{7,8},{8,9},{9,10},{10,1... | collective-permute-start | bytes 196616 | tf_op jit(solution)/shard_map/ppermute | solution.py:636
  101.2 7.5 %collective-permute-start.13 = (f32[128,128]{1,0:T(8,128)S(1)}, f32[128,128]{1,0:T(8,128)S(1)}, u32[]{:S(2)}, u32[]{:S(2)}) collective-permute-start(f32[128,128]{1,0:T(8,128)S(1)} %get-tuple-element.85), channel_id=1, source_target_pairs={{1,0},{2,1},{3,2},{4,3},{5,4},{6,5},{7,6},{8,7},{9,8},{10,9},{11,1... | collective-permute-start | bytes 196616 | tf_op jit(solution)/shard_map/ppermute | solution.py:636
  110.1 5.9 %collective-permute-start.14 = (f32[64,128]{1,0:T(8,128)S(1)}, f32[64,128]{1,0:T(8,128)S(1)}, u32[]{:S(2)}, u32[]{:S(2)}) collective-permute-start(f32[64,128]{1,0:T(8,128)S(1)} %get-tuple-element.90), channel_id=1, source_target_pairs={{0,1},{1,2},{2,3},{3,4},{4,5},{5,6},{6,7},{7,8},{8,9},{9,10},{10,1... | collective-permute-start | bytes 98312 | tf_op jit(solution)/shard_map/ppermute | solution.py:636
  114.0 6.7 %collective-permute-start.15 = (f32[64,128]{1,0:T(8,128)S(1)}, f32[64,128]{1,0:T(8,128)S(1)}, u32[]{:S(2)}, u32[]{:S(2)}) collective-permute-start(f32[64,128]{1,0:T(8,128)S(1)} %get-tuple-element.91), channel_id=1, source_target_pairs={{1,0},{2,1},{3,2},{4,3},{5,4},{6,5},{7,6},{8,7},{9,8},{10,9},{11,1... | collective-permute-start | bytes 98312 | tf_op jit(solution)/shard_map/ppermute | solution.py:636
  134.4 52.0 %all-to-all-start.1 = ((f32[64,1,128]{2,1,0:T(1,128)}), f32[64,1,128]{2,1,0:T(1,128)S(1)}, u32[]{:S(2)}, u32[]{:S(2)}) async-start(f32[64,1,128]{2,1,0:T(1,128)} %shard_map.69), calls=%async_computation.1 | async-start | bytes 65536 | tf_op jit(solution)/shard_map/all_to_all | solution.py:706
  163.8 9.2 %collective-permute-start.16 = (f32[64,128]{1,0:T(8,128)S(1)}, f32[64,128]{1,0:T(8,128)S(1)}, u32[]{:S(2)}, u32[]{:S(2)}) collective-permute-start(f32[64,128]{1,0:T(8,128)S(1)} %get-tuple-element.101), channel_id=1, source_target_pairs={{0,1},{1,2},{2,3},{3,4},{4,5},{5,6},{6,7},{7,8},{8,9},{9,10},{10,1... | collective-permute-start | bytes 98312 | tf_op jit(solution)/shard_map/ppermute | solution.py:636
  167.2 6.7 %collective-permute-start.17 = (f32[64,128]{1,0:T(8,128)S(1)}, f32[64,128]{1,0:T(8,128)S(1)}, u32[]{:S(2)}, u32[]{:S(2)}) collective-permute-start(f32[64,128]{1,0:T(8,128)S(1)} %get-tuple-element.102), channel_id=1, source_target_pairs={{1,0},{2,1},{3,2},{4,3},{5,4},{6,5},{7,6},{8,7},{9,8},{10,9},{11,1... | collective-permute-start | bytes 98312 | tf_op jit(solution)/shard_map/ppermute | solution.py:636

commit v4 on v3

--- a/solution.py
+++ b/solution.py
@@ -9,7 +9,7 @@
 
 GX = ("gx_0", "gx_1")
 GZ = ("gz_0", "gz_1")
-GX_GY = ("gx_0", "gx_1", "gy")
+PLANE = ("gx_0", "gx_1", "gy", "gz_1")
 GX_GY_GZ = ("gx_0", "gx_1", "gy", "gz_0", "gz_1")
 F32 = jnp.float32
 PTS = 512
@@ -60,15 +60,20 @@
 
 
 def mix(matrix, values, which=range(8)):
-    out = []
-    for i in which:
-        total_value = None
-        for j in range(8):
-            if matrix[i][j] != 0.0:
-                term = matrix[i][j] * values[j]
-                total_value = term if total_value is None else total_value + term
-        out.append(total_value)
-    return out
+    sign = 1.0 if matrix is SQUARE else -1.0
+    plus = [values[j] + values[7 - j] for j in range(4)]
+    minus = [values[j] - values[7 - j] for j in range(4)]
+    done = {}
+    for i in sorted({min(i, 7 - i) for i in which}):
+        even = odd = None
+        for j in range(4):
+            p, q = matrix[i][j], matrix[i][7 - j]
+            e, o = 0.5 * (p + q) * plus[j], 0.5 * (p - q) * minus[j]
+            even = e if even is None else even + e
+            odd = o if odd is None else odd + o
+        done[i] = odd + even
+        done[7 - i] = even - odd if sign > 0 else odd - even
+    return [done[i] for i in which]
 
 
 def columns(matrix):
@@ -176,6 +181,22 @@
             far[high] = far_w[2] * g7 + far_w[3] * above
 
 
+def odd_place():
+    return lax.axis_index("gz_1")
+
+
+def route(near, other, at, low, high):
+    odd = jnp.full((1, LANES), odd_place(), jnp.int32) == 1
+    near[at, :] = jnp.where(odd, low, high)
+    other[at, :] = jnp.where(odd, high, low)
+
+
+def arrived(both, across, at):
+    odd = jnp.full((1, LANES), odd_place(), jnp.int32) == 1
+    pair, link = both[1 - odd_place(), at, :], across[at, :]
+    return jnp.where(odd, pair, link), jnp.where(odd, link, pair)
+
+
 def face(ref, lead, c):
     return ref[lead + (pl.ds(c, 64, stride=8), slice(None))]
 
@@ -226,7 +247,16 @@
     lax.fori_loop(0, 8, along_bc, 0)
 
 
-def pack_kernel(place, vel, inv, out, up, down):
+def pack_kernel(place, vel_hbm, inv_hbm, out, up, down, vel, inv, sems):
+    copies = [
+        pltpu.make_async_copy(vel_hbm, vel, sems.at[0]),
+        pltpu.make_async_copy(inv_hbm, inv, sems.at[1]),
+    ]
+    for copy in copies:
+        copy.start()
+    for copy in copies:
+        copy.wait()
+
     def move(s, carry):
         q = place[s]
         r = (q % 4) * 4 + q // 4
@@ -285,13 +315,16 @@
 
     lax.fori_loop(0, 3, component, 0)
     lane, _, _, _ = place_of(0)
-    for c, out in ((7, up), (0, down)):
-        for i in range(3):
-            out[slice(64 * i, 64 * i + 64), :] = face(rate, (i,), c)
+    for i in range(3):
+        at = slice(64 * i, 64 * i + 64)
+        route(up, down, at, face(rate, (i,), 0), face(rate, (i,), 7))
+    ends = []
+    for c in (0, 7):
         far = [face(rate_far, (i,), c) for i in range(3)]
-        out[192:256, :] = jnp.where(
-            lane < 32, far[0], jnp.where(lane < 64, roll(far[1], 32), roll(far[2], 64))
+        ends.append(
+            jnp.where(lane < 32, far[0], jnp.where(lane < 64, roll(far[1], 32), roll(far[2], 64)))
         )
+    route(up, down, slice(192, 256), *ends)
 
 
 def advance(vel, rate, below, above, acc_in, scale, acc_scale, v, acc):
@@ -315,17 +348,19 @@
                 set_face(acc, (i,), c, face(acc_in, (i,), c) + acc_scale * k)
 
 
-def thirds(ref):
-    return [ref[slice(64 * i, 64 * i + 64), :] for i in range(3)]
+def thirds(both, across):
+    got = [arrived(both, across, slice(64 * i, 64 * i + 64)) for i in range(3)]
+    return [pair[0] for pair in got], [pair[1] for pair in got]
 
 
 def second_kernel(
     vel, vel_far, rate, rate_far, below, above, acc, out, up, down, v, v_far, out_far
 ):
     advance(
-        vel, rate, thirds(below), thirds(above), vel, 0.5 * time_step, time_step / 6.0, v, acc
-    )
-    far = [[roll(ref[192:256, :], -32 * i) for i in range(3)] for ref in (below, above)]
+        vel, rate, *thirds(below, above), vel, 0.5 * time_step, time_step / 6.0, v, acc
+    )
+    far = arrived(below, above, slice(192, 256))
+    far = [[roll(part, -32 * i) for i in range(3)] for part in far]
     advance(vel_far, rate_far, far[0], far[1], None, 0.5 * time_step, 0.0, v_far, None)
     minus_cols = columns(MINUS)
     xw = x_weights(True)
@@ -351,15 +386,15 @@
         ref[i, high] = w[2] * f7 + w[3] * roll(f0, -1)
 
 
-def send_faces(rate, up, down):
+def send_faces(rate, near, other):
     for i in range(3):
-        up[slice(64 * i, 64 * i + 64), :] = face(rate, (i,), 7)
-        down[slice(64 * i, 64 * i + 64), :] = face(rate, (i,), 0)
+        at = slice(64 * i, 64 * i + 64)
+        route(near, other, at, face(rate, (i,), 0), face(rate, (i,), 7))
 
 
 def stage_kernel(scale, acc_scale):
     def kernel(vel, acc_in, rate, below, above, acc, out, up, down, v):
-        advance(vel, rate, thirds(below), thirds(above), acc_in, scale, acc_scale, v, acc)
+        advance(vel, rate, *thirds(below, above), acc_in, scale, acc_scale, v, acc)
         minus_cols = columns(MINUS)
         xw = x_weights(True)
         yw = y_weights(0, True)
@@ -382,7 +417,7 @@
 
 
 def source_kernel(acc_in, rate, below, above, advected, source, up, down, joined):
-    advance(acc_in, rate, thirds(below), thirds(above), None, time_step / 6.0, 0.0, advected, None)
+    advance(acc_in, rate, *thirds(below, above), None, time_step / 6.0, 0.0, advected, None)
     cols = columns(DERIV)
     wc = weight_column()
 
@@ -429,10 +464,8 @@
     take_high = jnp.where((block == 1) | (block == 5), F32(1.0), F32(0.0))
     y_join(full, (), (1.0, take_low, 1.0, take_high))
     x_join(full, (), x_weights(False))
-    up[0:64, :] = face(full, (), 7)
-    up[64:128, :] = diag_up[...]
-    down[0:64, :] = face(full, (), 0)
-    down[64:128, :] = diag_down[...]
+    route(up, down, slice(0, 64), face(full, (), 0), face(full, (), 7))
+    route(up, down, slice(64, 128), diag_down[...], diag_up[...])
 
 
 def diagonal_kernel(inv, inv_far, weighted, diag, up, down, weighted_far, diag_far):
@@ -531,8 +564,10 @@
     partial, below, above, diag, source, weighted,
     residual, inverse, first, local, out, up, down, sums, flux,
 ):
-    z_sum(partial, below[0:64, :], above[0:64, :], residual)
-    z_sum(diag, below[64:128, :], above[64:128, :], inverse)
+    zw = z_weights()
+    for src, dst, first_row in ((partial, residual, 0), (diag, inverse, 64)):
+        low, high = arrived(below, above, slice(first_row, first_row + 64))
+        z_sum(src, jnp.where(zw[1] > 0, low, F32(0.0)), jnp.where(zw[3] > 0, high, F32(0.0)), dst)
     inverse[...] = 1.0 / inverse[...]
     first[...] = residual[...] * inverse[...]
     operate(first, weighted, local, flux)
@@ -613,19 +648,20 @@
     residual[...] = early[0] - keep * late[0] + both * last[0]
 
 
-def call(kernel, outs, scratch=(), scalars=0, limit=16):
+def call(kernel, outs, scratch=(), scalars=0, raw=0):
     def run(*args):
         vm = pl.BlockSpec(memory_space=pltpu.VMEM)
         sm = pl.BlockSpec(memory_space=pltpu.SMEM)
-        result = pl.pallas_call(
+        hbm = pl.BlockSpec(memory_space=pltpu.MemorySpace.HBM)
+        return pl.pallas_call(
             kernel,
             out_shape=tuple(jax.ShapeDtypeStruct(shape, F32) for shape in outs),
-            in_specs=[sm] * scalars + [vm] * (len(args) - scalars),
+            in_specs=[sm] * scalars + [hbm] * raw + [vm] * (len(args) - scalars - raw),
             out_specs=tuple(vm for _ in outs),
-            scratch_shapes=[pltpu.VMEM(shape, F32) for shape in scratch],
-            compiler_params=pltpu.CompilerParams(vmem_limit_bytes=limit * 1024 * 1024),
+            scratch_shapes=[pltpu.VMEM(shape, F32) for shape in scratch]
+            + ([pltpu.SemaphoreType.DMA((raw,))] if raw else []),
+            compiler_params=pltpu.CompilerParams(vmem_limit_bytes=16 * 1024 * 1024),
         )(*args)
-        return result
 
     return run
 
@@ -636,6 +672,14 @@
     return lax.ppermute(values, axis, pairs)
 
 
+def paired(near, other):
+    count = lax.axis_size(GZ)
+    links = [pair for i in range(1, count - 1, 2) for pair in ((i, i + 1), (i + 1, i))]
+    across = lax.ppermute(other, GZ, links)
+    both = lax.all_gather(near, "gz_1")
+    return both, across
+
+
 def along(axis, up, down):
     return shift(up, axis, 1), shift(down, axis, -1)
 
@@ -648,9 +692,9 @@
 def step(velocity, inv_density, element_place):
     by_slot = jnp.transpose(velocity, (0, 2, 1))
     inv_slot = jnp.transpose(inv_density)
-    block, up, down = call(pack_kernel, [(64, PTS), (60, PTS), (60, PTS)], scalars=1)(
-        element_place, by_slot, inv_slot
-    )
+    block, up, down = call(
+        pack_kernel, [(64, PTS), (60, PTS), (60, PTS)], [(3, 16, PTS), (16, PTS)], 1, 2
+    )(element_place, by_slot, inv_slot)
     below, above = along("gy", up, down)
     middle = lax.all_gather(block, GX)
     sides = lax.all_gather(jnp.concatenate([below, above]), GX)
@@ -659,7 +703,7 @@
         [THREE, THREE, THREE, THREE, (256, LANES), (256, LANES), FULL, FULL],
         [(256, PTS)],
     )(middle, sides)
-    below, above = along(GZ, up, down)
+    below, above = paired(up, down)
     weighted, diag, diag_up, diag_down = call(
         diagonal_kernel, [FULL, FULL, FACE, FACE], [FULL, FULL]
     )(inv, inv_far)
@@ -667,13 +711,13 @@
         second_kernel, [THREE, THREE, (192, LANES), (192, LANES)], [THREE, THREE, THREE]
     )(vel, vel_far, rate, rate_far, below, above)
     for scale in (0.5 * time_step, time_step):
-        below, above = along(GZ, up, down)
+        below, above = paired(up, down)
         acc, rate, up, down = call(
             stage_kernel(scale, time_step / 3.0),
             [THREE, THREE, (192, LANES), (192, LANES)],
             [THREE],
         )(vel, acc, rate, below, above)
-    below, above = along(GZ, up, down)
+    below, above = paired(up, down)
     advected, source, up, down, joined = call(
         source_kernel, [THREE, FULL, (128, LANES), (128, LANES), FULL]
     )(acc, rate, below, above)
@@ -684,7 +728,7 @@
     full, up, down = call(spread_kernel, [FULL, (128, LANES), (128, LANES)])(
         joined, below, above, diag_up, diag_down
     )
-    below, above = along(GZ, up, down)
+    below, above = paired(up, down)
     residual, inverse, first, local, partial, up, down, sums = call(
         operator_one_kernel, [FULL, FULL, FULL, FULL, FULL, FACE, FACE, (2, 8, LANES)], [FULL]
     )(full, below, above, diag, source, weighted)
@@ -693,17 +737,17 @@
         element_place, residual, first
     )
     applied, second, partial, up, down, totals = call(
-        operator_two_kernel, [FULL, FULL, FULL, FACE, FACE, (16, 1, LANES)], [FULL, FULL]
+        operator_two_kernel, [FULL, FULL, FULL, FACE, FACE, (lax.axis_size(PLANE), 1, LANES)], [FULL, FULL]
     )(partial, below, above, inverse, weighted, local, sums)
     below, above = along(GZ, up, down)
-    pieces = lax.all_to_all(totals, GX_GY, 0, 0)
-    count = lax.axis_size(GZ)
+    pieces = lax.all_to_all(totals, PLANE, 0, 0)
+    count = lax.axis_size("gz_0")
     (pieces,) = call(gather_kernel, [(count, 1, LANES)])(pieces)
     (late,) = call(fields_kernel, [(2, 16, PTS)], [(LANES, PTS)], 1)(element_place, applied, second)
     (last,) = call(last_kernel, [(1, 16, PTS)], [FULL, (LANES, PTS)], 1)(
         element_place, partial, below, above
     )
-    pieces = lax.all_to_all(pieces, GZ, 0, 0)
+    pieces = lax.all_to_all(pieces, "gz_0", 0, 0)
     pressure, residual = call(final_kernel, [(16, PTS), (16, PTS)])(pieces, early, late, last)
     return (
         jnp.transpose(advected_slots, (0, 2, 1)),

time: 190 us -> 185 us (0.974)
  blocking collectives: 30.9 us -> 66 us
  waiting for transfers between devices: 41.1 us -> 21.1 us
  starting transfers between devices: 87.7 us -> 70.3 us
    ppermute x18 -> x8, starting transfers between devices: 58.3 us -> 22.3 us  [shift(): return lax.ppermute(values, axis, pairs)]
    all_gather x0 -> x5, blocking collectives: none -> 35.4 us  [paired(): both = lax.all_gather(near, 'gz_1')]
    ppermute x18 -> x8, waiting for transfers between devices: 29.3 us -> 9.9 us  [shift(): return lax.ppermute(values, axis, pairs)]
    ppermute x0 -> x5, starting transfers between devices: none -> 15.3 us  [paired(): across = lax.ppermute(other, GZ, links)]
    all_to_all x1, starting transfers between devices: 29.4 us -> 32.7 us  [step(): pieces = lax.all_to_all(pieces, 'gz_0', 0, 0)]
  transfers between devices with their start and end apart: 19 -> 14, of which waited for: 14 -> 5; matrix products, arithmetic and copies ran while one was open for 0% -> 0% of each run, Pallas kernels for 2% -> 3%
where the time goes in v4:
time: 185 us; the launch traced here: 183 us
  starting transfers between devices  70.3 us (38%)
  blocking collectives  66 us (36%)
  Pallas kernels  22.8 us (12%)
  waiting for transfers between devices  21.1 us (11%)
  local copies, waits for them, and re-layouts  2.3 us (1%)
    all_gather x5, blocking collectives, paired(): both = lax.all_gather(near, 'gz_1')  35.4 us
    all_to_all x1, starting transfers between devices, step(): pieces = lax.all_to_all(pieces, 'gz_0', 0, 0)  32.7 us
    pallas_call x16, Pallas kernels, run(): pl.pallas_call(kernel, out_shape=tuple((jax.ShapeDtypeStruct(shape, F32)...  22.8 us
    ppermute x8, starting transfers between devices, shift(): return lax.ppermute(values, axis, pairs)  22.3 us
    ppermute x5, starting transfers between devices, paired(): across = lax.ppermute(other, GZ, links)  15.3 us
    all_gather x1, blocking collectives, step(): sides = lax.all_gather(jnp.concatenate([below, above]), GX)  11.3 us
    all_to_all x1, blocking collectives, step(): pieces = lax.all_to_all(totals, PLANE, 0, 0)  11.2 us
    all_to_all x1, waiting for transfers between devices, step(): pieces = lax.all_to_all(pieces, 'gz_0', 0, 0)  11.1 us
  transfers between devices with their start and end apart: 14, of which 5 were waited for; matrix products, arithmetic and copies ran while one was open for 0% of the time, Pallas kernels for 3%

profile of v4, /device:TPU:6, one launch (start us, length us, event | category | flops | bytes accessed | tf_op | source)
XLA Modules:
  0.0 183.3 jit_solution(14882345598618409638)
XLA Ops:
  4.0 3.5 %collective-permute-start = (f32[60,512]{1,0:T(8,128)S(1)}, f32[60,512]{1,0:T(8,128)S(1)}, u32[]{:S(2)}, u32[]{:S(2)}) collective-permute-start(f32[60,512]{1,0:T(8,128)S(1)} %get-tuple-element.55), channel_id=1, source_target_pairs={{0,64},{64,128},{128,192},{1,65},{65,129},{129,193},{2,66},{66,130... | collective-permute-start | bytes 368648 | tf_op jit(solution)/shard_map/ppermute | solution.py:672
  8.8 8.0 %all-gather = f32[256,512]{1,0:T(8,128)S(1)} all-gather(f32[64,512]{1,0:T(8,128)S(1)} %get-tuple-element.54), channel_id=2, replica_groups=mesh['gx_0'=2,'gx_1'=2,'gy'=4,'gz_0'=32,'gz_1'=2] {'gx_0','gx_1'}, dimensions={0}, use_global_device_ids=true | all-gather | bytes 655360 | tf_op jit(solution)/shard_map/all_gather | solution.py:699
  16.8 11.3 %all-gather.1 = f32[480,512]{1,0:T(8,128)S(1)} all-gather(f32[120,512]{1,0:T(8,128)S(1)} %pad_maximum_fusion), channel_id=3, replica_groups=mesh['gx_0'=2,'gx_1'=2,'gy'=4,'gz_0'=32,'gz_1'=2] {'gx_0','gx_1'}, dimensions={0}, use_global_device_ids=true | all-gather | bytes 1228800 | tf_op jit(solution)/shard_map/all_gather | solution.py:700
  28.1 4.0 %shard_map.59 = (f32[3,512,128]{2,1,0:T(8,128)S(1)}, f32[3,512,128]{2,1,0:T(8,128)S(1)}, f32[3,512,128]{2,1,0:T(8,128)S(1)}, f32[3,512,128]{2,1,0:T(8,128)S(1)},...) custom-call(f32[4,64,512]{2,1,0:T(8,128)S(1)} %bitcast.13, ...), custom_call_target="tpu_custom_call" | custom-call | tf_op jit(solution)/shard_map/pallas_call | solution.py:656
  32.1 4.1 %collective-permute-start.2 = (f32[256,128]{1,0:T(8,128)S(1)}, f32[256,128]{1,0:T(8,128)S(1)}, u32[]{:S(2)}, u32[]{:S(2)}) collective-permute-start(f32[256,128]{1,0:T(8,128)S(1)} %get-tuple-element.62), channel_id=1, source_target_pairs={{1,2},{2,1},{3,4},{4,3},{5,6},{6,5},{7,8},{8,7},{9,10},{10,9},{11,... | collective-permute-start | bytes 393224 | tf_op jit(solution)/shard_map/ppermute | solution.py:678
  36.2 10.7 %all-gather.2 = f32[512,128]{1,0:T(8,128)S(1)} all-gather(f32[256,128]{1,0:T(8,128)S(1)} %get-tuple-element.61), channel_id=4, replica_groups=mesh['gx_0'=2,'gx_1'=2,'gy'=4,'gz_0'=32,'gz_1'=2] {'gz_1'}, dimensions={0}, use_global_device_ids=true | all-gather | bytes 393216 | tf_op jit(solution)/shard_map/all_gather | solution.py:679
  46.9 3.2 %shard_map.60 = (f32[3,512,128]{2,1,0:T(8,128)S(1)}, f32[3,512,128]{2,1,0:T(8,128)S(1)}, f32[192,128]{1,0:T(8,128)S(1)}, f32[192,128]{1,0:T(8,128)S(1)}) custom-call(f32[3,512,128]{2,1,0:T(8,128)S(1)} %get-tuple-element.57.vel, f32[3,512,128]{2,1,0:T(8,128)S(1)} %get-tuple-element.58.vel_far, f32[3,512,128]{2,1,0:T(8,128)S(1)} %get-tuple-element.59.rate, ...), custom_call_target="tpu_custom_call" | custom-call | tf_op jit(solution)/shard_map/pallas_call | solution.py:656
  52.0 7.2 %all-gather.3 = f32[384,128]{1,0:T(8,128)S(1)} all-gather(f32[192,128]{1,0:T(8,128)S(1)} %get-tuple-element.65), channel_id=5, replica_groups=mesh['gx_0'=2,'gx_1'=2,'gy'=4,'gz_0'=32,'gz_1'=2] {'gz_1'}, dimensions={0}, use_global_device_ids=true | all-gather | bytes 294912 | tf_op jit(solution)/shard_map/all_gather | solution.py:679
  59.3 2.4 %shard_map.61 = (f32[3,512,128]{2,1,0:T(8,128)S(1)}, f32[3,512,128]{2,1,0:T(8,128)S(1)}, f32[192,128]{1,0:T(8,128)S(1)}, f32[192,128]{1,0:T(8,128)S(1)}) custom-call(f32[3,512,128]{2,1,0:T(8,128)S(1)} %get-tuple-element.57.vel, f32[3,512,128]{2,1,0:T(8,128)S(1)} %get-tuple-element.63.acc_in, f32[3,512,128]{2,1,0:T(8,128)S(1)} %get-tuple-element.64.rate, ...), custom_call_target="tpu_custom_call" | custom-call | tf_op jit(solution)/shard_map/pallas_call | solution.py:656
  61.7 2.9 %collective-permute-start.4 = (f32[192,128]{1,0:T(8,128)S(1)}, f32[192,128]{1,0:T(8,128)S(1)}, u32[]{:S(2)}, u32[]{:S(2)}) collective-permute-start(f32[192,128]{1,0:T(8,128)S(1)} %get-tuple-element.70), channel_id=1, source_target_pairs={{1,2},{2,1},{3,4},{4,3},{5,6},{6,5},{7,8},{8,7},{9,10},{10,9},{11,... | collective-permute-start | bytes 294920 | tf_op jit(solution)/shard_map/ppermute | solution.py:678
  64.5 6.3 %all-gather.4 = f32[384,128]{1,0:T(8,128)S(1)} all-gather(f32[192,128]{1,0:T(8,128)S(1)} %get-tuple-element.69), channel_id=6, replica_groups=mesh['gx_0'=2,'gx_1'=2,'gy'=4,'gz_0'=32,'gz_1'=2] {'gz_1'}, dimensions={0}, use_global_device_ids=true | all-gather | bytes 294912 | tf_op jit(solution)/shard_map/all_gather | solution.py:679
  73.2 3.2 %collective-permute-start.5 = (f32[192,128]{1,0:T(8,128)S(1)}, f32[192,128]{1,0:T(8,128)S(1)}, u32[]{:S(2)}, u32[]{:S(2)}) collective-permute-start(f32[192,128]{1,0:T(8,128)S(1)} %get-tuple-element.74), channel_id=1, source_target_pairs={{1,2},{2,1},{3,4},{4,3},{5,6},{6,5},{7,8},{8,7},{9,10},{10,9},{11,... | collective-permute-start | bytes 294920 | tf_op jit(solution)/shard_map/ppermute | solution.py:678
  76.4 6.2 %all-gather.5 = f32[384,128]{1,0:T(8,128)S(1)} all-gather(f32[192,128]{1,0:T(8,128)S(1)} %get-tuple-element.73), channel_id=7, replica_groups=mesh['gx_0'=2,'gx_1'=2,'gy'=4,'gz_0'=32,'gz_1'=2] {'gz_1'}, dimensions={0}, use_global_device_ids=true | all-gather | bytes 294912 | tf_op jit(solution)/shard_map/all_gather | solution.py:679
  83.5 4.5 %collective-permute-start.6 = (f32[128,128]{1,0:T(8,128)S(1)}, f32[128,128]{1,0:T(8,128)S(1)}, u32[]{:S(2)}, u32[]{:S(2)}) collective-permute-start(f32[128,128]{1,0:T(8,128)S(1)} %get-tuple-element.77), channel_id=1, source_target_pairs={{0,64},{64,128},{128,192},{1,65},{65,129},{129,193},{2,66},{66,130... | collective-permute-start | bytes 196616 | tf_op jit(solution)/shard_map/ppermute | solution.py:672
  89.9 4.3 %collective-permute-done.7.above = f32[128,128]{1,0:T(8,128)S(1)} collective-permute-done((f32[128,128]{1,0:T(8,128)S(1)}, f32[128,128]{1,0:T(8,128)S(1)}, u32[]{:S(2)}, u32[]{:S(2)}) %collective-permute-start.7) | collective-permute-done | bytes 65568 | tf_op jit(solution)/shard_map/ppermute | solution.py:672
  94.4 3.3 %collective-permute-start.8 = (f32[128,128]{1,0:T(8,128)S(1)}, f32[128,128]{1,0:T(8,128)S(1)}, u32[]{:S(2)}, u32[]{:S(2)}) collective-permute-start(f32[128,128]{1,0:T(8,128)S(1)} %get-tuple-element.85), channel_id=1, source_target_pairs={{1,2},{2,1},{3,4},{4,3},{5,6},{6,5},{7,8},{8,7},{9,10},{10,9},{11,... | collective-permute-start | bytes 196616 | tf_op jit(solution)/shard_map/ppermute | solution.py:678
  97.7 4.9 %all-gather.6 = f32[256,128]{1,0:T(8,128)S(1)} all-gather(f32[128,128]{1,0:T(8,128)S(1)} %get-tuple-element.84), channel_id=8, replica_groups=mesh['gx_0'=2,'gx_1'=2,'gy'=4,'gz_0'=32,'gz_1'=2] {'gz_1'}, dimensions={0}, use_global_device_ids=true | all-gather | bytes 196608 | tf_op jit(solution)/shard_map/all_gather | solution.py:679
  104.0 3.5 %collective-permute-start.9 = (f32[64,128]{1,0:T(8,128)S(1)}, f32[64,128]{1,0:T(8,128)S(1)}, u32[]{:S(2)}, u32[]{:S(2)}) collective-permute-start(f32[64,128]{1,0:T(8,128)S(1)} %get-tuple-element.90), channel_id=1, source_target_pairs={{0,1},{1,2},{2,3},{3,4},{4,5},{5,6},{6,7},{7,8},{8,9},{9,10},{10,1... | collective-permute-start | bytes 98312 | tf_op jit(solution)/shard_map/ppermute | solution.py:672
  107.4 2.4 %collective-permute-start.10 = (f32[64,128]{1,0:T(8,128)S(1)}, f32[64,128]{1,0:T(8,128)S(1)}, u32[]{:S(2)}, u32[]{:S(2)}) collective-permute-start(f32[64,128]{1,0:T(8,128)S(1)} %get-tuple-element.91), channel_id=1, source_target_pairs={{1,0},{2,1},{3,2},{4,3},{5,4},{6,5},{7,6},{8,7},{9,8},{10,9},{11,1... | collective-permute-start | bytes 98312 | tf_op jit(solution)/shard_map/ppermute | solution.py:672
  109.8 4.3 %collective-permute-done.10.above = f32[64,128]{1,0:T(8,128)S(1)} collective-permute-done((f32[64,128]{1,0:T(8,128)S(1)}, f32[64,128]{1,0:T(8,128)S(1)}, u32[]{:S(2)}, u32[]{:S(2)}) %collective-permute-start.10) | collective-permute-done | bytes 32800 | tf_op jit(solution)/shard_map/ppermute | solution.py:672
  115.4 11.2 %all_to_all.10.pieces = f32[32,1,128]{2,1,0:T(1,128)S(1)} all-to-all(f32[32,1,128]{2,1,0:T(1,128)S(1)} %get-tuple-element.95), channel_id=1, replica_groups=mesh['gx_0'=2,'gx_1'=2,'gy'=4,'gz_0'=32,'gz_1'=2] {'gx_0','gx_1','gy','g..., dimensions={0} | all-to-all | bytes 32768 | tf_op jit(solution)/shard_map/all_to_all | solution.py:743
  127.3 32.7 %all-to-all-start.1 = ((f32[32,1,128]{2,1,0:T(1,128)}), f32[32,1,128]{2,1,0:T(1,128)S(1)}, u32[]{:S(2)}, u32[]{:S(2)}) async-start(f32[32,1,128]{2,1,0:T(1,128)} %shard_map.69), calls=%async_computation.1 | async-start | bytes 32768 | tf_op jit(solution)/shard_map/all_to_all | solution.py:750
  160.0 3.7 %collective-permute-start.11 = (f32[64,128]{1,0:T(8,128)S(1)}, f32[64,128]{1,0:T(8,128)S(1)}, u32[]{:S(2)}, u32[]{:S(2)}) collective-permute-start(f32[64,128]{1,0:T(8,128)S(1)} %get-tuple-element.101), channel_id=1, source_target_pairs={{0,1},{1,2},{2,3},{3,4},{4,5},{5,6},{6,7},{7,8},{8,9},{9,10},{10,1... | collective-permute-start | bytes 98312 | tf_op jit(solution)/shard_map/ppermute | solution.py:672
  171.2 11.1 %all-to-all-done.1.pieces = f32[32,1,128]{2,1,0:T(1,128)S(1)} async-done(((f32[32,1,128]{2,1,0:T(1,128)}), f32[32,1,128]{2,1,0:T(1,128)S(1)}, u32[]{:S(2)}, u32[]{:S(2)}) %all-to-all-start.1) | async-done | bytes 16416 | tf_op jit(solution)/shard_map/all_to_all | solution.py:750
  (35 shorter events, 23.5 us)
Async XLA Ops:
  0.6 0.7 copy-start.2
  1.3 0.9 copy-start
  2.2 0.8 copy-start.1
  4.0 12.8 %collective-permute-start = (f32[60,512]{1,0:T(8,128)S(1)}, f32[60,512]{1,0:T(8,128)S(1)}, u32[]{:S(2)}, u32[]{:S(2)}) collective-permute-start(f32[60,512]{1,0:T(8,128)S(1)} %get-tuple-element.55), channel_id=1, source_target_pairs={{0,64},{64,128},{128,192},{1,65},{65,129},{129,193},{2,66},{66,130... | collective-permute-start | bytes 368648 | tf_op jit(solution)/shard_map/ppermute | solution.py:672
  7.5 9.3 %collective-permute-start.1 = (f32[60,512]{1,0:T(8,128)S(1)}, f32[60,512]{1,0:T(8,128)S(1)}, u32[]{:S(2)}, u32[]{:S(2)}) collective-permute-start(f32[60,512]{1,0:T(8,128)S(1)} %get-tuple-element.56), channel_id=1, source_target_pairs={{64,0},{128,64},{192,128},{65,1},{129,65},{193,129},{66,2},{130,66... | collective-permute-start | bytes 368648 | tf_op jit(solution)/shard_map/ppermute | solution.py:672
  32.1 14.8 %collective-permute-start.2 = (f32[256,128]{1,0:T(8,128)S(1)}, f32[256,128]{1,0:T(8,128)S(1)}, u32[]{:S(2)}, u32[]{:S(2)}) collective-permute-start(f32[256,128]{1,0:T(8,128)S(1)} %get-tuple-element.62), channel_id=1, source_target_pairs={{1,2},{2,1},{3,4},{4,3},{5,6},{6,5},{7,8},{8,7},{9,10},{10,9},{11,... | collective-permute-start | bytes 393224 | tf_op jit(solution)/shard_map/ppermute | solution.py:678
  50.1 9.2 %collective-permute-start.3 = (f32[192,128]{1,0:T(8,128)S(1)}, f32[192,128]{1,0:T(8,128)S(1)}, u32[]{:S(2)}, u32[]{:S(2)}) collective-permute-start(f32[192,128]{1,0:T(8,128)S(1)} %get-tuple-element.66), channel_id=1, source_target_pairs={{1,2},{2,1},{3,4},{4,3},{5,6},{6,5},{7,8},{8,7},{9,10},{10,9},{11,... | collective-permute-start | bytes 294920 | tf_op jit(solution)/shard_map/ppermute | solution.py:678
  61.7 9.2 %collective-permute-start.4 = (f32[192,128]{1,0:T(8,128)S(1)}, f32[192,128]{1,0:T(8,128)S(1)}, u32[]{:S(2)}, u32[]{:S(2)}) collective-permute-start(f32[192,128]{1,0:T(8,128)S(1)} %get-tuple-element.70), channel_id=1, source_target_pairs={{1,2},{2,1},{3,4},{4,3},{5,6},{6,5},{7,8},{8,7},{9,10},{10,9},{11,... | collective-permute-start | bytes 294920 | tf_op jit(solution)/shard_map/ppermute | solution.py:678
  73.2 9.4 %collective-permute-start.5 = (f32[192,128]{1,0:T(8,128)S(1)}, f32[192,128]{1,0:T(8,128)S(1)}, u32[]{:S(2)}, u32[]{:S(2)}) collective-permute-start(f32[192,128]{1,0:T(8,128)S(1)} %get-tuple-element.74), channel_id=1, source_target_pairs={{1,2},{2,1},{3,4},{4,3},{5,6},{6,5},{7,8},{8,7},{9,10},{10,9},{11,... | collective-permute-start | bytes 294920 | tf_op jit(solution)/shard_map/ppermute | solution.py:678
  83.5 6.4 %collective-permute-start.6 = (f32[128,128]{1,0:T(8,128)S(1)}, f32[128,128]{1,0:T(8,128)S(1)}, u32[]{:S(2)}, u32[]{:S(2)}) collective-permute-start(f32[128,128]{1,0:T(8,128)S(1)} %get-tuple-element.77), channel_id=1, source_target_pairs={{0,64},{64,128},{128,192},{1,65},{65,129},{129,193},{2,66},{66,130... | collective-permute-start | bytes 196616 | tf_op jit(solution)/shard_map/ppermute | solution.py:672
  88.0 6.2 %collective-permute-start.7 = (f32[128,128]{1,0:T(8,128)S(1)}, f32[128,128]{1,0:T(8,128)S(1)}, u32[]{:S(2)}, u32[]{:S(2)}) collective-permute-start(f32[128,128]{1,0:T(8,128)S(1)} %get-tuple-element.78), channel_id=1, source_target_pairs={{64,0},{128,64},{192,128},{65,1},{129,65},{193,129},{66,2},{130,66... | collective-permute-start | bytes 196616 | tf_op jit(solution)/shard_map/ppermute | solution.py:672
  94.4 8.2 %collective-permute-start.8 = (f32[128,128]{1,0:T(8,128)S(1)}, f32[128,128]{1,0:T(8,128)S(1)}, u32[]{:S(2)}, u32[]{:S(2)}) collective-permute-start(f32[128,128]{1,0:T(8,128)S(1)} %get-tuple-element.85), channel_id=1, source_target_pairs={{1,2},{2,1},{3,4},{4,3},{5,6},{6,5},{7,8},{8,7},{9,10},{10,9},{11,... | collective-permute-start | bytes 196616 | tf_op jit(solution)/shard_map/ppermute | solution.py:678
  104.0 5.9 %collective-permute-start.9 = (f32[64,128]{1,0:T(8,128)S(1)}, f32[64,128]{1,0:T(8,128)S(1)}, u32[]{:S(2)}, u32[]{:S(2)}) collective-permute-start(f32[64,128]{1,0:T(8,128)S(1)} %get-tuple-element.90), channel_id=1, source_target_pairs={{0,1},{1,2},{2,3},{3,4},{4,5},{5,6},{6,7},{7,8},{8,9},{9,10},{10,1... | collective-permute-start | bytes 98312 | tf_op jit(solution)/shard_map/ppermute | solution.py:672
  107.4 6.7 %collective-permute-start.10 = (f32[64,128]{1,0:T(8,128)S(1)}, f32[64,128]{1,0:T(8,128)S(1)}, u32[]{:S(2)}, u32[]{:S(2)}) collective-permute-start(f32[64,128]{1,0:T(8,128)S(1)} %get-tuple-element.91), channel_id=1, source_target_pairs={{1,0},{2,1},{3,2},{4,3},{5,4},{6,5},{7,6},{8,7},{9,8},{10,9},{11,1... | collective-permute-start | bytes 98312 | tf_op jit(solution)/shard_map/ppermute | solution.py:672
  127.3 55.1 %all-to-all-start.1 = ((f32[32,1,128]{2,1,0:T(1,128)}), f32[32,1,128]{2,1,0:T(1,128)S(1)}, u32[]{:S(2)}, u32[]{:S(2)}) async-start(f32[32,1,128]{2,1,0:T(1,128)} %shard_map.69), calls=%async_computation.1 | async-start | bytes 32768 | tf_op jit(solution)/shard_map/all_to_all | solution.py:750
  160.0 9.2 %collective-permute-start.11 = (f32[64,128]{1,0:T(8,128)S(1)}, f32[64,128]{1,0:T(8,128)S(1)}, u32[]{:S(2)}, u32[]{:S(2)}) collective-permute-start(f32[64,128]{1,0:T(8,128)S(1)} %get-tuple-element.101), channel_id=1, source_target_pairs={{0,1},{1,2},{2,3},{3,4},{4,5},{5,6},{6,7},{7,8},{8,9},{9,10},{10,1... | collective-permute-start | bytes 98312 | tf_op jit(solution)/shard_map/ppermute | solution.py:672
  163.7 6.8 %collective-permute-start.12 = (f32[64,128]{1,0:T(8,128)S(1)}, f32[64,128]{1,0:T(8,128)S(1)}, u32[]{:S(2)}, u32[]{:S(2)}) collective-permute-start(f32[64,128]{1,0:T(8,128)S(1)} %get-tuple-element.102), channel_id=1, source_target_pairs={{1,0},{2,1},{3,2},{4,3},{5,4},{6,5},{7,6},{8,7},{9,8},{10,9},{11,1... | collective-permute-start | bytes 98312 | tf_op jit(solution)/shard_map/ppermute | solution.py:672

commit v5 on v4

--- a/solution.py
+++ b/solution.py
@@ -392,7 +392,35 @@
         route(near, other, at, face(rate, (i,), 0), face(rate, (i,), 7))
 
 
-def stage_kernel(scale, acc_scale):
+def send_own_faces(rate, near, other):
+    lane, _, _, _ = place_of(0)
+    ends = []
+    for c in (0, 7):
+        f = [face(rate, (i,), c) for i in range(3)]
+        ends.append(
+            (
+                jnp.where(lane < 64, roll(f[0], -32), roll(f[1], 32)),
+                jnp.where(lane < 64, roll(f[2][0:32], -32), roll(f[2][32:64], 32)),
+            )
+        )
+    route(near, other, slice(0, 64), ends[0][0], ends[1][0])
+    route(near, other, slice(64, 96), ends[0][1], ends[1][1])
+
+
+def own_thirds(both, across):
+    wide = arrived(both, across, slice(0, 64))
+    rest = arrived(both, across, slice(64, 96))
+    return [
+        [
+            roll(w, 32),
+            roll(w, -32),
+            jnp.concatenate([roll(r, 32), roll(r, -32)], axis=0),
+        ]
+        for w, r in zip(wide, rest)
+    ]
+
+
+def stage_kernel(scale, acc_scale, send):
     def kernel(vel, acc_in, rate, below, above, acc, out, up, down, v):
         advance(vel, rate, *thirds(below, above), acc_in, scale, acc_scale, v, acc)
         minus_cols = columns(MINUS)
@@ -406,7 +434,7 @@
             return carry
 
         lax.fori_loop(0, 3, component, 0)
-        send_faces(out, up, down)
+        send(out, up, down)
 
     return kernel
 
@@ -417,7 +445,7 @@
 
 
 def source_kernel(acc_in, rate, below, above, advected, source, up, down, joined):
-    advance(acc_in, rate, *thirds(below, above), None, time_step / 6.0, 0.0, advected, None)
+    advance(acc_in, rate, *own_thirds(below, above), None, time_step / 6.0, 0.0, advected, None)
     cols = columns(DERIV)
     wc = weight_column()
 
@@ -502,10 +530,12 @@
     down[...] = face(diag, (), 0)
 
 
-def z_sum(src, below, above, dst):
+def z_sum(src, both, across, first_row, dst):
+    zw = z_weights()
+    low, high = arrived(both, across, slice(first_row, first_row + 64))
     dst[...] = src[...]
-    set_face(dst, (), 0, face(src, (), 0) + below)
-    set_face(dst, (), 7, face(src, (), 7) + above)
+    set_face(dst, (), 0, face(src, (), 0) + jnp.where(zw[1] > 0, low, F32(0.0)))
+    set_face(dst, (), 7, face(src, (), 7) + jnp.where(zw[3] > 0, high, F32(0.0)))
 
 
 def operate(u, weighted, out, flux):
@@ -564,18 +594,15 @@
     partial, below, above, diag, source, weighted,
     residual, inverse, first, local, out, up, down, sums, flux,
 ):
-    zw = z_weights()
-    for src, dst, first_row in ((partial, residual, 0), (diag, inverse, 64)):
-        low, high = arrived(below, above, slice(first_row, first_row + 64))
-        z_sum(src, jnp.where(zw[1] > 0, low, F32(0.0)), jnp.where(zw[3] > 0, high, F32(0.0)), dst)
+    z_sum(partial, below, above, 0, residual)
+    z_sum(diag, below, above, 64, inverse)
     inverse[...] = 1.0 / inverse[...]
     first[...] = residual[...] * inverse[...]
     operate(first, weighted, local, flux)
     out[...] = local[...]
     x_join(out, (), x_weights(False))
     y_join(out, (), y_weights(0, False))
-    up[...] = face(out, (), 7)
-    down[...] = face(out, (), 0)
+    route(up, down, slice(0, 64), face(out, (), 0), face(out, (), 7))
     sums[0] = dot(source, first)
     sums[1] = dot(local, first)
 
@@ -584,7 +611,7 @@
     partial, below, above, inverse, weighted, local, sums,
     applied, second, out, up, down, totals, local_two, flux,
 ):
-    z_sum(partial, below[...], above[...], applied)
+    z_sum(partial, below, above, 0, applied)
     second[...] = applied[...] * inverse[...]
     operate(second, weighted, local_two, flux)
     mask = own_mask()
@@ -598,8 +625,7 @@
     out[...] = local_two[...]
     x_join(out, (), x_weights(False))
     y_join(out, (), y_weights(0, False))
-    up[...] = face(out, (), 7)
-    down[...] = face(out, (), 0)
+    route(up, down, slice(0, 64), face(out, (), 0), face(out, (), 7))
 
 
 def to_slots(place, ref, lead, out, k, scratch):
@@ -624,7 +650,7 @@
 
 
 def last_kernel(place, partial, below, above, out, full, scratch):
-    z_sum(partial, below[...], above[...], full)
+    z_sum(partial, below, above, 0, full)
     to_slots(place, full, (), out, 0, scratch)
 
 
@@ -690,8 +716,9 @@
 
 
 def step(velocity, inv_density, element_place):
-    by_slot = jnp.transpose(velocity, (0, 2, 1))
-    inv_slot = jnp.transpose(inv_density)
+    hbm = pltpu.MemorySpace.HBM
+    by_slot = pltpu.with_memory_space_constraint(jnp.transpose(velocity, (0, 2, 1)), hbm)
+    inv_slot = pltpu.with_memory_space_constraint(jnp.transpose(inv_density), hbm)
     block, up, down = call(
         pack_kernel, [(64, PTS), (60, PTS), (60, PTS)], [(3, 16, PTS), (16, PTS)], 1, 2
     )(element_place, by_slot, inv_slot)
@@ -710,11 +737,11 @@
     acc, rate, up, down = call(
         second_kernel, [THREE, THREE, (192, LANES), (192, LANES)], [THREE, THREE, THREE]
     )(vel, vel_far, rate, rate_far, below, above)
-    for scale in (0.5 * time_step, time_step):
+    for scale, send, rows in ((0.5 * time_step, send_faces, 192), (time_step, send_own_faces, 96)):
         below, above = paired(up, down)
         acc, rate, up, down = call(
-            stage_kernel(scale, time_step / 3.0),
-            [THREE, THREE, (192, LANES), (192, LANES)],
+            stage_kernel(scale, time_step / 3.0, send),
+            [THREE, THREE, (rows, LANES), (rows, LANES)],
             [THREE],
         )(vel, acc, rate, below, above)
     below, above = paired(up, down)
@@ -732,14 +759,14 @@
     residual, inverse, first, local, partial, up, down, sums = call(
         operator_one_kernel, [FULL, FULL, FULL, FULL, FULL, FACE, FACE, (2, 8, LANES)], [FULL]
     )(full, below, above, diag, source, weighted)
-    below, above = along(GZ, up, down)
+    below, above = paired(up, down)
     (early,) = call(fields_kernel, [(2, 16, PTS)], [(LANES, PTS)], 1)(
         element_place, residual, first
     )
     applied, second, partial, up, down, totals = call(
         operator_two_kernel, [FULL, FULL, FULL, FACE, FACE, (lax.axis_size(PLANE), 1, LANES)], [FULL, FULL]
     )(partial, below, above, inverse, weighted, local, sums)
-    below, above = along(GZ, up, down)
+    below, above = paired(up, down)
     pieces = lax.all_to_all(totals, PLANE, 0, 0)
     count = lax.axis_size("gz_0")
     (pieces,) = call(gather_kernel, [(count, 1, LANES)])(pieces)

time: 185 us -> 179 us (0.968)
  blocking collectives: 66 us -> 74.6 us
  starting transfers between devices: 70.3 us -> 63.2 us
  waiting for transfers between devices: 21.1 us -> 14.3 us
    ppermute x8 -> x4, starting transfers between devices: 22.3 us -> 10.6 us  [shift(): return lax.ppermute(values, axis, pairs)]
    all_gather x5 -> x7, blocking collectives: 35.4 us -> 43.1 us  [paired(): both = lax.all_gather(near, 'gz_1')]
    ppermute x5 -> x7, starting transfers between devices: 15.3 us -> 22.5 us  [paired(): across = lax.ppermute(other, GZ, links)]
    ppermute x8 -> x4, waiting for transfers between devices: 9.9 us -> 4.33 us  [shift(): return lax.ppermute(values, axis, pairs)]
    all_to_all x1, starting transfers between devices: 32.7 us -> 30.1 us  [step(): pieces = lax.all_to_all(pieces, 'gz_0', 0, 0)]
  transfers between devices with their start and end apart: 14 -> 12, of which waited for: 5 -> 3; matrix products, arithmetic and copies ran while one was open for 0% -> 0% of each run, Pallas kernels for 3% -> 3%
where the time goes in v5:
time: 179 us; the launch traced here: 177 us
  blocking collectives  74.6 us (42%)
  starting transfers between devices  63.2 us (35%)
  Pallas kernels  23.7 us (13%)
  waiting for transfers between devices  14.3 us (8%)
    all_gather x7, blocking collectives, paired(): both = lax.all_gather(near, 'gz_1')  43.1 us
    all_to_all x1, starting transfers between devices, step(): pieces = lax.all_to_all(pieces, 'gz_0', 0, 0)  30.1 us
    pallas_call x16, Pallas kernels, run(): pl.pallas_call(kernel, out_shape=tuple((jax.ShapeDtypeStruct(shape, F32)...  23.7 us
    ppermute x7, starting transfers between devices, paired(): across = lax.ppermute(other, GZ, links)  22.5 us
    all_to_all x1, blocking collectives, step(): pieces = lax.all_to_all(totals, PLANE, 0, 0)  12.2 us
    all_gather x1, blocking collectives, step(): sides = lax.all_gather(jnp.concatenate([below, above]), GX)  11.3 us
    ppermute x4, starting transfers between devices, shift(): return lax.ppermute(values, axis, pairs)  10.6 us
    all_to_all x1, waiting for transfers between devices, step(): pieces = lax.all_to_all(pieces, 'gz_0', 0, 0)  9.99 us
  transfers between devices with their start and end apart: 12, of which 3 were waited for; matrix products, arithmetic and copies ran while one was open for 0% of the time, Pallas kernels for 3%

profile of v5, /device:TPU:6, one launch (start us, length us, event | category | flops | bytes accessed | tf_op | source)
XLA Modules:
  0.0 177.3 jit_solution(17683534595469561894)
XLA Ops:
  3.0 3.5 %collective-permute-start = (f32[60,512]{1,0:T(8,128)S(1)}, f32[60,512]{1,0:T(8,128)S(1)}, u32[]{:S(2)}, u32[]{:S(2)}) collective-permute-start(f32[60,512]{1,0:T(8,128)S(1)} %get-tuple-element.55), channel_id=1, source_target_pairs={{0,64},{64,128},{128,192},{1,65},{65,129},{129,193},{2,66},{66,130... | collective-permute-start | bytes 368648 | tf_op jit(solution)/shard_map/ppermute | solution.py:698
  7.8 8.0 %all-gather = f32[256,512]{1,0:T(8,128)S(1)} all-gather(f32[64,512]{1,0:T(8,128)S(1)} %get-tuple-element.54), channel_id=2, replica_groups=mesh['gx_0'=2,'gx_1'=2,'gy'=4,'gz_0'=32,'gz_1'=2] {'gx_0','gx_1'}, dimensions={0}, use_global_device_ids=true | all-gather | bytes 655360 | tf_op jit(solution)/shard_map/all_gather | solution.py:726
  15.9 11.3 %all-gather.1 = f32[480,512]{1,0:T(8,128)S(1)} all-gather(f32[120,512]{1,0:T(8,128)S(1)} %pad_maximum_fusion), channel_id=3, replica_groups=mesh['gx_0'=2,'gx_1'=2,'gy'=4,'gz_0'=32,'gz_1'=2] {'gx_0','gx_1'}, dimensions={0}, use_global_device_ids=true | all-gather | bytes 1228800 | tf_op jit(solution)/shard_map/all_gather | solution.py:727
  27.2 4.0 %shard_map.59 = (f32[3,512,128]{2,1,0:T(8,128)S(1)}, f32[3,512,128]{2,1,0:T(8,128)S(1)}, f32[3,512,128]{2,1,0:T(8,128)S(1)}, f32[3,512,128]{2,1,0:T(8,128)S(1)},...) custom-call(f32[4,64,512]{2,1,0:T(8,128)S(1)} %bitcast.15, ...), custom_call_target="tpu_custom_call" | custom-call | tf_op jit(solution)/shard_map/pallas_call | solution.py:682
  31.2 4.1 %collective-permute-start.2 = (f32[256,128]{1,0:T(8,128)S(1)}, f32[256,128]{1,0:T(8,128)S(1)}, u32[]{:S(2)}, u32[]{:S(2)}) collective-permute-start(f32[256,128]{1,0:T(8,128)S(1)} %get-tuple-element.62), channel_id=1, source_target_pairs={{1,2},{2,1},{3,4},{4,3},{5,6},{6,5},{7,8},{8,7},{9,10},{10,9},{11,... | collective-permute-start | bytes 393224 | tf_op jit(solution)/shard_map/ppermute | solution.py:704
  35.3 10.7 %all-gather.2 = f32[512,128]{1,0:T(8,128)S(1)} all-gather(f32[256,128]{1,0:T(8,128)S(1)} %get-tuple-element.61), channel_id=4, replica_groups=mesh['gx_0'=2,'gx_1'=2,'gy'=4,'gz_0'=32,'gz_1'=2] {'gz_1'}, dimensions={0}, use_global_device_ids=true | all-gather | bytes 393216 | tf_op jit(solution)/shard_map/all_gather | solution.py:705
  46.0 3.2 %shard_map.60 = (f32[3,512,128]{2,1,0:T(8,128)S(1)}, f32[3,512,128]{2,1,0:T(8,128)S(1)}, f32[192,128]{1,0:T(8,128)S(1)}, f32[192,128]{1,0:T(8,128)S(1)}) custom-call(f32[3,512,128]{2,1,0:T(8,128)S(1)} %get-tuple-element.57.vel, f32[3,512,128]{2,1,0:T(8,128)S(1)} %get-tuple-element.58.vel_far, f32[3,512,128]{2,1,0:T(8,128)S(1)} %get-tuple-element.59.rate, ...), custom_call_target="tpu_custom_call" | custom-call | tf_op jit(solution)/shard_map/pallas_call | solution.py:682
  51.1 7.2 %all-gather.3 = f32[384,128]{1,0:T(8,128)S(1)} all-gather(f32[192,128]{1,0:T(8,128)S(1)} %get-tuple-element.65), channel_id=5, replica_groups=mesh['gx_0'=2,'gx_1'=2,'gy'=4,'gz_0'=32,'gz_1'=2] {'gz_1'}, dimensions={0}, use_global_device_ids=true | all-gather | bytes 294912 | tf_op jit(solution)/shard_map/all_gather | solution.py:705
  60.7 2.9 %collective-permute-start.4 = (f32[192,128]{1,0:T(8,128)S(1)}, f32[192,128]{1,0:T(8,128)S(1)}, u32[]{:S(2)}, u32[]{:S(2)}) collective-permute-start(f32[192,128]{1,0:T(8,128)S(1)} %get-tuple-element.70), channel_id=1, source_target_pairs={{1,2},{2,1},{3,4},{4,3},{5,6},{6,5},{7,8},{8,7},{9,10},{10,9},{11,... | collective-permute-start | bytes 294920 | tf_op jit(solution)/shard_map/ppermute | solution.py:704
  63.6 6.3 %all-gather.4 = f32[384,128]{1,0:T(8,128)S(1)} all-gather(f32[192,128]{1,0:T(8,128)S(1)} %get-tuple-element.69), channel_id=6, replica_groups=mesh['gx_0'=2,'gx_1'=2,'gy'=4,'gz_0'=32,'gz_1'=2] {'gz_1'}, dimensions={0}, use_global_device_ids=true | all-gather | bytes 294912 | tf_op jit(solution)/shard_map/all_gather | solution.py:705
  69.9 2.4 %shard_map.62 = (f32[3,512,128]{2,1,0:T(8,128)S(1)}, f32[3,512,128]{2,1,0:T(8,128)S(1)}, f32[96,128]{1,0:T(8,128)S(1)}, f32[96,128]{1,0:T(8,128)S(1)}) custom-call(f32[3,512,128]{2,1,0:T(8,128)S(1)} %get-tuple-element.57.vel, f32[3,512,128]{2,1,0:T(8,128)S(1)} %get-tuple-element.67.acc_in, f32[3,512,128]{2,1,0:T(8,128)S(1)} %get-tuple-element.68.rate, ...), custom_call_target="tpu_custom_call" | custom-call | tf_op jit(solution)/shard_map/pallas_call | solution.py:682
  72.4 3.2 %collective-permute-start.5 = (f32[96,128]{1,0:T(8,128)S(1)}, f32[96,128]{1,0:T(8,128)S(1)}, u32[]{:S(2)}, u32[]{:S(2)}) collective-permute-start(f32[96,128]{1,0:T(8,128)S(1)} %get-tuple-element.74), channel_id=1, source_target_pairs={{1,2},{2,1},{3,4},{4,3},{5,6},{6,5},{7,8},{8,7},{9,10},{10,9},{11,... | collective-permute-start | bytes 147464 | tf_op jit(solution)/shard_map/ppermute | solution.py:704
  75.5 4.8 %all-gather.5 = f32[192,128]{1,0:T(8,128)S(1)} all-gather(f32[96,128]{1,0:T(8,128)S(1)} %get-tuple-element.73), channel_id=7, replica_groups=mesh['gx_0'=2,'gx_1'=2,'gy'=4,'gz_0'=32,'gz_1'=2] {'gz_1'}, dimensions={0}, use_global_device_ids=true | all-gather | bytes 147456 | tf_op jit(solution)/shard_map/all_gather | solution.py:705
  81.2 4.5 %collective-permute-start.6 = (f32[128,128]{1,0:T(8,128)S(1)}, f32[128,128]{1,0:T(8,128)S(1)}, u32[]{:S(2)}, u32[]{:S(2)}) collective-permute-start(f32[128,128]{1,0:T(8,128)S(1)} %get-tuple-element.77), channel_id=1, source_target_pairs={{0,64},{64,128},{128,192},{1,65},{65,129},{129,193},{2,66},{66,130... | collective-permute-start | bytes 196616 | tf_op jit(solution)/shard_map/ppermute | solution.py:698
  87.7 4.3 %collective-permute-done.7.above = f32[128,128]{1,0:T(8,128)S(1)} collective-permute-done((f32[128,128]{1,0:T(8,128)S(1)}, f32[128,128]{1,0:T(8,128)S(1)}, u32[]{:S(2)}, u32[]{:S(2)}) %collective-permute-start.7) | collective-permute-done | bytes 65568 | tf_op jit(solution)/shard_map/ppermute | solution.py:698
  92.2 3.6 %collective-permute-start.8 = (f32[128,128]{1,0:T(8,128)S(1)}, f32[128,128]{1,0:T(8,128)S(1)}, u32[]{:S(2)}, u32[]{:S(2)}) collective-permute-start(f32[128,128]{1,0:T(8,128)S(1)} %get-tuple-element.85), channel_id=1, source_target_pairs={{1,2},{2,1},{3,4},{4,3},{5,6},{6,5},{7,8},{8,7},{9,10},{10,9},{11,... | collective-permute-start | bytes 196616 | tf_op jit(solution)/shard_map/ppermute | solution.py:704
  95.8 4.9 %all-gather.6 = f32[256,128]{1,0:T(8,128)S(1)} all-gather(f32[128,128]{1,0:T(8,128)S(1)} %get-tuple-element.84), channel_id=8, replica_groups=mesh['gx_0'=2,'gx_1'=2,'gy'=4,'gz_0'=32,'gz_1'=2] {'gz_1'}, dimensions={0}, use_global_device_ids=true | all-gather | bytes 196608 | tf_op jit(solution)/shard_map/all_gather | solution.py:705
  102.0 3.2 %collective-permute-start.9 = (f32[64,128]{1,0:T(8,128)S(1)}, f32[64,128]{1,0:T(8,128)S(1)}, u32[]{:S(2)}, u32[]{:S(2)}) collective-permute-start(f32[64,128]{1,0:T(8,128)S(1)} %get-tuple-element.91), channel_id=1, source_target_pairs={{1,2},{2,1},{3,4},{4,3},{5,6},{6,5},{7,8},{8,7},{9,10},{10,9},{11,... | collective-permute-start | bytes 98312 | tf_op jit(solution)/shard_map/ppermute | solution.py:704
  105.2 4.6 %all-gather.7 = f32[128,128]{1,0:T(8,128)S(1)} all-gather(f32[64,128]{1,0:T(8,128)S(1)} %get-tuple-element.90), channel_id=9, replica_groups=mesh['gx_0'=2,'gx_1'=2,'gy'=4,'gz_0'=32,'gz_1'=2] {'gz_1'}, dimensions={0}, use_global_device_ids=true | all-gather | bytes 98304 | tf_op jit(solution)/shard_map/all_gather | solution.py:705
  111.1 12.2 %all_to_all.10.pieces = f32[32,1,128]{2,1,0:T(1,128)S(1)} all-to-all(f32[32,1,128]{2,1,0:T(1,128)S(1)} %get-tuple-element.95), channel_id=1, replica_groups=mesh['gx_0'=2,'gx_1'=2,'gy'=4,'gz_0'=32,'gz_1'=2] {'gx_0','gx_1','gy','g..., dimensions={0} | all-to-all | bytes 32768 | tf_op jit(solution)/shard_map/all_to_all | solution.py:770
  123.9 30.1 %all-to-all-start.1 = ((f32[32,1,128]{2,1,0:T(1,128)}), f32[32,1,128]{2,1,0:T(1,128)S(1)}, u32[]{:S(2)}, u32[]{:S(2)}) async-start(f32[32,1,128]{2,1,0:T(1,128)} %shard_map.69), calls=%async_computation.1 | async-start | bytes 32768 | tf_op jit(solution)/shard_map/all_to_all | solution.py:777
  154.1 3.7 %collective-permute-start.10 = (f32[64,128]{1,0:T(8,128)S(1)}, f32[64,128]{1,0:T(8,128)S(1)}, u32[]{:S(2)}, u32[]{:S(2)}) collective-permute-start(f32[64,128]{1,0:T(8,128)S(1)} %get-tuple-element.102), channel_id=1, source_target_pairs={{1,2},{2,1},{3,4},{4,3},{5,6},{6,5},{7,8},{8,7},{9,10},{10,9},{11,... | collective-permute-start | bytes 98312 | tf_op jit(solution)/shard_map/ppermute | solution.py:704
  161.1 4.6 %all-gather.8 = f32[128,128]{1,0:T(8,128)S(1)} all-gather(f32[64,128]{1,0:T(8,128)S(1)} %get-tuple-element.101), channel_id=10, replica_groups=mesh['gx_0'=2,'gx_1'=2,'gy'=4,'gz_0'=32,'gz_1'=2] {'gz_1'}, dimensions={0}, use_global_device_ids=true | all-gather | bytes 98304 | tf_op jit(solution)/shard_map/all_gather | solution.py:705
  166.4 10.0 %all-to-all-done.1.pieces = f32[32,1,128]{2,1,0:T(1,128)S(1)} async-done(((f32[32,1,128]{2,1,0:T(1,128)}), f32[32,1,128]{2,1,0:T(1,128)S(1)}, u32[]{:S(2)}, u32[]{:S(2)}) %all-to-all-start.1) | async-done | bytes 16416 | tf_op jit(solution)/shard_map/all_to_all | solution.py:777
  (29 shorter events, 19.3 us)
Async XLA Ops:
  0.6 0.7 copy-start
  3.0 12.8 %collective-permute-start = (f32[60,512]{1,0:T(8,128)S(1)}, f32[60,512]{1,0:T(8,128)S(1)}, u32[]{:S(2)}, u32[]{:S(2)}) collective-permute-start(f32[60,512]{1,0:T(8,128)S(1)} %get-tuple-element.55), channel_id=1, source_target_pairs={{0,64},{64,128},{128,192},{1,65},{65,129},{129,193},{2,66},{66,130... | collective-permute-start | bytes 368648 | tf_op jit(solution)/shard_map/ppermute | solution.py:698
  6.5 9.3 %collective-permute-start.1 = (f32[60,512]{1,0:T(8,128)S(1)}, f32[60,512]{1,0:T(8,128)S(1)}, u32[]{:S(2)}, u32[]{:S(2)}) collective-permute-start(f32[60,512]{1,0:T(8,128)S(1)} %get-tuple-element.56), channel_id=1, source_target_pairs={{64,0},{128,64},{192,128},{65,1},{129,65},{193,129},{66,2},{130,66... | collective-permute-start | bytes 368648 | tf_op jit(solution)/shard_map/ppermute | solution.py:698
  31.2 14.8 %collective-permute-start.2 = (f32[256,128]{1,0:T(8,128)S(1)}, f32[256,128]{1,0:T(8,128)S(1)}, u32[]{:S(2)}, u32[]{:S(2)}) collective-permute-start(f32[256,128]{1,0:T(8,128)S(1)} %get-tuple-element.62), channel_id=1, source_target_pairs={{1,2},{2,1},{3,4},{4,3},{5,6},{6,5},{7,8},{8,7},{9,10},{10,9},{11,... | collective-permute-start | bytes 393224 | tf_op jit(solution)/shard_map/ppermute | solution.py:704
  49.2 9.2 %collective-permute-start.3 = (f32[192,128]{1,0:T(8,128)S(1)}, f32[192,128]{1,0:T(8,128)S(1)}, u32[]{:S(2)}, u32[]{:S(2)}) collective-permute-start(f32[192,128]{1,0:T(8,128)S(1)} %get-tuple-element.66), channel_id=1, source_target_pairs={{1,2},{2,1},{3,4},{4,3},{5,6},{6,5},{7,8},{8,7},{9,10},{10,9},{11,... | collective-permute-start | bytes 294920 | tf_op jit(solution)/shard_map/ppermute | solution.py:704
  60.7 9.2 %collective-permute-start.4 = (f32[192,128]{1,0:T(8,128)S(1)}, f32[192,128]{1,0:T(8,128)S(1)}, u32[]{:S(2)}, u32[]{:S(2)}) collective-permute-start(f32[192,128]{1,0:T(8,128)S(1)} %get-tuple-element.70), channel_id=1, source_target_pairs={{1,2},{2,1},{3,4},{4,3},{5,6},{6,5},{7,8},{8,7},{9,10},{10,9},{11,... | collective-permute-start | bytes 294920 | tf_op jit(solution)/shard_map/ppermute | solution.py:704
  72.4 7.9 %collective-permute-start.5 = (f32[96,128]{1,0:T(8,128)S(1)}, f32[96,128]{1,0:T(8,128)S(1)}, u32[]{:S(2)}, u32[]{:S(2)}) collective-permute-start(f32[96,128]{1,0:T(8,128)S(1)} %get-tuple-element.74), channel_id=1, source_target_pairs={{1,2},{2,1},{3,4},{4,3},{5,6},{6,5},{7,8},{8,7},{9,10},{10,9},{11,... | collective-permute-start | bytes 147464 | tf_op jit(solution)/shard_map/ppermute | solution.py:704
  81.2 6.4 %collective-permute-start.6 = (f32[128,128]{1,0:T(8,128)S(1)}, f32[128,128]{1,0:T(8,128)S(1)}, u32[]{:S(2)}, u32[]{:S(2)}) collective-permute-start(f32[128,128]{1,0:T(8,128)S(1)} %get-tuple-element.77), channel_id=1, source_target_pairs={{0,64},{64,128},{128,192},{1,65},{65,129},{129,193},{2,66},{66,130... | collective-permute-start | bytes 196616 | tf_op jit(solution)/shard_map/ppermute | solution.py:698
  85.8 6.2 %collective-permute-start.7 = (f32[128,128]{1,0:T(8,128)S(1)}, f32[128,128]{1,0:T(8,128)S(1)}, u32[]{:S(2)}, u32[]{:S(2)}) collective-permute-start(f32[128,128]{1,0:T(8,128)S(1)} %get-tuple-element.78), channel_id=1, source_target_pairs={{64,0},{128,64},{192,128},{65,1},{129,65},{193,129},{66,2},{130,66... | collective-permute-start | bytes 196616 | tf_op jit(solution)/shard_map/ppermute | solution.py:698
  92.2 8.5 %collective-permute-start.8 = (f32[128,128]{1,0:T(8,128)S(1)}, f32[128,128]{1,0:T(8,128)S(1)}, u32[]{:S(2)}, u32[]{:S(2)}) collective-permute-start(f32[128,128]{1,0:T(8,128)S(1)} %get-tuple-element.85), channel_id=1, source_target_pairs={{1,2},{2,1},{3,4},{4,3},{5,6},{6,5},{7,8},{8,7},{9,10},{10,9},{11,... | collective-permute-start | bytes 196616 | tf_op jit(solution)/shard_map/ppermute | solution.py:704
  102.0 7.8 %collective-permute-start.9 = (f32[64,128]{1,0:T(8,128)S(1)}, f32[64,128]{1,0:T(8,128)S(1)}, u32[]{:S(2)}, u32[]{:S(2)}) collective-permute-start(f32[64,128]{1,0:T(8,128)S(1)} %get-tuple-element.91), channel_id=1, source_target_pairs={{1,2},{2,1},{3,4},{4,3},{5,6},{6,5},{7,8},{8,7},{9,10},{10,9},{11,... | collective-permute-start | bytes 98312 | tf_op jit(solution)/shard_map/ppermute | solution.py:704
  123.9 52.5 %all-to-all-start.1 = ((f32[32,1,128]{2,1,0:T(1,128)}), f32[32,1,128]{2,1,0:T(1,128)S(1)}, u32[]{:S(2)}, u32[]{:S(2)}) async-start(f32[32,1,128]{2,1,0:T(1,128)} %shard_map.69), calls=%async_computation.1 | async-start | bytes 32768 | tf_op jit(solution)/shard_map/all_to_all | solution.py:777
  154.1 11.7 %collective-permute-start.10 = (f32[64,128]{1,0:T(8,128)S(1)}, f32[64,128]{1,0:T(8,128)S(1)}, u32[]{:S(2)}, u32[]{:S(2)}) collective-permute-start(f32[64,128]{1,0:T(8,128)S(1)} %get-tuple-element.102), channel_id=1, source_target_pairs={{1,2},{2,1},{3,4},{4,3},{5,6},{6,5},{7,8},{8,7},{9,10},{10,9},{11,... | collective-permute-start | bytes 98312 | tf_op jit(solution)/shard_map/ppermute | solution.py:704

commit v6 on v5

--- a/solution.py
+++ b/solution.py
@@ -214,7 +214,7 @@
             out[i, at] = vel[0, at] * got[a]
         return carry
 
-    lax.fori_loop(0, 8, along_a, 0)
+    lax.fori_loop(0, 8, along_a, 0, unroll=8)
 
     def along_bc(a, carry):
         start = 64 * a
@@ -225,7 +225,7 @@
             out[i, at] = out[i, at] + (vel[1, at] * got[b] + vel[2, at] * inner)
         return carry
 
-    lax.fori_loop(0, 8, along_bc, 0)
+    lax.fori_loop(0, 8, along_bc, 0, unroll=4)
 
 
 def convect_y_faces(i, v, vel, out, minus_cols):
@@ -244,11 +244,12 @@
             out[i, at] = out[i, at] + (vel[1, at] * value + vel[2, at] * inner)
         return carry
 
-    lax.fori_loop(0, 8, along_bc, 0)
-
-
-def pack_kernel(place, vel_hbm, inv_hbm, out, up, down, vel, inv, sems):
+    lax.fori_loop(0, 8, along_bc, 0, unroll=4)
+
+
+def pack_kernel(place_hbm, vel_hbm, inv_hbm, out, up, down, vel, inv, place, sems):
     copies = [
+        pltpu.make_async_copy(place_hbm, place, sems.at[2]),
         pltpu.make_async_copy(vel_hbm, vel, sems.at[0]),
         pltpu.make_async_copy(inv_hbm, inv, sems.at[1]),
     ]
@@ -339,7 +340,7 @@
                 acc[i, at] = acc_in[i, at] + acc_scale * r
         return carry
 
-    lax.fori_loop(0, 64, step, 0, unroll=2)
+    lax.fori_loop(0, 64, step, 0, unroll=8)
     for i in range(3):
         for c, got, own, other in ((0, below, zw[0], zw[1]), (7, above, zw[2], zw[3])):
             k = own * face(rate, (i,), c) + other * got[i]
@@ -456,7 +457,7 @@
             source[rows8(64 * a + start)] = got[a]
         return carry
 
-    lax.fori_loop(0, 8, along_a, 0)
+    lax.fori_loop(0, 8, along_a, 0, unroll=8)
     for a in range(8):
         start = 64 * a
         got = mix(DERIV, [advected[1, slice(start + 8 * b, start + 8 * b + 8)] for b in range(8)])
@@ -554,7 +555,7 @@
             out[at[a]] = got[a]
         return carry
 
-    lax.fori_loop(0, 8, along_a, 0)
+    lax.fori_loop(0, 8, along_a, 0, unroll=8)
 
     for a in range(8):
         start = 64 * a
@@ -573,7 +574,7 @@
         out[at] = out[at] + mix_inner(cols_t, flux, (), 8 * k)
         return carry
 
-    lax.fori_loop(0, 64, along_c, 0, unroll=4)
+    lax.fori_loop(0, 64, along_c, 0, unroll=16)
 
 
 def own_mask():
@@ -685,7 +686,7 @@
             in_specs=[sm] * scalars + [hbm] * raw + [vm] * (len(args) - scalars - raw),
             out_specs=tuple(vm for _ in outs),
             scratch_shapes=[pltpu.VMEM(shape, F32) for shape in scratch]
-            + ([pltpu.SemaphoreType.DMA((raw,))] if raw else []),
+            + ([pltpu.SMEM((16,), jnp.int32), pltpu.SemaphoreType.DMA((raw,))] if raw else []),
             compiler_params=pltpu.CompilerParams(vmem_limit_bytes=16 * 1024 * 1024),
         )(*args)
 
@@ -720,8 +721,8 @@
     by_slot = pltpu.with_memory_space_constraint(jnp.transpose(velocity, (0, 2, 1)), hbm)
     inv_slot = pltpu.with_memory_space_constraint(jnp.transpose(inv_density), hbm)
     block, up, down = call(
-        pack_kernel, [(64, PTS), (60, PTS), (60, PTS)], [(3, 16, PTS), (16, PTS)], 1, 2
-    )(element_place, by_slot, inv_slot)
+        pack_kernel, [(64, PTS), (60, PTS), (60, PTS)], [(3, 16, PTS), (16, PTS)], 0, 3
+    )(pltpu.with_memory_space_constraint(element_place, hbm), by_slot, inv_slot)
     below, above = along("gy", up, down)
     middle = lax.all_gather(block, GX)
     sides = lax.all_gather(jnp.concatenate([below, above]), GX)

time: 179 us -> 175 us (0.978)
  Pallas kernels: 23.7 us -> 20.3 us
    pallas_call x16, Pallas kernels: 23.7 us -> 20.3 us  [run(): pl.pallas_call(kernel, out_shape=tuple((jax.ShapeDtypeStruct(shape, F32)...]
where the time goes in v6:
time: 175 us; the launch traced here: 173 us
  blocking collectives  74.6 us (43%)
  starting transfers between devices  63.2 us (36%)
  Pallas kernels  20.3 us (12%)
  waiting for transfers between devices  14.3 us (8%)
    all_gather x7, blocking collectives, paired(): both = lax.all_gather(near, 'gz_1')  43.1 us
    all_to_all x1, starting transfers between devices, step(): pieces = lax.all_to_all(pieces, 'gz_0', 0, 0)  30.1 us
    ppermute x7, starting transfers between devices, paired(): across = lax.ppermute(other, GZ, links)  22.5 us
    pallas_call x16, Pallas kernels, run(): pl.pallas_call(kernel, out_shape=tuple((jax.ShapeDtypeStruct(shape, F32)...  20.3 us
    all_to_all x1, blocking collectives, step(): pieces = lax.all_to_all(totals, PLANE, 0, 0)  12.2 us
    all_gather x1, blocking collectives, step(): sides = lax.all_gather(jnp.concatenate([below, above]), GX)  11.3 us
    ppermute x4, starting transfers between devices, shift(): return lax.ppermute(values, axis, pairs)  10.6 us
    all_to_all x1, waiting for transfers between devices, step(): pieces = lax.all_to_all(pieces, 'gz_0', 0, 0)  9.97 us
  transfers between devices with their start and end apart: 12, of which 3 were waited for; matrix products, arithmetic and copies ran while one was open for 0% of the time, Pallas kernels for 3%

profile of v6, /device:TPU:6, one launch (start us, length us, event | category | flops | bytes accessed | tf_op | source)
XLA Modules:
  0.0 173.3 jit_solution(8290681840894874664)
XLA Ops:
  1.9 3.5 %collective-permute-start = (f32[60,512]{1,0:T(8,128)S(1)}, f32[60,512]{1,0:T(8,128)S(1)}, u32[]{:S(2)}, u32[]{:S(2)}) collective-permute-start(f32[60,512]{1,0:T(8,128)S(1)} %get-tuple-element.55), channel_id=1, source_target_pairs={{0,64},{64,128},{128,192},{1,65},{65,129},{129,193},{2,66},{66,130... | collective-permute-start | bytes 368648 | tf_op jit(solution)/shard_map/ppermute | solution.py:699
  6.7 8.0 %all-gather = f32[256,512]{1,0:T(8,128)S(1)} all-gather(f32[64,512]{1,0:T(8,128)S(1)} %get-tuple-element.54), channel_id=2, replica_groups=mesh['gx_0'=2,'gx_1'=2,'gy'=4,'gz_0'=32,'gz_1'=2] {'gx_0','gx_1'}, dimensions={0}, use_global_device_ids=true | all-gather | bytes 655360 | tf_op jit(solution)/shard_map/all_gather | solution.py:727
  14.7 11.3 %all-gather.1 = f32[480,512]{1,0:T(8,128)S(1)} all-gather(f32[120,512]{1,0:T(8,128)S(1)} %pad_maximum_fusion), channel_id=3, replica_groups=mesh['gx_0'=2,'gx_1'=2,'gy'=4,'gz_0'=32,'gz_1'=2] {'gx_0','gx_1'}, dimensions={0}, use_global_device_ids=true | all-gather | bytes 1228800 | tf_op jit(solution)/shard_map/all_gather | solution.py:728
  26.0 3.3 %shard_map.59 = (f32[3,512,128]{2,1,0:T(8,128)S(1)}, f32[3,512,128]{2,1,0:T(8,128)S(1)}, f32[3,512,128]{2,1,0:T(8,128)S(1)}, f32[3,512,128]{2,1,0:T(8,128)S(1)},...) custom-call(f32[4,64,512]{2,1,0:T(8,128)S(1)} %bitcast.15, ...), custom_call_target="tpu_custom_call" | custom-call | tf_op jit(solution)/shard_map/pallas_call | solution.py:683
  29.3 4.1 %collective-permute-start.2 = (f32[256,128]{1,0:T(8,128)S(1)}, f32[256,128]{1,0:T(8,128)S(1)}, u32[]{:S(2)}, u32[]{:S(2)}) collective-permute-start(f32[256,128]{1,0:T(8,128)S(1)} %get-tuple-element.62), channel_id=1, source_target_pairs={{1,2},{2,1},{3,4},{4,3},{5,6},{6,5},{7,8},{8,7},{9,10},{10,9},{11,... | collective-permute-start | bytes 393224 | tf_op jit(solution)/shard_map/ppermute | solution.py:705
  33.4 10.7 %all-gather.2 = f32[512,128]{1,0:T(8,128)S(1)} all-gather(f32[256,128]{1,0:T(8,128)S(1)} %get-tuple-element.61), channel_id=4, replica_groups=mesh['gx_0'=2,'gx_1'=2,'gy'=4,'gz_0'=32,'gz_1'=2] {'gz_1'}, dimensions={0}, use_global_device_ids=true | all-gather | bytes 393216 | tf_op jit(solution)/shard_map/all_gather | solution.py:706
  44.1 2.4 %shard_map.60 = (f32[3,512,128]{2,1,0:T(8,128)S(1)}, f32[3,512,128]{2,1,0:T(8,128)S(1)}, f32[192,128]{1,0:T(8,128)S(1)}, f32[192,128]{1,0:T(8,128)S(1)}) custom-call(f32[3,512,128]{2,1,0:T(8,128)S(1)} %get-tuple-element.57.vel, f32[3,512,128]{2,1,0:T(8,128)S(1)} %get-tuple-element.58.vel_far, f32[3,512,128]{2,1,0:T(8,128)S(1)} %get-tuple-element.59.rate, ...), custom_call_target="tpu_custom_call" | custom-call | tf_op jit(solution)/shard_map/pallas_call | solution.py:683
  48.4 7.2 %all-gather.3 = f32[384,128]{1,0:T(8,128)S(1)} all-gather(f32[192,128]{1,0:T(8,128)S(1)} %get-tuple-element.65), channel_id=5, replica_groups=mesh['gx_0'=2,'gx_1'=2,'gy'=4,'gz_0'=32,'gz_1'=2] {'gz_1'}, dimensions={0}, use_global_device_ids=true | all-gather | bytes 294912 | tf_op jit(solution)/shard_map/all_gather | solution.py:706
  57.6 2.9 %collective-permute-start.4 = (f32[192,128]{1,0:T(8,128)S(1)}, f32[192,128]{1,0:T(8,128)S(1)}, u32[]{:S(2)}, u32[]{:S(2)}) collective-permute-start(f32[192,128]{1,0:T(8,128)S(1)} %get-tuple-element.70), channel_id=1, source_target_pairs={{1,2},{2,1},{3,4},{4,3},{5,6},{6,5},{7,8},{8,7},{9,10},{10,9},{11,... | collective-permute-start | bytes 294920 | tf_op jit(solution)/shard_map/ppermute | solution.py:705
  60.5 6.3 %all-gather.4 = f32[384,128]{1,0:T(8,128)S(1)} all-gather(f32[192,128]{1,0:T(8,128)S(1)} %get-tuple-element.69), channel_id=6, replica_groups=mesh['gx_0'=2,'gx_1'=2,'gy'=4,'gz_0'=32,'gz_1'=2] {'gz_1'}, dimensions={0}, use_global_device_ids=true | all-gather | bytes 294912 | tf_op jit(solution)/shard_map/all_gather | solution.py:706
  66.8 2.0 %shard_map.62 = (f32[3,512,128]{2,1,0:T(8,128)S(1)}, f32[3,512,128]{2,1,0:T(8,128)S(1)}, f32[96,128]{1,0:T(8,128)S(1)}, f32[96,128]{1,0:T(8,128)S(1)}) custom-call(f32[3,512,128]{2,1,0:T(8,128)S(1)} %get-tuple-element.57.vel, f32[3,512,128]{2,1,0:T(8,128)S(1)} %get-tuple-element.67.acc_in, f32[3,512,128]{2,1,0:T(8,128)S(1)} %get-tuple-element.68.rate, ...), custom_call_target="tpu_custom_call" | custom-call | tf_op jit(solution)/shard_map/pallas_call | solution.py:683
  68.8 3.2 %collective-permute-start.5 = (f32[96,128]{1,0:T(8,128)S(1)}, f32[96,128]{1,0:T(8,128)S(1)}, u32[]{:S(2)}, u32[]{:S(2)}) collective-permute-start(f32[96,128]{1,0:T(8,128)S(1)} %get-tuple-element.74), channel_id=1, source_target_pairs={{1,2},{2,1},{3,4},{4,3},{5,6},{6,5},{7,8},{8,7},{9,10},{10,9},{11,... | collective-permute-start | bytes 147464 | tf_op jit(solution)/shard_map/ppermute | solution.py:705
  72.0 4.8 %all-gather.5 = f32[192,128]{1,0:T(8,128)S(1)} all-gather(f32[96,128]{1,0:T(8,128)S(1)} %get-tuple-element.73), channel_id=7, replica_groups=mesh['gx_0'=2,'gx_1'=2,'gy'=4,'gz_0'=32,'gz_1'=2] {'gz_1'}, dimensions={0}, use_global_device_ids=true | all-gather | bytes 147456 | tf_op jit(solution)/shard_map/all_gather | solution.py:706
  77.5 4.5 %collective-permute-start.6 = (f32[128,128]{1,0:T(8,128)S(1)}, f32[128,128]{1,0:T(8,128)S(1)}, u32[]{:S(2)}, u32[]{:S(2)}) collective-permute-start(f32[128,128]{1,0:T(8,128)S(1)} %get-tuple-element.77), channel_id=1, source_target_pairs={{0,64},{64,128},{128,192},{1,65},{65,129},{129,193},{2,66},{66,130... | collective-permute-start | bytes 196616 | tf_op jit(solution)/shard_map/ppermute | solution.py:699
  84.0 4.3 %collective-permute-done.7.above = f32[128,128]{1,0:T(8,128)S(1)} collective-permute-done((f32[128,128]{1,0:T(8,128)S(1)}, f32[128,128]{1,0:T(8,128)S(1)}, u32[]{:S(2)}, u32[]{:S(2)}) %collective-permute-start.7) | collective-permute-done | bytes 65568 | tf_op jit(solution)/shard_map/ppermute | solution.py:699
  88.5 3.6 %collective-permute-start.8 = (f32[128,128]{1,0:T(8,128)S(1)}, f32[128,128]{1,0:T(8,128)S(1)}, u32[]{:S(2)}, u32[]{:S(2)}) collective-permute-start(f32[128,128]{1,0:T(8,128)S(1)} %get-tuple-element.85), channel_id=1, source_target_pairs={{1,2},{2,1},{3,4},{4,3},{5,6},{6,5},{7,8},{8,7},{9,10},{10,9},{11,... | collective-permute-start | bytes 196616 | tf_op jit(solution)/shard_map/ppermute | solution.py:705
  92.1 4.9 %all-gather.6 = f32[256,128]{1,0:T(8,128)S(1)} all-gather(f32[128,128]{1,0:T(8,128)S(1)} %get-tuple-element.84), channel_id=8, replica_groups=mesh['gx_0'=2,'gx_1'=2,'gy'=4,'gz_0'=32,'gz_1'=2] {'gz_1'}, dimensions={0}, use_global_device_ids=true | all-gather | bytes 196608 | tf_op jit(solution)/shard_map/all_gather | solution.py:706
  98.2 3.2 %collective-permute-start.9 = (f32[64,128]{1,0:T(8,128)S(1)}, f32[64,128]{1,0:T(8,128)S(1)}, u32[]{:S(2)}, u32[]{:S(2)}) collective-permute-start(f32[64,128]{1,0:T(8,128)S(1)} %get-tuple-element.91), channel_id=1, source_target_pairs={{1,2},{2,1},{3,4},{4,3},{5,6},{6,5},{7,8},{8,7},{9,10},{10,9},{11,... | collective-permute-start | bytes 98312 | tf_op jit(solution)/shard_map/ppermute | solution.py:705
  101.3 4.6 %all-gather.7 = f32[128,128]{1,0:T(8,128)S(1)} all-gather(f32[64,128]{1,0:T(8,128)S(1)} %get-tuple-element.90), channel_id=9, replica_groups=mesh['gx_0'=2,'gx_1'=2,'gy'=4,'gz_0'=32,'gz_1'=2] {'gz_1'}, dimensions={0}, use_global_device_ids=true | all-gather | bytes 98304 | tf_op jit(solution)/shard_map/all_gather | solution.py:706
  107.1 12.2 %all_to_all.10.pieces = f32[32,1,128]{2,1,0:T(1,128)S(1)} all-to-all(f32[32,1,128]{2,1,0:T(1,128)S(1)} %get-tuple-element.95), channel_id=1, replica_groups=mesh['gx_0'=2,'gx_1'=2,'gy'=4,'gz_0'=32,'gz_1'=2] {'gx_0','gx_1','gy','g..., dimensions={0} | all-to-all | bytes 32768 | tf_op jit(solution)/shard_map/all_to_all | solution.py:771
  119.9 30.1 %all-to-all-start.1 = ((f32[32,1,128]{2,1,0:T(1,128)}), f32[32,1,128]{2,1,0:T(1,128)S(1)}, u32[]{:S(2)}, u32[]{:S(2)}) async-start(f32[32,1,128]{2,1,0:T(1,128)} %shard_map.69), calls=%async_computation.1 | async-start | bytes 32768 | tf_op jit(solution)/shard_map/all_to_all | solution.py:778
  150.0 3.7 %collective-permute-start.10 = (f32[64,128]{1,0:T(8,128)S(1)}, f32[64,128]{1,0:T(8,128)S(1)}, u32[]{:S(2)}, u32[]{:S(2)}) collective-permute-start(f32[64,128]{1,0:T(8,128)S(1)} %get-tuple-element.102), channel_id=1, source_target_pairs={{1,2},{2,1},{3,4},{4,3},{5,6},{6,5},{7,8},{8,7},{9,10},{10,9},{11,... | collective-permute-start | bytes 98312 | tf_op jit(solution)/shard_map/ppermute | solution.py:705
  157.1 4.6 %all-gather.8 = f32[128,128]{1,0:T(8,128)S(1)} all-gather(f32[64,128]{1,0:T(8,128)S(1)} %get-tuple-element.101), channel_id=10, replica_groups=mesh['gx_0'=2,'gx_1'=2,'gy'=4,'gz_0'=32,'gz_1'=2] {'gz_1'}, dimensions={0}, use_global_device_ids=true | all-gather | bytes 98304 | tf_op jit(solution)/shard_map/all_gather | solution.py:706
  162.4 10.0 %all-to-all-done.1.pieces = f32[32,1,128]{2,1,0:T(1,128)S(1)} async-done(((f32[32,1,128]{2,1,0:T(1,128)}), f32[32,1,128]{2,1,0:T(1,128)S(1)}, u32[]{:S(2)}, u32[]{:S(2)}) %all-to-all-start.1) | async-done | bytes 16416 | tf_op jit(solution)/shard_map/all_to_all | solution.py:778
  (29 shorter events, 17.2 us)
Async XLA Ops:
  1.9 12.8 %collective-permute-start = (f32[60,512]{1,0:T(8,128)S(1)}, f32[60,512]{1,0:T(8,128)S(1)}, u32[]{:S(2)}, u32[]{:S(2)}) collective-permute-start(f32[60,512]{1,0:T(8,128)S(1)} %get-tuple-element.55), channel_id=1, source_target_pairs={{0,64},{64,128},{128,192},{1,65},{65,129},{129,193},{2,66},{66,130... | collective-permute-start | bytes 368648 | tf_op jit(solution)/shard_map/ppermute | solution.py:699
  5.4 9.3 %collective-permute-start.1 = (f32[60,512]{1,0:T(8,128)S(1)}, f32[60,512]{1,0:T(8,128)S(1)}, u32[]{:S(2)}, u32[]{:S(2)}) collective-permute-start(f32[60,512]{1,0:T(8,128)S(1)} %get-tuple-element.56), channel_id=1, source_target_pairs={{64,0},{128,64},{192,128},{65,1},{129,65},{193,129},{66,2},{130,66... | collective-permute-start | bytes 368648 | tf_op jit(solution)/shard_map/ppermute | solution.py:699
  29.3 14.8 %collective-permute-start.2 = (f32[256,128]{1,0:T(8,128)S(1)}, f32[256,128]{1,0:T(8,128)S(1)}, u32[]{:S(2)}, u32[]{:S(2)}) collective-permute-start(f32[256,128]{1,0:T(8,128)S(1)} %get-tuple-element.62), channel_id=1, source_target_pairs={{1,2},{2,1},{3,4},{4,3},{5,6},{6,5},{7,8},{8,7},{9,10},{10,9},{11,... | collective-permute-start | bytes 393224 | tf_op jit(solution)/shard_map/ppermute | solution.py:705
  46.5 9.2 %collective-permute-start.3 = (f32[192,128]{1,0:T(8,128)S(1)}, f32[192,128]{1,0:T(8,128)S(1)}, u32[]{:S(2)}, u32[]{:S(2)}) collective-permute-start(f32[192,128]{1,0:T(8,128)S(1)} %get-tuple-element.66), channel_id=1, source_target_pairs={{1,2},{2,1},{3,4},{4,3},{5,6},{6,5},{7,8},{8,7},{9,10},{10,9},{11,... | collective-permute-start | bytes 294920 | tf_op jit(solution)/shard_map/ppermute | solution.py:705
  57.6 9.2 %collective-permute-start.4 = (f32[192,128]{1,0:T(8,128)S(1)}, f32[192,128]{1,0:T(8,128)S(1)}, u32[]{:S(2)}, u32[]{:S(2)}) collective-permute-start(f32[192,128]{1,0:T(8,128)S(1)} %get-tuple-element.70), channel_id=1, source_target_pairs={{1,2},{2,1},{3,4},{4,3},{5,6},{6,5},{7,8},{8,7},{9,10},{10,9},{11,... | collective-permute-start | bytes 294920 | tf_op jit(solution)/shard_map/ppermute | solution.py:705
  68.8 7.9 %collective-permute-start.5 = (f32[96,128]{1,0:T(8,128)S(1)}, f32[96,128]{1,0:T(8,128)S(1)}, u32[]{:S(2)}, u32[]{:S(2)}) collective-permute-start(f32[96,128]{1,0:T(8,128)S(1)} %get-tuple-element.74), channel_id=1, source_target_pairs={{1,2},{2,1},{3,4},{4,3},{5,6},{6,5},{7,8},{8,7},{9,10},{10,9},{11,... | collective-permute-start | bytes 147464 | tf_op jit(solution)/shard_map/ppermute | solution.py:705
  77.5 6.4 %collective-permute-start.6 = (f32[128,128]{1,0:T(8,128)S(1)}, f32[128,128]{1,0:T(8,128)S(1)}, u32[]{:S(2)}, u32[]{:S(2)}) collective-permute-start(f32[128,128]{1,0:T(8,128)S(1)} %get-tuple-element.77), channel_id=1, source_target_pairs={{0,64},{64,128},{128,192},{1,65},{65,129},{129,193},{2,66},{66,130... | collective-permute-start | bytes 196616 | tf_op jit(solution)/shard_map/ppermute | solution.py:699
  82.1 6.2 %collective-permute-start.7 = (f32[128,128]{1,0:T(8,128)S(1)}, f32[128,128]{1,0:T(8,128)S(1)}, u32[]{:S(2)}, u32[]{:S(2)}) collective-permute-start(f32[128,128]{1,0:T(8,128)S(1)} %get-tuple-element.78), channel_id=1, source_target_pairs={{64,0},{128,64},{192,128},{65,1},{129,65},{193,129},{66,2},{130,66... | collective-permute-start | bytes 196616 | tf_op jit(solution)/shard_map/ppermute | solution.py:699
  88.5 8.5 %collective-permute-start.8 = (f32[128,128]{1,0:T(8,128)S(1)}, f32[128,128]{1,0:T(8,128)S(1)}, u32[]{:S(2)}, u32[]{:S(2)}) collective-permute-start(f32[128,128]{1,0:T(8,128)S(1)} %get-tuple-element.85), channel_id=1, source_target_pairs={{1,2},{2,1},{3,4},{4,3},{5,6},{6,5},{7,8},{8,7},{9,10},{10,9},{11,... | collective-permute-start | bytes 196616 | tf_op jit(solution)/shard_map/ppermute | solution.py:705
  98.2 7.8 %collective-permute-start.9 = (f32[64,128]{1,0:T(8,128)S(1)}, f32[64,128]{1,0:T(8,128)S(1)}, u32[]{:S(2)}, u32[]{:S(2)}) collective-permute-start(f32[64,128]{1,0:T(8,128)S(1)} %get-tuple-element.91), channel_id=1, source_target_pairs={{1,2},{2,1},{3,4},{4,3},{5,6},{6,5},{7,8},{8,7},{9,10},{10,9},{11,... | collective-permute-start | bytes 98312 | tf_op jit(solution)/shard_map/ppermute | solution.py:705
  119.9 52.5 %all-to-all-start.1 = ((f32[32,1,128]{2,1,0:T(1,128)}), f32[32,1,128]{2,1,0:T(1,128)S(1)}, u32[]{:S(2)}, u32[]{:S(2)}) async-start(f32[32,1,128]{2,1,0:T(1,128)} %shard_map.69), calls=%async_computation.1 | async-start | bytes 32768 | tf_op jit(solution)/shard_map/all_to_all | solution.py:778
  150.0 3.7 %copy-start = (s32[16]{0:T(128)S(1)}, s32[16]{0:T(128)}, u32[]{:S(2)}) copy-start(s32[16]{0:T(128)} %place.7) | copy-start | bytes 196
  150.0 11.7 %collective-permute-start.10 = (f32[64,128]{1,0:T(8,128)S(1)}, f32[64,128]{1,0:T(8,128)S(1)}, u32[]{:S(2)}, u32[]{:S(2)}) collective-permute-start(f32[64,128]{1,0:T(8,128)S(1)} %get-tuple-element.102), channel_id=1, source_target_pairs={{1,2},{2,1},{3,4},{4,3},{5,6},{6,5},{7,8},{8,7},{9,10},{10,9},{11,... | collective-permute-start | bytes 98312 | tf_op jit(solution)/shard_map/ppermute | solution.py:705
